TPU v7x, 128 devices: a whole 4x4x4 slice. The times are simulated.
128 devices in a mesh: grp: 4 (over y), sub: 32 (over x, z, core).
Axes of the slice: x: 4, y: 4, z: 4, core: 2. Of those that a mesh axis runs over, the one named last changes fastest.
Arguments:
- initial_field: float32 [4, 64, 16384], P('grp', 'sub'), may hold values from -6 to 6
- conduct: float32 [4, 64, 16384], P('grp', 'sub'), may hold values from 0.02 to 0.12
- velocity: float32 [4, 64, 16384], P('grp', 'sub'), may hold values from 0 to 0.25
- heat_release: float32 [4, 64, 16384], P('grp', 'sub'), may hold values from 0.01 to 0.1
- group_kind: int32 [4], replicated, may hold values from 0 to 1, as said below
- partner: int32 [4], replicated, may hold values from 0 to 3, as said below
- surface_cell: int32 [4, 16384], P('grp', 'sub'), may hold values from 0 to 32767
- patch_count: int32 [4, 32], P('grp'), may hold values from 1 to 24, 256 in all within a row
- patch_centres: int32 [4, 768, 128], P('grp', 'sub'), may hold values from 0 to 16383, as said below
- patch_targets: int32 [4, 768, 128], P('grp', 'sub'), may hold values from 0 to 16383
- patch_maps: float32 [4, 768, 128, 128], P('grp', 'sub'), may hold values from -0.25 to 0.95
Outputs:
- temperature: float32 [4, 64, 16384], P('grp', 'sub')
- interface: float32 [4, 2, 16384], P('grp', None, 'sub')
Inputs may be any that keep to these rules, and one draw needn't show every extreme that they name: `group_kind`: both kinds occur. partner[g] is a group of the other kind than g. Slots 0 to patch_count[g, j] - 1 of device j of group g are live; each group's counts sum to 256; in each group some device holds 24. `patch_centres`: the centres of slot s of group g lie in the cyclic window of 1024 consecutive nodes that starts at (s // 24) * 512 - 512 // 2 + h[g], for one shift h[g] of each group.
All inputs are finite; a program needn't handle non-finite values.
Results may differ from a plain program's by a relative error of at most 0.00013.
Values sent between devices are 32-bit elements; how exact they have to be, the bound alone decides.
No kernel may reach another device: no remote copies, remote signals or barrier semaphores. Data moves between devices by JAX's collectives and lax.ppermute only.
A program may use at most 64 MiB of HBM per device.

v0:
```python
import functools

import jax
import jax.numpy as jnp
from jax import lax
from jax.experimental import pallas as pl
from jax.experimental.pallas import tpu as pltpu
from jax.sharding import PartitionSpec as P

STEPS = 4
COUPLE = 4
ROWS = 128
HALO = 4
WIDE = 12
F32 = jnp.float32
BF16 = jnp.bfloat16
VMEM = pltpu.VMEM
SMEM = pltpu.SMEM


def iota(shape, dim):
    return lax.broadcasted_iota(jnp.int32, shape, dim)


def in_plane(x):
    return (
        pltpu.roll(x, 1, 0)
        + pltpu.roll(x, ROWS - 1, 0)
        + pltpu.roll(x, 1, 1)
        + pltpu.roll(x, 127, 1)
    )


def split(x):
    high = x.astype(BF16)
    return high, (x - high.astype(F32)).astype(BF16)


def run_steps(cur, nxt, coef, gas):
    bufs = (cur, nxt)
    for step in range(STEPS):
        src, dst = bufs[step % 2], bufs[(step + 1) % 2]

        def body(p, carry, src=src, dst=dst):
            x = src[p]
            down = src[p - 1]
            lap = src[p + 1] + down + in_plane(x) - 6.0 * x
            heat = gas * coef[2, p - 1]
            dst[p] = (
                x
                + coef[0, p - 1] * lap
                - gas * coef[1, p - 1] * (x - down)
                + heat * (0.5 + 0.5 * jnp.tanh(x))
            )
            return carry

        lax.fori_loop(step + 1, WIDE - 1 - step, body, 0)


def pick_nodes(tables, surf, count):
    lanes = [jnp.broadcast_to(surf[g : g + 1] & 127, (8, 128)) for g in range(4)]
    rows = [jnp.broadcast_to(surf[g : g + 1] >> 7, (8, 128)) - iota((8, 128), 0) for g in range(4)]

    def body(v, acc):
        out = []
        for t, table in enumerate(tables):
            tile = table(v)
            for g in range(4):
                got = jnp.take_along_axis(tile, lanes[g], axis=1, mode="promise_in_bounds")
                out.append(jnp.where(rows[g] == 8 * v, got, acc[4 * t + g]))
        return tuple(out)

    start = tuple(jnp.zeros((8, 128), F32) for _ in range(4 * len(tables)))
    acc = lax.fori_loop(0, count, body, start)
    return [
        jnp.concatenate([jnp.sum(acc[4 * t + g], axis=0, keepdims=True) for g in range(4)], axis=0)
        for t in range(len(tables))
    ]


def scatter_block(surf, inc):
    left, right = [], []
    for g in range(4):
        lane = surf[g : g + 1] & 127
        row = surf[g : g + 1] >> 7
        left.append(jnp.where(iota((256, 128), 0) == row, 1.0, 0.0).astype(BF16))
        hit = iota((128, 128), 0) == lane
        high = jnp.where(hit, inc[g : g + 1], 0.0)
        top = high.astype(BF16)
        low = (high - top.astype(F32)).astype(BF16)
        right.append(jnp.concatenate([top, low], axis=0))
    out = lax.dot_general(
        jnp.concatenate(left, axis=1),
        jnp.concatenate(right, axis=1),
        (((1,), (1,)), ((), ())),
        preferred_element_type=F32,
    )
    return out[:, :128] + out[:, 128:]


def finish(ints, cur, coef, surf_ref, flux, keep, export):
    core = ints[0]
    for p in range(4):
        keep[pl.ds(p * ROWS, ROWS), :] = cur[HALO + p]
    for p in range(2):
        x = cur[HALO + 2 * core + p]
        flux[pl.ds(p * ROWS, ROWS), :] = coef[0, HALO - 1 + 2 * core + p] * (4.0 * x - in_plane(x))

    def plane_tile(first):
        def tile(v):
            return cur[first + v // 16, pl.ds(pl.multiple_of((v % 16) * 8, 8), 8), :]

        return tile

    def flux_tile(v):
        return flux[pl.ds(pl.multiple_of(v * 8, 8), 8), :]

    own, own_flux = pick_nodes(
        [plane_tile(HALO + 2 * core), flux_tile], surf_ref[pl.ds(2 + core, 1)][0], 32
    )
    (mate,) = pick_nodes([plane_tile(HALO + 2 - 2 * core)], surf_ref[pl.ds(3 - core, 1)][0], 32)
    is_first = core == 0
    keep[pl.ds(4 * ROWS, 8), :] = jnp.concatenate(
        [jnp.where(is_first, own, mate), jnp.where(is_first, mate, own)], axis=0
    )
    block = jnp.concatenate([own, own_flux], axis=0)
    export[...] = jnp.broadcast_to(block[None], export.shape)


def first_kernel(ints, flts, own, mate, left, left_mate, right, right_mate,
                 keep, export, coef, surf, cur, nxt, flux):
    core = ints[0]
    other = 1 - core
    for base, mine, its in ((0, left, left_mate), (4, own, mate), (8, right, right_mate)):
        for p in range(2):
            cur[base + 2 * core + p] = mine[pl.ds(p * ROWS, ROWS), :]
            cur[base + 2 * other + p] = its[pl.ds(p * ROWS, ROWS), :]
        tail = mine[pl.ds(1024, 8), :].astype(jnp.int32)
        tail_mate = its[pl.ds(1024, 8), :].astype(jnp.int32)
        surf[pl.ds(base // 2 + core, 1)] = tail[:4][None]
        surf[pl.ds(base // 2 + other, 1)] = tail_mate[:4][None]
    for which in range(3):
        def rows(ref, p, which=which):
            return ref[pl.ds(256 * (which + 1) + p * ROWS, ROWS), :]

        for p in range(2):
            coef[which, 3 + 2 * core + p] = rows(own, p)
            coef[which, 3 + 2 * other + p] = rows(mate, p)
        coef[which, 0] = jnp.where(core == 0, rows(left, 1), rows(left_mate, 1))
        coef[which, 1] = jnp.where(core == 0, rows(left_mate, 0), rows(left, 0))
        coef[which, 2] = jnp.where(core == 0, rows(left_mate, 1), rows(left, 1))
        coef[which, 7] = jnp.where(core == 0, rows(right, 0), rows(right_mate, 0))
        coef[which, 8] = jnp.where(core == 0, rows(right, 1), rows(right_mate, 1))
        coef[which, 9] = jnp.where(core == 0, rows(right_mate, 0), rows(right, 0))
    run_steps(cur, nxt, coef, flts[2])
    finish(ints, cur, coef, surf, flux, keep, export)


def middle_kernel(ints, flts, parts, own, left, right, coef, surf, keep, export, cur, nxt, flux):
    total = lax.fori_loop(1, parts.shape[0], lambda i, acc: acc + parts[i], parts[0])
    for side, ref in enumerate((left, own, right)):
        temps = ref[pl.ds(4 * ROWS, 8), :]
        inc = total[8 * side : 8 * side + 8] - flts[0] * temps
        for half in range(2):
            block = 2 * side + half
            add = scatter_block(surf[block], inc[4 * half : 4 * half + 4])
            for p in range(2):
                row = (2 * half + p) * ROWS
                cur[2 * block + p] = ref[pl.ds(row, ROWS), :] + add[p * ROWS : (p + 1) * ROWS]
    run_steps(cur, nxt, coef, flts[2])
    finish(ints, cur, coef, surf, flux, keep, export)


def last_kernel(ints, flts, parts, own, surf, field, interface):
    core = ints[0]
    total = lax.fori_loop(1, parts.shape[0], lambda i, acc: acc + parts[i], parts[0])
    interface[...] = total
    temps = own[pl.ds(4 * ROWS, 8), :]
    temps = jnp.where(core == 0, temps[:4], temps[4:])
    inc = flts[0] * (total[:4] - temps) + flts[1] * total[4:]
    add = scatter_block(surf[pl.ds(2 + core, 1)][0], inc)
    start = pl.multiple_of(core * 2 * ROWS, 2 * ROWS)
    field[...] = own[pl.ds(start, 2 * ROWS), :] + add


def patch_kernel(ints, flts, source, local, targets, maps, out, *, final):
    slots = local.shape[0]
    parts = 2 if final else 1
    lanes = [local[pl.ds(8 * w, 8), :] & 127 for w in range(slots // 8)]
    rows = [local[pl.ds(8 * w, 8), :] >> 7 for w in range(slots // 8)]
    vals = [[jnp.zeros((8, 128), F32) for _ in rows] for _ in range(parts)]
    for i in range(3):
        tile = source[ints[3 + i]]
        tables = [tile[:4], tile[4:]] if final else [flts[0] * tile[:4] + flts[1] * tile[4:]]
        for q, table in enumerate(tables):
            for j in range(4):
                line = jnp.broadcast_to(table[j : j + 1], (8, 128))
                for w in range(slots // 8):
                    got = jnp.take_along_axis(line, lanes[w], axis=1, mode="promise_in_bounds")
                    vals[q][w] = jnp.where(rows[w] == 4 * i + j, got, vals[q][w])
    live = ints[1]
    columns = []
    for q in range(parts):
        held = [jnp.where(iota((8, 128), 0) + 8 * w < live, vals[q][w], 0.0) for w in range(slots // 8)]
        full = jnp.concatenate(held + [jnp.zeros((128 - slots, 128), F32)], axis=0)
        columns.append(full.T)
    left, right = [], [[] for _ in range(parts)]
    for s in range(slots):
        aim = targets[s : s + 1, :]
        left.append(jnp.where(iota((128, 128), 0) == aim >> 7, 1.0, 0.0).astype(BF16))
        hit = iota((128, 128), 0) == (aim & 127)
        table = maps[s]
        for q in range(parts):
            value = jnp.sum(table * columns[q][:, s : s + 1], axis=0, keepdims=True)
            top = value.astype(BF16).astype(F32)
            right[q].append(
                jnp.concatenate(
                    [jnp.where(hit, top, 0.0).astype(BF16), jnp.where(hit, value - top, 0.0).astype(BF16)],
                    axis=0,
                )
            )
    lhs = jnp.concatenate(left, axis=1)
    sums = []
    for q in range(parts):
        both = lax.dot_general(
            lhs, jnp.concatenate(right[q], axis=1), (((1,), (1,)), ((), ())), preferred_element_type=F32
        )
        sums.append(both[:, :128] + both[:, 128:])
    chips = out.shape[0] // 2
    for c in range(chips):
        if final:
            for k in range(2):
                r = 2 * c + k
                out[r] = jnp.concatenate([s[4 * r : 4 * r + 4] for s in sums], axis=0)
        else:
            for side in range(3):
                n = c + side - 1
                piece = sums[0][8 * n : 8 * n + 8] if 0 <= n < chips else jnp.zeros((8, 128), F32)
                for k in range(2):
                    out[2 * c + k, pl.ds(8 * side, 8), :] = piece


def call(kernel, n_in, outs, scratch=()):
    specs = [pl.BlockSpec(memory_space=SMEM)] * 2 + [pl.BlockSpec(memory_space=VMEM)] * (n_in - 2)
    return pl.pallas_call(
        kernel,
        out_shape=[jax.ShapeDtypeStruct(s, d) for s, d in outs],
        in_specs=specs,
        out_specs=[pl.BlockSpec(memory_space=VMEM)] * len(outs),
        scratch_shapes=[pltpu.VMEM(s, F32) for s in scratch],
        compiler_params=pltpu.CompilerParams(vmem_limit_bytes=40 * 1024 * 1024),
    )


def local(
    initial_field,
    conduct,
    velocity,
    heat_release,
    group_kind,
    partner,
    surface_cell,
    patch_count,
    patch_centres,
    patch_targets,
    patch_maps,
):
    subs = lax.axis_size("sub")
    groups = lax.axis_size("grp")
    me = lax.axis_index("sub")
    group = lax.axis_index("grp")
    nodes = surface_cell.shape[1] * subs
    block = surface_cell.shape[1]
    slots = patch_maps.shape[1]
    kind = group_kind[group]
    gain_temp = jnp.where(kind == 0, 0.5, 0.25).astype(F32)
    gain_flux = jnp.where(kind == 0, -0.25, 0.25).astype(F32)
    gas = (kind == 0).astype(F32)
    flts = jnp.stack([gain_temp, gain_flux, gas])

    rows = 2 * ROWS
    surf_rows = surface_cell.reshape(block // 128, 128).astype(F32)
    payload = jnp.concatenate(
        [a.reshape(rows, 128) for a in (initial_field, conduct, velocity, heat_release)]
        + [surf_rows, surf_rows],
        axis=0,
    )
    up = [(i, i + 2) for i in range(subs - 2)]
    down = [(i + 2, i) for i in range(subs - 2)]
    swap = [(i, i ^ 1) for i in range(subs)]
    left = lax.ppermute(payload, "sub", up)
    right = lax.ppermute(payload, "sub", down)
    mate = lax.ppermute(payload, "sub", swap)
    left_mate = lax.ppermute(left, "sub", swap)
    right_mate = lax.ppermute(right, "sub", swap)

    centres = patch_centres[0]
    targets = patch_targets[0]
    live = patch_count[0, me]
    anchor = centres[0, 0]
    apart = ((centres - anchor + nodes // 2) & (nodes - 1)) - nodes // 2
    apart = jnp.where(jnp.arange(slots)[:, None] < live, apart, 0)
    first = ((anchor + jnp.min(apart)) & (nodes - 1)) // block
    place = (centres - first * block) & (nodes - 1)
    base = partner[group] * subs
    ints = jnp.stack(
        [me & 1, live, group] + [base + ((first + i) & (subs - 1)) for i in range(3)]
    ).astype(jnp.int32)
    maps = jnp.swapaxes(patch_maps[0], 1, 2)

    keep_shape = ((4 * ROWS + 8, 128), F32)
    send_shape = ((groups * subs, 8, 128), F32)
    work = [(WIDE, ROWS, 128), (WIDE, ROWS, 128), (2 * ROWS, 128)]
    keep, send, coef, surf = call(
        first_kernel,
        8,
        [keep_shape, send_shape, ((3, WIDE - 2, ROWS, 128), F32), ((6, 4, 128), jnp.int32)],
        work,
    )(ints, flts, payload, mate, left, left_mate, right, right_mate)
    for iteration in range(COUPLE):
        final = iteration == COUPLE - 1
        if not final:
            left = lax.ppermute(keep, "sub", up)
            right = lax.ppermute(keep, "sub", down)
        source = lax.all_to_all(send, ("grp", "sub"), 0, 0, tiled=True)
        (parts,) = call(
            functools.partial(patch_kernel, final=final), 6, [((subs, 8 if final else 24, 128), F32)]
        )(ints, flts, source, place, targets, maps)
        parts = lax.all_to_all(parts, "sub", 0, 0, tiled=True)
        if final:
            field, interface = call(last_kernel, 5, [((2 * ROWS, 128), F32), ((8, 128), F32)])(
                ints, flts, parts, keep, surf
            )
        else:
            keep, send = call(middle_kernel, 8, [keep_shape, send_shape], work)(
                ints, flts, parts, keep, left, right, coef, surf
            )
    return field.reshape(initial_field.shape), interface.reshape(1, 2, block)


def solution(mesh):
    placed = (
        P("grp", "sub", None),
        P("grp", "sub", None),
        P("grp", "sub", None),
        P("grp", "sub", None),
        P(),
        P(),
        P("grp", "sub"),
        P("grp", None),
        P("grp", "sub", None),
        P("grp", "sub", None),
        P("grp", "sub", None, None),
    )
    return jax.shard_map(
        local,
        mesh=mesh,
        in_specs=placed,
        out_specs=(P("grp", "sub", None), P("grp", None, "sub")),
        check_vma=False,
    )
```

profile of v0, /device:TPU:1, one launch (start us, length us, event | category | flops | bytes accessed | tf_op | source)
XLA Modules:
  0.0 276.6 jit_solution(3673063742779752185)
XLA Ops:
  0.7 1.1 reshape.43
  1.7 1.0 reshape.44
  2.8 1.0 reshape.45
  3.8 1.0 reshape.46
  5.5 4.4 %collective-permute-start.1 = (f32[1032,128]{1,0:T(8,128)S(1)}, f32[1032,128]{1,0:T(8,128)S(1)}, u32[]{:S(2)}, u32[]{:S(2)}) collective-permute-start(f32[1032,128]{1,0:T(8,128)S(1)} %concatenate.3.own), channel_id=1, source_target_pairs={{0,2},{1,3},{2,4},{3,5},{4,6},{5,7},{6,8},{7,9},{8,10},{9,11},{10,... | collective-permute-start | bytes 1585160 | tf_op jit(solution)/shard_map/ppermute | solution.py:291
  9.9 1.3 collective-permute-start.3
  11.2 1.0 collective-permute-start
  12.3 8.3 %collective-permute-done.1.left = f32[1032,128]{1,0:T(8,128)S(1)} collective-permute-done((f32[1032,128]{1,0:T(8,128)S(1)}, f32[1032,128]{1,0:T(8,128)S(1)}, u32[]{:S(2)}, u32[]{:S(2)}) %collective-permute-start.1) | collective-permute-done | bytes 528416 | tf_op jit(solution)/shard_map/ppermute | solution.py:291
  20.6 1.5 collective-permute-start.2
  22.1 2.6 collective-permute-done.3.right
  24.8 1.7 collective-permute-start.4
  26.4 0.8 copy-done.4
  29.0 1.3 select_reduce_fusion
  34.7 0.8 copy-done.6
  35.5 0.8 copy-done.8
  36.3 0.8 copy-done.10
  37.1 1.0 copy-done.5
  38.2 1.0 copy-done.7
  39.2 1.0 copy-done.9
  40.3 1.0 copy-done.11
  41.3 9.3 %shard_map.122 = (f32[520,128]{1,0:T(8,128)S(1)}, f32[128,8,128]{2,1,0:T(8,128)S(1)}, f32[3,10,128,128]{3,2,1,0:T(8,128)S(1)}, s32[6,4,128]{2,1,0:T(4,128)S(1)}) custom-call(s32[6]{0:T(128)S(1)} %stack.29.ints, f32[3]{0:T(128)S(1)} %pad_maximum_fusion.flts, f32[1032,128]{1,0:T(8,128)S(1)} %concatenate.3.own, f32[1032,128]{1,0:T(8,128)S(1)} %copy-done.7, ...), custom_call_target="tpu_custom_call" | custom-call | tf_op jit(solution)/shard_map/pallas_call | solution.py:314
  50.7 0.8 copy-done.12
  52.1 10.9 %all-to-all-start = ((f32[128,8,128]{2,1,0:T(8,128)}), f32[128,8,128]{2,1,0:T(8,128)}, u32[]{:S(2)}, u32[]{:S(2)}) async-start(f32[128,8,128]{2,1,0:T(8,128)} %copy-done.12), calls=%async_computation | async-start | bytes 1048576 | tf_op jit(solution)/shard_map/all_to_all | solution.py:325
  62.9 1.9 copy.13
  65.5 10.6 %all-to-all-done.source = f32[128,8,128]{2,1,0:T(8,128)} async-done(((f32[128,8,128]{2,1,0:T(8,128)}), f32[128,8,128]{2,1,0:T(8,128)}, u32[]{:S(2)}, u32[]{:S(2)}) %all-to-all-start) | async-done | bytes 524320 | tf_op jit(solution)/shard_map/all_to_all | solution.py:325
  78.2 2.2 shard_map.123
  80.4 0.7 copy-done.3
  81.2 5.4 %all-to-all-start.1 = ((f32[32,24,128]{2,1,0:T(8,128)}), f32[32,24,128]{2,1,0:T(8,128)}, u32[]{:S(2)}, u32[]{:S(2)}) async-start(f32[32,24,128]{2,1,0:T(8,128)} %copy-done.3), calls=%async_computation.1 | async-start | bytes 786432 | tf_op jit(solution)/shard_map/all_to_all | solution.py:329
  86.6 3.3 %collective-permute-start.5 = (f32[520,128]{1,0:T(8,128)}, f32[520,128]{1,0:T(8,128)S(1)}, u32[]{:S(2)}, u32[]{:S(2)}) collective-permute-start(f32[520,128]{1,0:T(8,128)} %copy-done.13), channel_id=1, source_target_pairs={{0,2},{1,3},{2,4},{3,5},{4,6},{5,7},{6,8},{7,9},{8,10},{9,11},{10,... | collective-permute-start | bytes 798728 | tf_op jit(solution)/shard_map/ppermute | solution.py:323
  89.8 1.3 collective-permute-start.6
  91.1 6.9 %collective-permute-done.5.left = f32[520,128]{1,0:T(8,128)S(1)} collective-permute-done((f32[520,128]{1,0:T(8,128)}, f32[520,128]{1,0:T(8,128)S(1)}, u32[]{:S(2)}, u32[]{:S(2)}) %collective-permute-start.5) | collective-permute-done | bytes 266272 | tf_op jit(solution)/shard_map/ppermute | solution.py:323
  98.8 1.3 collective-permute-done.6.right
  100.8 1.0 copy-done.14
  101.8 0.9 copy-done.20
  102.7 0.9 copy-done.26
  105.7 10.6 %shard_map.124 = (f32[520,128]{1,0:T(8,128)S(1)}, f32[128,8,128]{2,1,0:T(8,128)S(1)}) custom-call(s32[6]{0:T(128)S(1)} %copy-done.41, f32[3]{0:T(128)S(1)} %copy-done.46, f32[32,24,128]{2,1,0:T(8,128)} %all-to-all-done.1.parts, f32[520,128]{1,0:T(8,128)S(1)} %copy-done.14, f32[520,128]{1,0:T(8,128)S(1)} %copy-done.20, f32[520,128]{1,0:T(8,128)S(1)} %copy-done.26, ...), custom_call_target="tpu_custom_call" | custom-call | tf_op jit(solution)/shard_map/pallas_call | solution.py:335
  117.0 22.4 %all_to_all.40.source = f32[128,8,128]{2,1,0:T(8,128)S(1)} all-to-all(f32[128,8,128]{2,1,0:T(8,128)S(1)} %get-tuple-element.18), channel_id=1, replica_groups=mesh['grp'=4,'sub'=32] {'grp','sub'}, dimensions={0} | all-to-all | bytes 1048576 | tf_op jit(solution)/shard_map/all_to_all | solution.py:325
  139.5 1.7 shard_map.125
  141.2 0.7 copy-done.1
  142.0 5.4 %all-to-all-start.3 = ((f32[32,24,128]{2,1,0:T(8,128)}), f32[32,24,128]{2,1,0:T(8,128)}, u32[]{:S(2)}, u32[]{:S(2)}) async-start(f32[32,24,128]{2,1,0:T(8,128)} %copy-done.1), calls=%async_computation.3 | async-start | bytes 786432 | tf_op jit(solution)/shard_map/all_to_all | solution.py:329
  147.4 3.3 %collective-permute-start.7 = (f32[520,128]{1,0:T(8,128)}, f32[520,128]{1,0:T(8,128)S(1)}, u32[]{:S(2)}, u32[]{:S(2)}) collective-permute-start(f32[520,128]{1,0:T(8,128)} %copy-done.17), channel_id=1, source_target_pairs={{0,2},{1,3},{2,4},{3,5},{4,6},{5,7},{6,8},{7,9},{8,10},{9,11},{10,... | collective-permute-start | bytes 798728 | tf_op jit(solution)/shard_map/ppermute | solution.py:323
  150.7 1.3 collective-permute-start.8
  152.0 6.9 %collective-permute-done.7.left = f32[520,128]{1,0:T(8,128)S(1)} collective-permute-done((f32[520,128]{1,0:T(8,128)}, f32[520,128]{1,0:T(8,128)S(1)}, u32[]{:S(2)}, u32[]{:S(2)}) %collective-permute-start.7) | collective-permute-done | bytes 266272 | tf_op jit(solution)/shard_map/ppermute | solution.py:323
  159.6 1.3 collective-permute-done.8.right
  161.6 1.0 copy-done.18
  162.6 0.9 copy-done.24
  163.5 0.9 copy-done.30
  166.5 10.6 %shard_map.126 = (f32[520,128]{1,0:T(8,128)S(1)}, f32[128,8,128]{2,1,0:T(8,128)S(1)}) custom-call(s32[6]{0:T(128)S(1)} %copy-done.42, f32[3]{0:T(128)S(1)} %copy-done.47, f32[32,24,128]{2,1,0:T(8,128)} %all-to-all-done.3.parts, f32[520,128]{1,0:T(8,128)S(1)} %copy-done.18, f32[520,128]{1,0:T(8,128)S(1)} %copy-done.24, f32[520,128]{1,0:T(8,128)S(1)} %copy-done.30, ...), custom_call_target="tpu_custom_call" | custom-call | tf_op jit(solution)/shard_map/pallas_call | solution.py:335
  177.9 22.4 %all_to_all.41.source = f32[128,8,128]{2,1,0:T(8,128)S(1)} all-to-all(f32[128,8,128]{2,1,0:T(8,128)S(1)} %get-tuple-element.20), channel_id=1, replica_groups=mesh['grp'=4,'sub'=32] {'grp','sub'}, dimensions={0} | all-to-all | bytes 1048576 | tf_op jit(solution)/shard_map/all_to_all | solution.py:325
  200.3 1.7 shard_map.127
  202.1 0.7 copy-done.2
  202.8 5.4 %all-to-all-start.5 = ((f32[32,24,128]{2,1,0:T(8,128)}), f32[32,24,128]{2,1,0:T(8,128)}, u32[]{:S(2)}, u32[]{:S(2)}) async-start(f32[32,24,128]{2,1,0:T(8,128)} %copy-done.2), calls=%async_computation.5 | async-start | bytes 786432 | tf_op jit(solution)/shard_map/all_to_all | solution.py:329
  208.2 1.3 collective-permute-start.10
  209.5 4.0 %collective-permute-start.9 = (f32[520,128]{1,0:T(8,128)}, f32[520,128]{1,0:T(8,128)S(1)}, u32[]{:S(2)}, u32[]{:S(2)}) collective-permute-start(f32[520,128]{1,0:T(8,128)} %copy-done.15), channel_id=1, source_target_pairs={{0,2},{1,3},{2,4},{3,5},{4,6},{5,7},{6,8},{7,9},{8,10},{9,11},{10,... | collective-permute-start | bytes 798728 | tf_op jit(solution)/shard_map/ppermute | solution.py:323
  213.5 7.7 %collective-permute-done.10.right = f32[520,128]{1,0:T(8,128)S(1)} collective-permute-done((f32[520,128]{1,0:T(8,128)}, f32[520,128]{1,0:T(8,128)S(1)}, u32[]{:S(2)}, u32[]{:S(2)}) %collective-permute-start.10) | collective-permute-done | bytes 266272 | tf_op jit(solution)/shard_map/ppermute | solution.py:324
  222.6 1.0 copy-done.16
  223.6 0.9 copy-done.22
  224.5 0.9 copy-done.28
  227.5 10.6 %shard_map.128 = (f32[520,128]{1,0:T(8,128)S(1)}, f32[128,8,128]{2,1,0:T(8,128)S(1)}) custom-call(s32[6]{0:T(128)S(1)} %copy-done.43, f32[3]{0:T(128)S(1)} %copy-done.48, f32[32,24,128]{2,1,0:T(8,128)} %all-to-all-done.5.parts, f32[520,128]{1,0:T(8,128)S(1)} %copy-done.16, f32[520,128]{1,0:T(8,128)S(1)} %copy-done.28, f32[520,128]{1,0:T(8,128)S(1)} %copy-done.22, ...), custom_call_target="tpu_custom_call" | custom-call | tf_op jit(solution)/shard_map/pallas_call | solution.py:335
  238.1 21.6 %all_to_all.42.source = f32[128,8,128]{2,1,0:T(8,128)S(1)} all-to-all(f32[128,8,128]{2,1,0:T(8,128)S(1)} %get-tuple-element.22), channel_id=1, replica_groups=mesh['grp'=4,'sub'=32] {'grp','sub'}, dimensions={0} | all-to-all | bytes 1048576 | tf_op jit(solution)/shard_map/all_to_all | solution.py:325
  259.8 2.4 shard_map.129
  262.1 12.1 %all_to_all.43.parts = f32[32,8,128]{2,1,0:T(8,128)S(1)} all-to-all(f32[32,8,128]{2,1,0:T(8,128)S(1)} %shard_map.129), channel_id=1, replica_groups=mesh['grp'=4,'sub'=32] {'sub'}, dimensions={0} | all-to-all | bytes 262144 | tf_op jit(solution)/shard_map/all_to_all | solution.py:329
  274.2 1.0 shard_map.130
  275.2 0.7 reshape.47
  (101 shorter events, 20.2 us)
Async XLA Ops:
  0.6 27.1 %copy-start = (s32[1,32]{1,0:T(1,128)S(1)}, s32[1,32]{1,0:T(1,128)}, u32[]{:S(2)}) copy-start(s32[1,32]{1,0:T(1,128)} %param.18) | copy-start | bytes 388
  0.6 26.6 %copy-start.49 = (s32[1,24,128]{2,1,0:T(8,128)S(1)}, s32[1,24,128]{2,1,0:T(8,128)}, u32[]{:S(2)}) copy-start(s32[1,24,128]{2,1,0:T(8,128)} %param.19) | copy-start | bytes 36868
  0.7 30.9 %copy-start.50 = (s32[4]{0:T(128)S(1)}, s32[4]{0:T(128)}, u32[]{:S(2)}) copy-start(s32[4]{0:T(128)} %param.16) | copy-start | bytes 52
  0.7 32.1 %copy-start.51 = (s32[4]{0:T(128)S(1)}, s32[4]{0:T(128)}, u32[]{:S(2)}) copy-start(s32[4]{0:T(128)} %param.15) | copy-start | bytes 52
  5.5 15.0 %collective-permute-start.1 = (f32[1032,128]{1,0:T(8,128)S(1)}, f32[1032,128]{1,0:T(8,128)S(1)}, u32[]{:S(2)}, u32[]{:S(2)}) collective-permute-start(f32[1032,128]{1,0:T(8,128)S(1)} %concatenate.3.own), channel_id=1, source_target_pairs={{0,2},{1,3},{2,4},{3,5},{4,6},{5,7},{6,8},{7,9},{8,10},{9,11},{10,... | collective-permute-start | bytes 1585160 | tf_op jit(solution)/shard_map/ppermute | solution.py:291
  9.9 14.8 %collective-permute-start.3 = (f32[1032,128]{1,0:T(8,128)S(1)}, f32[1032,128]{1,0:T(8,128)S(1)}, u32[]{:S(2)}, u32[]{:S(2)}) collective-permute-start(f32[1032,128]{1,0:T(8,128)S(1)} %concatenate.3.own), channel_id=1, source_target_pairs={{2,0},{3,1},{4,2},{5,3},{6,4},{7,5},{8,6},{9,7},{10,8},{11,9},{12,... | collective-permute-start | bytes 1585160 | tf_op jit(solution)/shard_map/ppermute | solution.py:292
  11.2 23.5 %collective-permute-start = (f32[1032,128]{1,0:T(8,128)S(1)}, f32[1032,128]{1,0:T(8,128)S(1)}, u32[]{:S(2)}, u32[]{:S(2)}) collective-permute-start(f32[1032,128]{1,0:T(8,128)S(1)} %concatenate.3.own), channel_id=1, source_target_pairs={{0,1},{1,0},{2,3},{3,2},{4,5},{5,4},{6,7},{7,6},{8,9},{9,8},{10,11... | collective-permute-start | bytes 1585160 | tf_op jit(solution)/shard_map/ppermute | solution.py:293
  20.6 14.9 %collective-permute-start.2 = (f32[1032,128]{1,0:T(8,128)S(1)}, f32[1032,128]{1,0:T(8,128)S(1)}, u32[]{:S(2)}, u32[]{:S(2)}) collective-permute-start(f32[1032,128]{1,0:T(8,128)S(1)} %collective-permute-done.1.left), channel_id=1, source_target_pairs={{0,1},{1,0},{2,3},{3,2},{4,5},{5,4},{6,7},{7,6},{8,9},{9,8},{10,11... | collective-permute-start | bytes 1585160 | tf_op jit(solution)/shard_map/ppermute | solution.py:294
  24.8 11.6 %collective-permute-start.4 = (f32[1032,128]{1,0:T(8,128)S(1)}, f32[1032,128]{1,0:T(8,128)S(1)}, u32[]{:S(2)}, u32[]{:S(2)}) collective-permute-start(f32[1032,128]{1,0:T(8,128)S(1)} %collective-permute-done.3.right), channel_id=1, source_target_pairs={{0,1},{1,0},{2,3},{3,2},{4,5},{5,4},{6,7},{7,6},{8,9},{9,8},{10,11... | collective-permute-start | bytes 1585160 | tf_op jit(solution)/shard_map/ppermute | solution.py:295
  26.4 0.8 copy-start.4
  34.6 16.0 %copy-start.39 = (s32[6]{0:T(128)}, s32[6]{0:T(128)S(1)}, u32[]{:S(2)}) copy-start(s32[6]{0:T(128)S(1)} %stack.29.ints) | copy-start | bytes 76
  34.7 0.8 copy-start.6
  35.5 0.8 copy-start.8
  36.3 0.8 copy-start.10
  37.1 1.0 copy-start.5
  38.2 1.0 copy-start.7
  39.2 1.0 copy-start.9
  40.3 1.0 copy-start.11
  50.6 0.8 copy-start.12
  52.0 10.9 %copy-start.13 = (f32[520,128]{1,0:T(8,128)}, f32[520,128]{1,0:T(8,128)S(1)}, u32[]{:S(2)}) copy-start(f32[520,128]{1,0:T(8,128)S(1)} %get-tuple-element.15.own) | copy-start | bytes 798724
  52.0 10.9 %copy-start.35 = (s32[6,4,128]{2,1,0:T(4,128)}, s32[6,4,128]{2,1,0:T(4,128)S(1)}, u32[]{:S(2)}) copy-start(s32[6,4,128]{2,1,0:T(4,128)S(1)} %get-tuple-element.17.surf) | copy-start | bytes 36868
  52.1 24.1 %all-to-all-start = ((f32[128,8,128]{2,1,0:T(8,128)}), f32[128,8,128]{2,1,0:T(8,128)}, u32[]{:S(2)}, u32[]{:S(2)}) async-start(f32[128,8,128]{2,1,0:T(8,128)} %copy-done.12), calls=%async_computation | async-start | bytes 1048576 | tf_op jit(solution)/shard_map/all_to_all | solution.py:325
  76.1 0.7 copy-start.31
  76.8 0.7 copy-start.40
  77.5 0.7 copy-start.45
  80.4 0.7 copy-start.3
  81.2 19.6 %all-to-all-start.1 = ((f32[32,24,128]{2,1,0:T(8,128)}), f32[32,24,128]{2,1,0:T(8,128)}, u32[]{:S(2)}, u32[]{:S(2)}) async-start(f32[32,24,128]{2,1,0:T(8,128)} %copy-done.3), calls=%async_computation.1 | async-start | bytes 786432 | tf_op jit(solution)/shard_map/all_to_all | solution.py:329
  86.6 11.5 %collective-permute-start.5 = (f32[520,128]{1,0:T(8,128)}, f32[520,128]{1,0:T(8,128)S(1)}, u32[]{:S(2)}, u32[]{:S(2)}) collective-permute-start(f32[520,128]{1,0:T(8,128)} %copy-done.13), channel_id=1, source_target_pairs={{0,2},{1,3},{2,4},{3,5},{4,6},{5,7},{6,8},{7,9},{8,10},{9,11},{10,... | collective-permute-start | bytes 798728 | tf_op jit(solution)/shard_map/ppermute | solution.py:323
  89.8 10.2 %collective-permute-start.6 = (f32[520,128]{1,0:T(8,128)}, f32[520,128]{1,0:T(8,128)S(1)}, u32[]{:S(2)}, u32[]{:S(2)}) collective-permute-start(f32[520,128]{1,0:T(8,128)} %copy-done.13), channel_id=1, source_target_pairs={{2,0},{3,1},{4,2},{5,3},{6,4},{7,5},{8,6},{9,7},{10,8},{11,9},{12,... | collective-permute-start | bytes 798728 | tf_op jit(solution)/shard_map/ppermute | solution.py:324
  98.1 0.7 copy-start.19
  100.1 0.7 copy-start.25
  100.8 1.0 copy-start.14
  101.8 1.0 copy-start.20
  102.7 1.0 copy-start.26
  103.7 0.7 copy-start.36
  104.4 0.7 copy-start.41
  105.0 0.7 copy-start.46
  105.7 33.8 %copy-start.32 = (s32[1,24,128]{2,1,0:T(8,128)S(1)}, s32[1,24,128]{2,1,0:T(8,128)}, u32[]{:S(2)}) copy-start(s32[1,24,128]{2,1,0:T(8,128)} %param.20) | copy-start | bytes 36868
  116.3 0.7 copy-start.17
  141.2 0.7 copy-start.1
  142.0 19.6 %all-to-all-start.3 = ((f32[32,24,128]{2,1,0:T(8,128)}), f32[32,24,128]{2,1,0:T(8,128)}, u32[]{:S(2)}, u32[]{:S(2)}) async-start(f32[32,24,128]{2,1,0:T(8,128)} %copy-done.1), calls=%async_computation.3 | async-start | bytes 786432 | tf_op jit(solution)/shard_map/all_to_all | solution.py:329
  147.4 11.5 %collective-permute-start.7 = (f32[520,128]{1,0:T(8,128)}, f32[520,128]{1,0:T(8,128)S(1)}, u32[]{:S(2)}, u32[]{:S(2)}) collective-permute-start(f32[520,128]{1,0:T(8,128)} %copy-done.17), channel_id=1, source_target_pairs={{0,2},{1,3},{2,4},{3,5},{4,6},{5,7},{6,8},{7,9},{8,10},{9,11},{10,... | collective-permute-start | bytes 798728 | tf_op jit(solution)/shard_map/ppermute | solution.py:323
  150.7 10.2 %collective-permute-start.8 = (f32[520,128]{1,0:T(8,128)}, f32[520,128]{1,0:T(8,128)S(1)}, u32[]{:S(2)}, u32[]{:S(2)}) collective-permute-start(f32[520,128]{1,0:T(8,128)} %copy-done.17), channel_id=1, source_target_pairs={{2,0},{3,1},{4,2},{5,3},{6,4},{7,5},{8,6},{9,7},{10,8},{11,9},{12,... | collective-permute-start | bytes 798728 | tf_op jit(solution)/shard_map/ppermute | solution.py:324
  158.9 0.7 copy-start.23
  160.9 0.7 copy-start.29
  161.6 1.0 copy-start.18
  162.6 1.0 copy-start.24
  163.5 1.0 copy-start.30
  164.5 0.7 copy-start.37
  165.8 0.7 copy-start.47
  166.5 33.8 %copy-start.33 = (s32[1,24,128]{2,1,0:T(8,128)S(1)}, s32[1,24,128]{2,1,0:T(8,128)}, u32[]{:S(2)}) copy-start(s32[1,24,128]{2,1,0:T(8,128)} %param.20) | copy-start | bytes 36868
  177.1 0.7 copy-start.15
  202.0 0.7 copy-start.2
  202.8 19.8 %all-to-all-start.5 = ((f32[32,24,128]{2,1,0:T(8,128)}), f32[32,24,128]{2,1,0:T(8,128)}, u32[]{:S(2)}, u32[]{:S(2)}) async-start(f32[32,24,128]{2,1,0:T(8,128)} %copy-done.2), calls=%async_computation.5 | async-start | bytes 786432 | tf_op jit(solution)/shard_map/all_to_all | solution.py:329
  208.2 13.0 %collective-permute-start.10 = (f32[520,128]{1,0:T(8,128)}, f32[520,128]{1,0:T(8,128)S(1)}, u32[]{:S(2)}, u32[]{:S(2)}) collective-permute-start(f32[520,128]{1,0:T(8,128)} %copy-done.15), channel_id=1, source_target_pairs={{2,0},{3,1},{4,2},{5,3},{6,4},{7,5},{8,6},{9,7},{10,8},{11,9},{12,... | collective-permute-start | bytes 798728 | tf_op jit(solution)/shard_map/ppermute | solution.py:324
  209.5 12.4 %collective-permute-start.9 = (f32[520,128]{1,0:T(8,128)}, f32[520,128]{1,0:T(8,128)S(1)}, u32[]{:S(2)}, u32[]{:S(2)}) collective-permute-start(f32[520,128]{1,0:T(8,128)} %copy-done.15), channel_id=1, source_target_pairs={{0,2},{1,3},{2,4},{3,5},{4,6},{5,7},{6,8},{7,9},{8,10},{9,11},{10,... | collective-permute-start | bytes 798728 | tf_op jit(solution)/shard_map/ppermute | solution.py:323
  221.2 0.7 copy-start.21
  221.9 0.7 copy-start.27
  222.6 1.0 copy-start.16
  223.6 1.0 copy-start.22
  224.5 1.0 copy-start.28
  225.5 0.7 copy-start.38
  226.8 0.7 copy-start.48
  227.5 32.3 %copy-start.34 = (s32[1,24,128]{2,1,0:T(8,128)S(1)}, s32[1,24,128]{2,1,0:T(8,128)}, u32[]{:S(2)}) copy-start(s32[1,24,128]{2,1,0:T(8,128)} %param.20) | copy-start | bytes 36868
  (3 other events, 1.9 us)
where the time goes:
time: 278 us; the launch traced here: 277 us
  blocking collectives  78.6 us (28%)
  starting transfers between devices  51.4 us (18%)
  Pallas kernels  50.3 us (18%)
  waiting for transfers between devices  45.8 us (16%)
  local copies, waits for them, and re-layouts  43.8 us (16%)
  other arithmetic  3.45 us (1%)
  between operations  3.38 us (1%)
    all_to_all x3, blocking collectives, local(): source = lax.all_to_all(send, ('grp', 'sub'), 0, 0, tiled=True)  66.5 us
    unnamed x105, local copies, waits for them, and re-layouts  35.3 us
    pallas_call x3, Pallas kernels, local(): call(middle_kernel, 8, [keep_shape, send_shape], work)  31.9 us
    all_to_all x3, starting transfers between devices, local(): parts = lax.all_to_all(parts, 'sub', 0, 0, tiled=True)  16.1 us
    ppermute x3, waiting for transfers between devices, local(): left = lax.ppermute(keep, 'sub', up)  13.9 us
    all_to_all x1, blocking collectives, local(): parts = lax.all_to_all(parts, 'sub', 0, 0, tiled=True)  12.1 us
    all_to_all x1, starting transfers between devices, local(): source = lax.all_to_all(send, ('grp', 'sub'), 0, 0, tiled=True)  10.9 us
    all_to_all x1, waiting for transfers between devices, local(): source = lax.all_to_all(send, ('grp', 'sub'), 0, 0, tiled=True)  10.6 us
  transfers between devices with their start and end apart: 15, of which 8 were waited for; matrix products, arithmetic and copies ran while one was open for 3% of the time, Pallas kernels for 0%

commit v1 on v0

v1 whole, which is shorter than its diff:
```python
import functools

import jax
import jax.numpy as jnp
from jax import lax
from jax.experimental import pallas as pl
from jax.experimental.pallas import tpu as pltpu
from jax.sharding import PartitionSpec as P

STEPS = 4
COUPLE = 4
ROWS = 128
HALO = 4
WIDE = 12
F32 = jnp.float32
BF16 = jnp.bfloat16
VMEM = pltpu.VMEM
SMEM = pltpu.SMEM


def iota(shape, dim):
    return lax.broadcasted_iota(jnp.int32, shape, dim)


def in_plane(x):
    return (
        pltpu.roll(x, 1, 0)
        + pltpu.roll(x, ROWS - 1, 0)
        + pltpu.roll(x, 1, 1)
        + pltpu.roll(x, 127, 1)
    )


def run_steps(cur, nxt, coef):
    bufs = (cur, nxt)
    for step in range(STEPS):
        src, dst = bufs[step % 2], bufs[(step + 1) % 2]

        def body(p, carry, src=src, dst=dst):
            x = src[p]
            dst[p] = (
                x
                + coef[0, p - 1] * (src[p + 1] + in_plane(x) - 5.0 * x)
                + coef[1, p - 1] * (src[p - 1] - x)
                + coef[2, p - 1] * (1.0 + jnp.tanh(x))
            )
            return carry

        lax.fori_loop(step + 1, WIDE - 1 - step, body, 0, unroll=2)


def pick_nodes(jobs):
    keys = []
    for _, surf in jobs:
        lanes = [jnp.broadcast_to(surf[g : g + 1] & 127, (8, 128)) for g in range(4)]
        rows = [jnp.broadcast_to(surf[g : g + 1] >> 7, (8, 128)) - iota((8, 128), 0) for g in range(4)]
        keys.append((lanes, rows))

    def body(v, acc):
        out = []
        for (tables, _), (lanes, rows) in zip(jobs, keys):
            hits = [rows[g] == 8 * v for g in range(4)]
            for table in tables:
                tile = table(v)
                for g in range(4):
                    got = jnp.take_along_axis(tile, lanes[g], axis=1, mode="promise_in_bounds")
                    out.append(jnp.where(hits[g], got, acc[len(out)]))
        return tuple(out)

    total = sum(len(tables) for tables, _ in jobs)
    acc = lax.fori_loop(0, 32, body, tuple(jnp.zeros((8, 128), F32) for _ in range(4 * total)), unroll=8)
    return [
        jnp.concatenate([jnp.sum(acc[4 * t + g], axis=0, keepdims=True) for g in range(4)], axis=0)
        for t in range(total)
    ]


def scatter_block(surf, inc):
    left, right = [], []
    for g in range(4):
        lane = surf[g : g + 1] & 127
        row = surf[g : g + 1] >> 7
        left.append(jnp.where(iota((256, 128), 0) == row, 1.0, 0.0).astype(BF16))
        hit = iota((128, 128), 0) == lane
        value = inc[g : g + 1]
        top = value.astype(BF16).astype(F32)
        right.append(
            jnp.concatenate(
                [jnp.where(hit, top, 0.0).astype(BF16), jnp.where(hit, value - top, 0.0).astype(BF16)], axis=0
            )
        )
    out = lax.dot_general(
        jnp.concatenate(left, axis=1),
        jnp.concatenate(right, axis=1),
        (((1,), (1,)), ((), ())),
        preferred_element_type=F32,
    )
    return out[:, :128] + out[:, 128:]


def finish(ints, flts, cur, coef, surf_ref, flux, keep, export, full):
    core = ints[0]
    for p in range(4):
        keep[pl.ds(p * ROWS, ROWS), :] = cur[HALO + p]
    for p in range(2):
        x = cur[HALO + 2 * core + p]
        flux[pl.ds(p * ROWS, ROWS), :] = coef[0, HALO - 1 + 2 * core + p] * (4.0 * x - in_plane(x))

    def plane_tile(first):
        def tile(v):
            return cur[first + v // 16, pl.ds(pl.multiple_of((v % 16) * 8, 8), 8), :]

        return tile

    def flux_tile(v):
        return flux[pl.ds(pl.multiple_of(v * 8, 8), 8), :]

    own, own_flux, mate = pick_nodes(
        [
            ([plane_tile(HALO + 2 * core), flux_tile], surf_ref[pl.ds(2 + core, 1)][0]),
            ([plane_tile(HALO + 2 - 2 * core)], surf_ref[pl.ds(3 - core, 1)][0]),
        ]
    )
    is_first = core == 0
    keep[pl.ds(4 * ROWS, 8), :] = jnp.concatenate(
        [jnp.where(is_first, own, mate), jnp.where(is_first, mate, own)], axis=0
    )
    if full:
        block = jnp.concatenate([own, own_flux], axis=0)
    else:
        block = flts[3] * own + flts[4] * own_flux
    export[...] = jnp.broadcast_to(block[None], export.shape)


def pack_kernel(field, conduct, velocity, heat, surface, payload):
    for i, ref in enumerate((field, conduct, velocity, heat)):
        payload[pl.ds(256 * i, 256), :] = ref[...].reshape(2 * ROWS, 128)
    cells = surface[...].reshape(4, 128).astype(F32)
    payload[pl.ds(1024, 8), :] = jnp.concatenate([cells, cells], axis=0)


def prepare_kernel(kinds, partners, counts, centres, maps, ints, flts, place, turned):
    group = lax.axis_index("grp")
    me = lax.axis_index("sub")
    subs = counts.shape[1]
    nodes = subs * 512
    live = counts[0, me]
    kind = kinds[group]
    at = centres[...]
    anchor = at[0:1, 0:1]
    apart = ((at - anchor + nodes // 2) & (nodes - 1)) - nodes // 2
    apart = jnp.where(iota(at.shape, 0) < live, apart, 0)
    lowest = jnp.min(apart.astype(F32)).astype(jnp.int32)
    start = (jnp.max(anchor.astype(F32)).astype(jnp.int32) + lowest) & (nodes - 1)
    first = start >> 9
    place[...] = (at - first * 512) & (nodes - 1)
    ints[0] = me & 1
    ints[1] = live
    ints[2] = kind
    for i in range(3):
        ints[3 + i] = partners[group] * subs + ((first + i) & (subs - 1))
    is_gas = kind == 0
    flts[0] = jnp.where(is_gas, 0.5, 0.25)
    flts[1] = jnp.where(is_gas, -0.25, 0.25)
    flts[2] = jnp.where(is_gas, 1.0, 0.0)
    flts[3] = jnp.where(is_gas, 0.25, 0.5)
    flts[4] = jnp.where(is_gas, 0.25, -0.25)
    for s in range(maps.shape[0]):
        turned[s] = maps[s].T


def first_kernel(ints, flts, own, mate, left, left_mate, right, right_mate,
                 keep, export, saved, surf, cur, nxt, flux, coef, sem):
    core = ints[0]
    other = 1 - core
    for base, mine, its in ((0, left, left_mate), (4, own, mate), (8, right, right_mate)):
        for p in range(2):
            cur[base + 2 * core + p] = mine[pl.ds(p * ROWS, ROWS), :]
            cur[base + 2 * other + p] = its[pl.ds(p * ROWS, ROWS), :]
        tail = mine[pl.ds(1024, 8), :].astype(jnp.int32)
        tail_mate = its[pl.ds(1024, 8), :].astype(jnp.int32)
        surf[pl.ds(base // 2 + core, 1)] = tail[:4][None]
        surf[pl.ds(base // 2 + other, 1)] = tail_mate[:4][None]
    gas = flts[2]

    def store(p, ref, half):
        got = [ref[pl.ds(256 * (w + 1) + half * ROWS, ROWS), :] for w in range(3)]
        coef[0, p] = got[0]
        coef[1, p] = got[0] + gas * got[1]
        coef[2, p] = (0.5 * gas) * got[2]

    for half in range(2):
        store(3 + 2 * core + half, own, half)
        store(3 + 2 * other + half, mate, half)

    @pl.when(core == 0)
    def _():
        store(0, left, 1)
        store(1, left_mate, 0)
        store(2, left_mate, 1)
        store(7, right, 0)
        store(8, right, 1)
        store(9, right_mate, 0)

    @pl.when(core == 1)
    def _():
        store(0, left_mate, 1)
        store(1, left, 0)
        store(2, left, 1)
        store(7, right_mate, 0)
        store(8, right_mate, 1)
        store(9, right, 0)

    copy = pltpu.make_async_copy(coef, saved, sem)
    copy.start()
    run_steps(cur, nxt, coef)
    finish(ints, flts, cur, coef, surf, flux, keep, export, False)
    copy.wait()


def middle_kernel(ints, flts, parts, own, left, right, surf, saved, keep, export,
                  cur, nxt, flux, coef, sem, *, full):
    copy = pltpu.make_async_copy(saved, coef, sem)
    copy.start()
    total = sum_parts(parts)
    for side, ref in enumerate((left, own, right)):
        temps = ref[pl.ds(4 * ROWS, 8), :]
        inc = total[8 * side : 8 * side + 8] - flts[0] * temps
        for half in range(2):
            block = 2 * side + half
            add = scatter_block(surf[block], inc[4 * half : 4 * half + 4])
            for p in range(2):
                row = (2 * half + p) * ROWS
                cur[2 * block + p] = ref[pl.ds(row, ROWS), :] + add[p * ROWS : (p + 1) * ROWS]
    copy.wait()
    run_steps(cur, nxt, coef)
    finish(ints, flts, cur, coef, surf, flux, keep, export, full)


def sum_parts(parts):
    lanes = [parts[i] for i in range(4)]
    for i in range(4, parts.shape[0]):
        lanes[i % 4] = lanes[i % 4] + parts[i]
    return (lanes[0] + lanes[1]) + (lanes[2] + lanes[3])


def last_kernel(ints, flts, parts, own, surf, field, interface):
    core = ints[0]
    total = sum_parts(parts)
    interface[...] = total.reshape(2, 512)
    temps = own[pl.ds(4 * ROWS, 8), :]
    temps = jnp.where(core == 0, temps[:4], temps[4:])
    inc = flts[0] * (total[:4] - temps) + flts[1] * total[4:]
    add = scatter_block(surf[pl.ds(2 + core, 1)][0], inc)
    start = pl.multiple_of(core * 2 * ROWS, 2 * ROWS)
    field[...] = (own[pl.ds(start, 2 * ROWS), :] + add).reshape(2, 128 * ROWS)


def patch_kernel(ints, flts, source, place, targets, turned, out, maps, sem, *, final):
    slots = place.shape[0]
    copy = pltpu.make_async_copy(turned, maps, sem)
    copy.start()
    parts = 2 if final else 1
    lanes = [place[pl.ds(8 * w, 8), :] & 127 for w in range(slots // 8)]
    rows = [place[pl.ds(8 * w, 8), :] >> 7 for w in range(slots // 8)]
    vals = [[jnp.zeros((8, 128), F32) for _ in rows] for _ in range(parts)]
    for i in range(3):
        tile = source[ints[3 + i]]
        for q in range(parts):
            for j in range(4):
                line = jnp.broadcast_to(tile[4 * q + j : 4 * q + j + 1], (8, 128))
                for w in range(slots // 8):
                    got = jnp.take_along_axis(line, lanes[w], axis=1, mode="promise_in_bounds")
                    vals[q][w] = jnp.where(rows[w] == 4 * i + j, got, vals[q][w])
    live = ints[1]
    columns = []
    for q in range(parts):
        held = [jnp.where(iota((8, 128), 0) + 8 * w < live, vals[q][w], 0.0) for w in range(slots // 8)]
        full = jnp.concatenate(held + [jnp.zeros((128 - slots, 128), F32)], axis=0)
        columns.append(full.T)
    copy.wait()
    left, right = [], [[] for _ in range(parts)]
    for s in range(slots):
        aim = targets[s : s + 1, :]
        left.append(jnp.where(iota((128, 128), 0) == aim >> 7, 1.0, 0.0).astype(BF16))
        hit = iota((128, 128), 0) == (aim & 127)
        table = maps[s]
        for q in range(parts):
            value = jnp.sum(table * columns[q][:, s : s + 1], axis=0, keepdims=True)
            top = value.astype(BF16).astype(F32)
            right[q].append(
                jnp.concatenate(
                    [jnp.where(hit, top, 0.0).astype(BF16), jnp.where(hit, value - top, 0.0).astype(BF16)],
                    axis=0,
                )
            )
    lhs = jnp.concatenate(left, axis=1)
    sums = []
    for q in range(parts):
        both = lax.dot_general(
            lhs, jnp.concatenate(right[q], axis=1), (((1,), (1,)), ((), ())), preferred_element_type=F32
        )
        sums.append(both[:, :128] + both[:, 128:])
    chips = out.shape[0] // 2
    for c in range(chips):
        if final:
            for k in range(2):
                r = 2 * c + k
                out[r] = jnp.concatenate([s[4 * r : 4 * r + 4] for s in sums], axis=0)
        else:
            for side in range(3):
                n = c + side - 1
                piece = sums[0][8 * n : 8 * n + 8] if 0 <= n < chips else jnp.zeros((8, 128), F32)
                for k in range(2):
                    out[2 * c + k, pl.ds(8 * side, 8), :] = piece


def call(kernel, ins, outs, scratch=()):
    where = {"s": SMEM, "v": VMEM, "h": pl.ANY}
    return pl.pallas_call(
        kernel,
        out_shape=[jax.ShapeDtypeStruct(s, d) for s, d, _ in outs],
        in_specs=[pl.BlockSpec(memory_space=where[i]) for i in ins],
        out_specs=[pl.BlockSpec(memory_space=where[o]) for _, _, o in outs],
        scratch_shapes=[pltpu.VMEM(s, F32) if s else pltpu.SemaphoreType.DMA for s in scratch],
        compiler_params=pltpu.CompilerParams(vmem_limit_bytes=16 * 1024 * 1024),
    )


def local(
    initial_field,
    conduct,
    velocity,
    heat_release,
    group_kind,
    partner,
    surface_cell,
    patch_count,
    patch_centres,
    patch_targets,
    patch_maps,
):
    subs = lax.axis_size("sub")
    groups = lax.axis_size("grp")
    block = surface_cell.shape[1]
    slots = patch_maps.shape[1]
    planes, cells = initial_field.shape[1:]

    (payload,) = call(pack_kernel, "vvvvv", [((1032, 128), F32, "v")])(
        *(a.reshape(planes, cells) for a in (initial_field, conduct, velocity, heat_release)),
        surface_cell,
    )
    up = [(i, i + 2) for i in range(subs - 2)]
    down = [(i + 2, i) for i in range(subs - 2)]
    swap = [(i, i ^ 1) for i in range(subs)]
    left = lax.ppermute(payload, "sub", up)
    right = lax.ppermute(payload, "sub", down)
    mate = lax.ppermute(payload, "sub", swap)
    ints, flts, place, turned = call(
        prepare_kernel,
        "sssvv",
        [
            ((6,), jnp.int32, "s"),
            ((5,), F32, "s"),
            ((slots, 128), jnp.int32, "v"),
            ((slots, 128, 128), F32, "v"),
        ],
    )(group_kind, partner, patch_count, patch_centres[0], patch_maps[0])
    targets = patch_targets[0]
    left_mate = lax.ppermute(left, "sub", swap)
    right_mate = lax.ppermute(right, "sub", swap)

    keep_out = ((4 * ROWS + 8, 128), F32, "v")
    half_out = ((groups * subs, 4, 128), F32, "v")
    full_out = ((groups * subs, 8, 128), F32, "v")
    coef_shape = (3, WIDE - 2, ROWS, 128)
    work = [(WIDE, ROWS, 128), (WIDE, ROWS, 128), (2 * ROWS, 128), coef_shape, None]
    keep, send, coef, surf = call(
        first_kernel,
        "ssvvvvvv",
        [keep_out, half_out, (coef_shape, F32, "h"), ((6, 4, 128), jnp.int32, "v")],
        work,
    )(ints, flts, payload, mate, left, left_mate, right, right_mate)
    for iteration in range(COUPLE):
        final = iteration == COUPLE - 1
        if not final:
            left = lax.ppermute(keep, "sub", up)
            right = lax.ppermute(keep, "sub", down)
        source = lax.all_to_all(send, ("grp", "sub"), 0, 0, tiled=True)
        (parts,) = call(
            functools.partial(patch_kernel, final=final),
            "ssvvvh",
            [((subs, 8 if final else 24, 128), F32, "v")],
            [(slots, 128, 128), None],
        )(ints, flts, source, place, targets, turned)
        parts = lax.all_to_all(parts, "sub", 0, 0, tiled=True)
        if final:
            field, interface = call(
                last_kernel, "ssvvv", [((planes, cells), F32, "v"), ((2, block), F32, "v")]
            )(ints, flts, parts, keep, surf)
        else:
            full = iteration == COUPLE - 2
            keep, send = call(
                functools.partial(middle_kernel, full=full),
                "ssvvvvvh",
                [keep_out, full_out if full else half_out],
                work,
            )(ints, flts, parts, keep, left, right, surf, coef)
    return field[None], interface[None]


def solution(mesh):
    placed = (
        P("grp", "sub", None),
        P("grp", "sub", None),
        P("grp", "sub", None),
        P("grp", "sub", None),
        P(),
        P(),
        P("grp", "sub"),
        P("grp", None),
        P("grp", "sub", None),
        P("grp", "sub", None),
        P("grp", "sub", None, None),
    )
    return jax.shard_map(
        local,
        mesh=mesh,
        in_specs=placed,
        out_specs=(P("grp", "sub", None), P("grp", None, "sub")),
        check_vma=False,
    )
```

time: 278 us -> 233 us (0.84)
  Pallas kernels: 50.3 us -> 32.8 us
  blocking collectives: 78.6 us -> 95.4 us
  local copies, waits for them, and re-layouts: 43.8 us -> 28.9 us
  waiting for transfers between devices: 45.8 us -> 31.9 us
  starting transfers between devices: 51.4 us -> 41.4 us
  other arithmetic: 3.45 us -> 0 us
    pallas_call x9 -> x11, Pallas kernels: 50.3 us -> 32.8 us  [the longest x3 17.4 us: local(): call(functools.partial(middle_kernel, full=full), 'ssvvvvvh', [keep_out,...]
    all_to_all x3 -> x4, blocking collectives: 66.5 us -> 83.4 us  [local(): source = lax.all_to_all(send, ('grp', 'sub'), 0, 0, tiled=True)]
    ppermute x3, waiting for transfers between devices: 13.9 us -> 0.01 us  [local(): left = lax.ppermute(keep, 'sub', up)]
    ppermute x3, waiting for transfers between devices: 10.4 us -> 23.2 us  [local(): right = lax.ppermute(keep, 'sub', down)]
    all_to_all x1 -> x0, starting transfers between devices: 10.9 us -> none  [local(): source = lax.all_to_all(send, ('grp', 'sub'), 0, 0, tiled=True)]
    all_to_all x1 -> x0, waiting for transfers between devices: 10.6 us -> none  [local(): source = lax.all_to_all(send, ('grp', 'sub'), 0, 0, tiled=True)]
    ppermute x1, waiting for transfers between devices: 8.31 us -> 0.01 us  [local(): left = lax.ppermute(payload, 'sub', up)]
    unnamed x105 -> x88, local copies, waits for them, and re-layouts: 35.3 us -> 28.9 us
  transfers between devices with their start and end apart: 15 -> 14, of which waited for: 8 -> 4; matrix products, arithmetic and copies ran while one was open for 3% -> 0% of each run, Pallas kernels for 0% -> 1%
where the time goes in v1:
time: 233 us; the launch traced here: 231 us
  blocking collectives  95.4 us (41%)
  starting transfers between devices  41.4 us (18%)
  Pallas kernels  32.8 us (14%)
  waiting for transfers between devices  31.9 us (14%)
  local copies, waits for them, and re-layouts  28.9 us (12%)
    all_to_all x4, blocking collectives, local(): source = lax.all_to_all(send, ('grp', 'sub'), 0, 0, tiled=True)  83.4 us
    unnamed x88, local copies, waits for them, and re-layouts  28.9 us
    ppermute x3, waiting for transfers between devices, local(): right = lax.ppermute(keep, 'sub', down)  23.2 us
    pallas_call x3, Pallas kernels, local(): call(functools.partial(middle_kernel, full=full), 'ssvvvvvh', [keep_out,...  17.4 us
    all_to_all x3, starting transfers between devices, local(): parts = lax.all_to_all(parts, 'sub', 0, 0, tiled=True)  15.7 us
    all_to_all x1, blocking collectives, local(): parts = lax.all_to_all(parts, 'sub', 0, 0, tiled=True)  12.1 us
    ppermute x3, starting transfers between devices, local(): left = lax.ppermute(keep, 'sub', up)  12 us
    ppermute x1, waiting for transfers between devices, local(): right = lax.ppermute(payload, 'sub', down)  8.71 us
  transfers between devices with their start and end apart: 14, of which 4 were waited for; matrix products, arithmetic and copies ran while one was open for 0% of the time, Pallas kernels for 1%

profile of v1, /device:TPU:1, one launch (start us, length us, event | category | flops | bytes accessed | tf_op | source)
XLA Modules:
  0.0 231.4 jit_solution(5275797724510558174)
XLA Ops:
  0.6 0.9 copy-done.31
  1.5 0.9 copy-done.32
  2.4 0.9 copy-done.33
  3.3 0.9 copy-done.34
  4.3 0.7 copy-done.40
  5.0 1.3 collective-permute-start.3
  6.3 5.0 %collective-permute-start.1 = (f32[1032,128]{1,0:T(8,128)S(1)}, f32[1032,128]{1,0:T(8,128)S(1)}, u32[]{:S(2)}, u32[]{:S(2)}) collective-permute-start(f32[1032,128]{1,0:T(8,128)S(1)} %shard_map.123.own), channel_id=1, source_target_pairs={{0,2},{1,3},{2,4},{3,5},{4,6},{5,7},{6,8},{7,9},{8,10},{9,11},{10,... | collective-permute-start | bytes 1585160 | tf_op jit(solution)/shard_map/ppermute | solution.py:356
  11.3 1.0 collective-permute-start
  12.4 8.7 %collective-permute-done.3.right = f32[1032,128]{1,0:T(8,128)S(1)} collective-permute-done((f32[1032,128]{1,0:T(8,128)S(1)}, f32[1032,128]{1,0:T(8,128)S(1)}, u32[]{:S(2)}, u32[]{:S(2)}) %collective-permute-start.3) | collective-permute-done | bytes 528416 | tf_op jit(solution)/shard_map/ppermute | solution.py:357
  21.1 1.3 collective-permute-start.4
  22.3 1.2 collective-permute-start.2
  23.5 1.4 copy-done
  24.9 0.7 copy-done.39
  25.6 0.7 copy-done.41
  27.6 1.3 shard_map.122
  29.0 4.7 %shard_map.124 = (f32[520,128]{1,0:T(8,128)S(1)}, f32[128,4,128]{2,1,0:T(4,128)S(1)}, f32[3,10,128,128]{3,2,1,0:T(8,128)S(1)}, s32[6,4,128]{2,1,0:T(4,128)S(1)}) custom-call(s32[6]{0:T(128)S(1)} %get-tuple-element.18.ints, f32[5]{0:T(128)S(1)} %get-tuple-element.19.flts, f32[1032,128]{1,0:T(8,128)S(1)} %shard_map.123.own, ...), custom_call_target="tpu_custom_call" | custom-call | tf_op jit(solution)/shard_map/pallas_call | solution.py:378
  33.7 23.8 %all_to_all.40.source = f32[128,4,128]{2,1,0:T(4,128)S(1)} all-to-all(f32[128,4,128]{2,1,0:T(4,128)S(1)} %get-tuple-element.20), channel_id=1, replica_groups=mesh['grp'=4,'sub'=32] {'grp','sub'}, dimensions={0} | all-to-all | bytes 524288 | tf_op jit(solution)/shard_map/all_to_all | solution.py:389
  57.5 1.8 shard_map.125
  59.3 0.7 copy-done.3
  60.1 5.3 %all-to-all-start.1 = ((f32[32,24,128]{2,1,0:T(8,128)}), f32[32,24,128]{2,1,0:T(8,128)}, u32[]{:S(2)}, u32[]{:S(2)}) async-start(f32[32,24,128]{2,1,0:T(8,128)} %copy-done.3), calls=%async_computation.1 | async-start | bytes 786432 | tf_op jit(solution)/shard_map/all_to_all | solution.py:396
  65.3 1.3 collective-permute-start.6
  66.6 4.0 %collective-permute-start.5 = (f32[520,128]{1,0:T(8,128)}, f32[520,128]{1,0:T(8,128)S(1)}, u32[]{:S(2)}, u32[]{:S(2)}) collective-permute-start(f32[520,128]{1,0:T(8,128)} %copy-done.4), channel_id=1, source_target_pairs={{0,2},{1,3},{2,4},{3,5},{4,6},{5,7},{6,8},{7,9},{8,10},{9,11},{10,... | collective-permute-start | bytes 798728 | tf_op jit(solution)/shard_map/ppermute | solution.py:387
  70.6 7.7 %collective-permute-done.6.right = f32[520,128]{1,0:T(8,128)S(1)} collective-permute-done((f32[520,128]{1,0:T(8,128)}, f32[520,128]{1,0:T(8,128)S(1)}, u32[]{:S(2)}, u32[]{:S(2)}) %collective-permute-start.6) | collective-permute-done | bytes 266272 | tf_op jit(solution)/shard_map/ppermute | solution.py:388
  78.4 0.7 copy-done.10
  79.1 0.7 copy-done.16
  79.8 1.0 copy-done.5
  80.7 0.9 copy-done.11
  81.7 0.9 copy-done.17
  82.6 0.7 copy-done.28
  84.0 5.8 %shard_map.126 = (f32[520,128]{1,0:T(8,128)S(1)}, f32[128,4,128]{2,1,0:T(4,128)S(1)}) custom-call(s32[6]{0:T(128)S(1)} %get-tuple-element.18.ints, f32[5]{0:T(128)S(1)} %copy-done.36, f32[32,24,128]{2,1,0:T(8,128)} %all-to-all-done.1.parts, f32[520,128]{1,0:T(8,128)S(1)} %copy-done.5, f32[520,128]{1,0:T(8,128)S(1)} %copy-done.17, f32[520,128]{1,0:T(8,128)S(1)} %copy-done.11, ...), custom_call_target="tpu_custom_call" | custom-call | tf_op jit(solution)/shard_map/pallas_call | solution.py:403
  89.8 0.7 copy-done.8
  90.5 19.0 %all_to_all.41.source = f32[128,4,128]{2,1,0:T(4,128)S(1)} all-to-all(f32[128,4,128]{2,1,0:T(4,128)S(1)} %get-tuple-element.26), channel_id=1, replica_groups=mesh['grp'=4,'sub'=32] {'grp','sub'}, dimensions={0} | all-to-all | bytes 524288 | tf_op jit(solution)/shard_map/all_to_all | solution.py:389
  109.5 1.8 shard_map.127
  111.4 0.7 copy-done.1
  112.1 5.3 %all-to-all-start.3 = ((f32[32,24,128]{2,1,0:T(8,128)}), f32[32,24,128]{2,1,0:T(8,128)}, u32[]{:S(2)}, u32[]{:S(2)}) async-start(f32[32,24,128]{2,1,0:T(8,128)} %copy-done.1), calls=%async_computation.3 | async-start | bytes 786432 | tf_op jit(solution)/shard_map/all_to_all | solution.py:396
  117.3 1.3 collective-permute-start.8
  118.6 4.0 %collective-permute-start.7 = (f32[520,128]{1,0:T(8,128)}, f32[520,128]{1,0:T(8,128)S(1)}, u32[]{:S(2)}, u32[]{:S(2)}) collective-permute-start(f32[520,128]{1,0:T(8,128)} %copy-done.8), channel_id=1, source_target_pairs={{0,2},{1,3},{2,4},{3,5},{4,6},{5,7},{6,8},{7,9},{8,10},{9,11},{10,... | collective-permute-start | bytes 798728 | tf_op jit(solution)/shard_map/ppermute | solution.py:387
  122.7 7.7 %collective-permute-done.8.right = f32[520,128]{1,0:T(8,128)S(1)} collective-permute-done((f32[520,128]{1,0:T(8,128)}, f32[520,128]{1,0:T(8,128)S(1)}, u32[]{:S(2)}, u32[]{:S(2)}) %collective-permute-start.8) | collective-permute-done | bytes 266272 | tf_op jit(solution)/shard_map/ppermute | solution.py:388
  130.4 0.7 copy-done.14
  131.1 0.7 copy-done.20
  131.8 1.0 copy-done.9
  132.8 0.9 copy-done.15
  133.7 0.9 copy-done.21
  134.7 0.7 copy-done.29
  136.0 5.8 %shard_map.128 = (f32[520,128]{1,0:T(8,128)S(1)}, f32[128,4,128]{2,1,0:T(4,128)S(1)}) custom-call(s32[6]{0:T(128)S(1)} %get-tuple-element.18.ints, f32[5]{0:T(128)S(1)} %copy-done.37, f32[32,24,128]{2,1,0:T(8,128)} %all-to-all-done.3.parts, f32[520,128]{1,0:T(8,128)S(1)} %copy-done.9, f32[520,128]{1,0:T(8,128)S(1)} %copy-done.21, f32[520,128]{1,0:T(8,128)S(1)} %copy-done.15, ...), custom_call_target="tpu_custom_call" | custom-call | tf_op jit(solution)/shard_map/pallas_call | solution.py:403
  141.8 0.7 copy-done.6
  142.5 19.0 %all_to_all.42.source = f32[128,4,128]{2,1,0:T(4,128)S(1)} all-to-all(f32[128,4,128]{2,1,0:T(4,128)S(1)} %get-tuple-element.28), channel_id=1, replica_groups=mesh['grp'=4,'sub'=32] {'grp','sub'}, dimensions={0} | all-to-all | bytes 524288 | tf_op jit(solution)/shard_map/all_to_all | solution.py:389
  161.5 1.8 shard_map.129
  163.4 0.7 copy-done.2
  164.1 5.2 %all-to-all-start.5 = ((f32[32,24,128]{2,1,0:T(8,128)}), f32[32,24,128]{2,1,0:T(8,128)}, u32[]{:S(2)}, u32[]{:S(2)}) async-start(f32[32,24,128]{2,1,0:T(8,128)} %copy-done.2), calls=%async_computation.5 | async-start | bytes 786432 | tf_op jit(solution)/shard_map/all_to_all | solution.py:396
  169.4 1.3 collective-permute-start.10
  170.7 4.0 %collective-permute-start.9 = (f32[520,128]{1,0:T(8,128)}, f32[520,128]{1,0:T(8,128)S(1)}, u32[]{:S(2)}, u32[]{:S(2)}) collective-permute-start(f32[520,128]{1,0:T(8,128)} %copy-done.6), channel_id=1, source_target_pairs={{0,2},{1,3},{2,4},{3,5},{4,6},{5,7},{6,8},{7,9},{8,10},{9,11},{10,... | collective-permute-start | bytes 798728 | tf_op jit(solution)/shard_map/ppermute | solution.py:387
  174.7 7.7 %collective-permute-done.10.right = f32[520,128]{1,0:T(8,128)S(1)} collective-permute-done((f32[520,128]{1,0:T(8,128)}, f32[520,128]{1,0:T(8,128)S(1)}, u32[]{:S(2)}, u32[]{:S(2)}) %collective-permute-start.10) | collective-permute-done | bytes 266272 | tf_op jit(solution)/shard_map/ppermute | solution.py:388
  182.4 0.7 copy-done.12
  183.1 0.7 copy-done.18
  183.8 1.0 copy-done.7
  184.8 0.9 copy-done.13
  185.7 0.9 copy-done.19
  186.7 0.7 copy-done.30
  188.0 5.8 %shard_map.130 = (f32[520,128]{1,0:T(8,128)S(1)}, f32[128,8,128]{2,1,0:T(8,128)S(1)}) custom-call(s32[6]{0:T(128)S(1)} %get-tuple-element.18.ints, f32[5]{0:T(128)S(1)} %copy-done.38, f32[32,24,128]{2,1,0:T(8,128)} %all-to-all-done.5.parts, f32[520,128]{1,0:T(8,128)S(1)} %copy-done.7, f32[520,128]{1,0:T(8,128)S(1)} %copy-done.19, f32[520,128]{1,0:T(8,128)S(1)} %copy-done.13, ...), custom_call_target="tpu_custom_call" | custom-call | tf_op jit(solution)/shard_map/pallas_call | solution.py:403
  193.8 21.6 %all_to_all.43.source = f32[128,8,128]{2,1,0:T(8,128)S(1)} all-to-all(f32[128,8,128]{2,1,0:T(8,128)S(1)} %get-tuple-element.30), channel_id=1, replica_groups=mesh['grp'=4,'sub'=32] {'grp','sub'}, dimensions={0} | all-to-all | bytes 1048576 | tf_op jit(solution)/shard_map/all_to_all | solution.py:389
  215.5 2.3 %shard_map.131 = f32[32,8,128]{2,1,0:T(8,128)S(1)} custom-call(s32[6]{0:T(128)S(1)} %get-tuple-element.18.ints, f32[5]{0:T(128)S(1)} %copy-done.38, f32[128,8,128]{2,1,0:T(8,128)S(1)} %all_to_all.43.source, s32[24,128]{1,0:T(8,128)S(1)} %copy-done.26, s32[24,128]{1,0:T(8,128)S(1)} %bitcast.13, f32[24,128,128]{2,1,0:T(8,128)S(1)} %get-tuple-element.22.turned), custom_call_target="tpu_custom_call" | custom-call | tf_op jit(solution)/shard_map/pallas_call | solution.py:390
  217.8 12.1 %all_to_all.44.parts = f32[32,8,128]{2,1,0:T(8,128)S(1)} all-to-all(f32[32,8,128]{2,1,0:T(8,128)S(1)} %shard_map.131), channel_id=1, replica_groups=mesh['grp'=4,'sub'=32] {'sub'}, dimensions={0} | all-to-all | bytes 262144 | tf_op jit(solution)/shard_map/all_to_all | solution.py:396
  229.9 1.5 shard_map.132
  (68 shorter events, 3.4 us)
Async XLA Ops:
  0.6 0.9 copy-start.31
  1.5 0.9 copy-start.32
  2.4 0.9 copy-start.33
  3.3 0.9 copy-start.34
  4.3 0.7 copy-start.40
  5.0 16.1 %collective-permute-start.3 = (f32[1032,128]{1,0:T(8,128)S(1)}, f32[1032,128]{1,0:T(8,128)S(1)}, u32[]{:S(2)}, u32[]{:S(2)}) collective-permute-start(f32[1032,128]{1,0:T(8,128)S(1)} %shard_map.123.own), channel_id=1, source_target_pairs={{2,0},{3,1},{4,2},{5,3},{6,4},{7,5},{8,6},{9,7},{10,8},{11,9},{12,... | collective-permute-start | bytes 1585160 | tf_op jit(solution)/shard_map/ppermute | solution.py:357
  6.3 16.0 %collective-permute-start.1 = (f32[1032,128]{1,0:T(8,128)S(1)}, f32[1032,128]{1,0:T(8,128)S(1)}, u32[]{:S(2)}, u32[]{:S(2)}) collective-permute-start(f32[1032,128]{1,0:T(8,128)S(1)} %shard_map.123.own), channel_id=1, source_target_pairs={{0,2},{1,3},{2,4},{3,5},{4,6},{5,7},{6,8},{7,9},{8,10},{9,11},{10,... | collective-permute-start | bytes 1585160 | tf_op jit(solution)/shard_map/ppermute | solution.py:356
  11.3 17.6 %collective-permute-start = (f32[1032,128]{1,0:T(8,128)S(1)}, f32[1032,128]{1,0:T(8,128)S(1)}, u32[]{:S(2)}, u32[]{:S(2)}) collective-permute-start(f32[1032,128]{1,0:T(8,128)S(1)} %shard_map.123.own), channel_id=1, source_target_pairs={{0,1},{1,0},{2,3},{3,2},{4,5},{5,4},{6,7},{7,6},{8,9},{9,8},{10,11... | collective-permute-start | bytes 1585160 | tf_op jit(solution)/shard_map/ppermute | solution.py:358
  21.1 7.9 %collective-permute-start.4 = (f32[1032,128]{1,0:T(8,128)S(1)}, f32[1032,128]{1,0:T(8,128)S(1)}, u32[]{:S(2)}, u32[]{:S(2)}) collective-permute-start(f32[1032,128]{1,0:T(8,128)S(1)} %collective-permute-done.3.right), channel_id=1, source_target_pairs={{0,1},{1,0},{2,3},{3,2},{4,5},{5,4},{6,7},{7,6},{8,9},{9,8},{10,11... | collective-permute-start | bytes 1585160 | tf_op jit(solution)/shard_map/ppermute | solution.py:371
  22.3 6.6 %collective-permute-start.2 = (f32[1032,128]{1,0:T(8,128)S(1)}, f32[1032,128]{1,0:T(8,128)S(1)}, u32[]{:S(2)}, u32[]{:S(2)}) collective-permute-start(f32[1032,128]{1,0:T(8,128)S(1)} %collective-permute-done.1.left), channel_id=1, source_target_pairs={{0,1},{1,0},{2,3},{3,2},{4,5},{5,4},{6,7},{7,6},{8,9},{9,8},{10,11... | collective-permute-start | bytes 1585160 | tf_op jit(solution)/shard_map/ppermute | solution.py:370
  23.5 1.4 copy-start
  24.9 0.7 copy-start.39
  25.6 0.7 copy-start.41
  26.3 0.7 copy-start.42
  26.9 0.7 copy-start.43
  28.9 28.6 %copy-start.23 = (s32[24,128]{1,0:T(8,128)}, s32[24,128]{1,0:T(8,128)S(1)}, u32[]{:S(2)}) copy-start(s32[24,128]{1,0:T(8,128)S(1)} %get-tuple-element.21.place) | copy-start | bytes 36868
  28.9 28.5 %copy-start.35 = (f32[5]{0:T(128)}, f32[5]{0:T(128)S(1)}, u32[]{:S(2)}) copy-start(f32[5]{0:T(128)S(1)} %get-tuple-element.19.flts) | copy-start | bytes 64
  29.0 28.5 %copy-start.22 = (s32[1,24,128]{2,1,0:T(8,128)S(1)}, s32[1,24,128]{2,1,0:T(8,128)}, u32[]{:S(2)}) copy-start(s32[1,24,128]{2,1,0:T(8,128)} %param.20) | copy-start | bytes 36868
  33.7 23.8 %copy-start.4 = (f32[520,128]{1,0:T(8,128)}, f32[520,128]{1,0:T(8,128)S(1)}, u32[]{:S(2)}) copy-start(f32[520,128]{1,0:T(8,128)S(1)} %get-tuple-element.23.own) | copy-start | bytes 798724
  33.7 23.8 %copy-start.27 = (s32[6,4,128]{2,1,0:T(4,128)}, s32[6,4,128]{2,1,0:T(4,128)S(1)}, u32[]{:S(2)}) copy-start(s32[6,4,128]{2,1,0:T(4,128)S(1)} %get-tuple-element.24.surf) | copy-start | bytes 36868
  59.3 0.7 copy-start.3
  60.1 19.7 %all-to-all-start.1 = ((f32[32,24,128]{2,1,0:T(8,128)}), f32[32,24,128]{2,1,0:T(8,128)}, u32[]{:S(2)}, u32[]{:S(2)}) async-start(f32[32,24,128]{2,1,0:T(8,128)} %copy-done.3), calls=%async_computation.1 | async-start | bytes 786432 | tf_op jit(solution)/shard_map/all_to_all | solution.py:396
  65.3 13.0 %collective-permute-start.6 = (f32[520,128]{1,0:T(8,128)}, f32[520,128]{1,0:T(8,128)S(1)}, u32[]{:S(2)}, u32[]{:S(2)}) collective-permute-start(f32[520,128]{1,0:T(8,128)} %copy-done.4), channel_id=1, source_target_pairs={{2,0},{3,1},{4,2},{5,3},{6,4},{7,5},{8,6},{9,7},{10,8},{11,9},{12,... | collective-permute-start | bytes 798728 | tf_op jit(solution)/shard_map/ppermute | solution.py:388
  66.6 12.4 %collective-permute-start.5 = (f32[520,128]{1,0:T(8,128)}, f32[520,128]{1,0:T(8,128)S(1)}, u32[]{:S(2)}, u32[]{:S(2)}) collective-permute-start(f32[520,128]{1,0:T(8,128)} %copy-done.4), channel_id=1, source_target_pairs={{0,2},{1,3},{2,4},{3,5},{4,6},{5,7},{6,8},{7,9},{8,10},{9,11},{10,... | collective-permute-start | bytes 798728 | tf_op jit(solution)/shard_map/ppermute | solution.py:387
  78.4 0.7 copy-start.10
  79.1 0.7 copy-start.16
  79.8 1.0 copy-start.5
  80.7 1.0 copy-start.11
  81.7 1.0 copy-start.17
  82.6 0.7 copy-start.28
  83.3 0.7 copy-start.36
  84.0 25.5 %copy-start.24 = (s32[24,128]{1,0:T(8,128)S(1)}, s32[24,128]{1,0:T(8,128)}, u32[]{:S(2)}) copy-start(s32[24,128]{1,0:T(8,128)} %copy-done.23) | copy-start | bytes 36868
  89.8 0.7 copy-start.8
  111.3 0.7 copy-start.1
  112.1 19.7 %all-to-all-start.3 = ((f32[32,24,128]{2,1,0:T(8,128)}), f32[32,24,128]{2,1,0:T(8,128)}, u32[]{:S(2)}, u32[]{:S(2)}) async-start(f32[32,24,128]{2,1,0:T(8,128)} %copy-done.1), calls=%async_computation.3 | async-start | bytes 786432 | tf_op jit(solution)/shard_map/all_to_all | solution.py:396
  117.3 13.0 %collective-permute-start.8 = (f32[520,128]{1,0:T(8,128)}, f32[520,128]{1,0:T(8,128)S(1)}, u32[]{:S(2)}, u32[]{:S(2)}) collective-permute-start(f32[520,128]{1,0:T(8,128)} %copy-done.8), channel_id=1, source_target_pairs={{2,0},{3,1},{4,2},{5,3},{6,4},{7,5},{8,6},{9,7},{10,8},{11,9},{12,... | collective-permute-start | bytes 798728 | tf_op jit(solution)/shard_map/ppermute | solution.py:388
  118.6 12.4 %collective-permute-start.7 = (f32[520,128]{1,0:T(8,128)}, f32[520,128]{1,0:T(8,128)S(1)}, u32[]{:S(2)}, u32[]{:S(2)}) collective-permute-start(f32[520,128]{1,0:T(8,128)} %copy-done.8), channel_id=1, source_target_pairs={{0,2},{1,3},{2,4},{3,5},{4,6},{5,7},{6,8},{7,9},{8,10},{9,11},{10,... | collective-permute-start | bytes 798728 | tf_op jit(solution)/shard_map/ppermute | solution.py:387
  130.4 0.7 copy-start.14
  131.1 0.7 copy-start.20
  131.8 1.0 copy-start.9
  132.8 1.0 copy-start.15
  133.7 1.0 copy-start.21
  134.7 0.7 copy-start.29
  135.4 0.7 copy-start.37
  136.0 25.5 %copy-start.25 = (s32[24,128]{1,0:T(8,128)S(1)}, s32[24,128]{1,0:T(8,128)}, u32[]{:S(2)}) copy-start(s32[24,128]{1,0:T(8,128)} %copy-done.23) | copy-start | bytes 36868
  141.8 0.7 copy-start.6
  163.4 0.7 copy-start.2
  164.1 19.7 %all-to-all-start.5 = ((f32[32,24,128]{2,1,0:T(8,128)}), f32[32,24,128]{2,1,0:T(8,128)}, u32[]{:S(2)}, u32[]{:S(2)}) async-start(f32[32,24,128]{2,1,0:T(8,128)} %copy-done.2), calls=%async_computation.5 | async-start | bytes 786432 | tf_op jit(solution)/shard_map/all_to_all | solution.py:396
  169.4 13.0 %collective-permute-start.10 = (f32[520,128]{1,0:T(8,128)}, f32[520,128]{1,0:T(8,128)S(1)}, u32[]{:S(2)}, u32[]{:S(2)}) collective-permute-start(f32[520,128]{1,0:T(8,128)} %copy-done.6), channel_id=1, source_target_pairs={{2,0},{3,1},{4,2},{5,3},{6,4},{7,5},{8,6},{9,7},{10,8},{11,9},{12,... | collective-permute-start | bytes 798728 | tf_op jit(solution)/shard_map/ppermute | solution.py:388
  170.7 12.4 %collective-permute-start.9 = (f32[520,128]{1,0:T(8,128)}, f32[520,128]{1,0:T(8,128)S(1)}, u32[]{:S(2)}, u32[]{:S(2)}) collective-permute-start(f32[520,128]{1,0:T(8,128)} %copy-done.6), channel_id=1, source_target_pairs={{0,2},{1,3},{2,4},{3,5},{4,6},{5,7},{6,8},{7,9},{8,10},{9,11},{10,... | collective-permute-start | bytes 798728 | tf_op jit(solution)/shard_map/ppermute | solution.py:387
  182.4 0.7 copy-start.12
  183.1 0.7 copy-start.18
  183.8 1.0 copy-start.7
  184.8 1.0 copy-start.13
  185.7 1.0 copy-start.19
  186.7 0.7 copy-start.30
  187.4 0.7 copy-start.38
  188.0 27.4 %copy-start.26 = (s32[24,128]{1,0:T(8,128)S(1)}, s32[24,128]{1,0:T(8,128)}, u32[]{:S(2)}) copy-start(s32[24,128]{1,0:T(8,128)} %copy-done.23) | copy-start | bytes 36868

commit v2 on v1

--- a/solution.py
+++ b/solution.py
@@ -6,6 +6,7 @@
 from jax.experimental import pallas as pl
 from jax.experimental.pallas import tpu as pltpu
 from jax.sharding import PartitionSpec as P
+
 
 STEPS = 4
 COUPLE = 4
@@ -132,9 +133,9 @@
     export[...] = jnp.broadcast_to(block[None], export.shape)
 
 
-def pack_kernel(field, conduct, velocity, heat, surface, payload):
-    for i, ref in enumerate((field, conduct, velocity, heat)):
-        payload[pl.ds(256 * i, 256), :] = ref[...].reshape(2 * ROWS, 128)
+def pack_kernel(fields, surface, payload):
+    for i in range(4):
+        payload[pl.ds(256 * i, 256), :] = fields[i].reshape(2 * ROWS, 128)
     cells = surface[...].reshape(4, 128).astype(F32)
     payload[pl.ds(1024, 8), :] = jnp.concatenate([cells, cells], axis=0)
 
@@ -170,7 +171,7 @@
 
 
 def first_kernel(ints, flts, own, mate, left, left_mate, right, right_mate,
-                 keep, export, saved, surf, cur, nxt, flux, coef, sem):
+                 keep, export, coef, surf, cur, nxt, flux):
     core = ints[0]
     other = 1 - core
     for base, mine, its in ((0, left, left_mate), (4, own, mate), (8, right, right_mate)):
@@ -211,28 +212,29 @@
         store(8, right_mate, 1)
         store(9, right, 0)
 
-    copy = pltpu.make_async_copy(coef, saved, sem)
-    copy.start()
     run_steps(cur, nxt, coef)
     finish(ints, flts, cur, coef, surf, flux, keep, export, False)
-    copy.wait()
-
-
-def middle_kernel(ints, flts, parts, own, left, right, surf, saved, keep, export,
-                  cur, nxt, flux, coef, sem, *, full):
-    copy = pltpu.make_async_copy(saved, coef, sem)
-    copy.start()
+
+
+def middle_kernel(ints, flts, parts, own, beside, other, surf, coef, keep, export,
+                  cur, nxt, flux, *, full):
+    first = ints[0] == 0
     total = sum_parts(parts)
-    for side, ref in enumerate((left, own, right)):
-        temps = ref[pl.ds(4 * ROWS, 8), :]
-        inc = total[8 * side : 8 * side + 8] - flts[0] * temps
-        for half in range(2):
+
+    def sides(start, size):
+        near = beside[pl.ds(start, size), :]
+        far = other[pl.ds(start, size), :]
+        return jnp.where(first, near, far), own[pl.ds(start, size), :], jnp.where(first, far, near)
+
+    temps = sides(4 * ROWS, 8)
+    incs = [total[8 * side : 8 * side + 8] - flts[0] * temps[side] for side in range(3)]
+    for half in range(2):
+        planes = sides(2 * half * ROWS, 2 * ROWS)
+        for side in range(3):
             block = 2 * side + half
-            add = scatter_block(surf[block], inc[4 * half : 4 * half + 4])
-            for p in range(2):
-                row = (2 * half + p) * ROWS
-                cur[2 * block + p] = ref[pl.ds(row, ROWS), :] + add[p * ROWS : (p + 1) * ROWS]
-    copy.wait()
+            out = planes[side] + scatter_block(surf[block], incs[side][4 * half : 4 * half + 4])
+            cur[2 * block] = out[:ROWS]
+            cur[2 * block + 1] = out[ROWS:]
     run_steps(cur, nxt, coef)
     finish(ints, flts, cur, coef, surf, flux, keep, export, full)
 
@@ -256,10 +258,8 @@
     field[...] = (own[pl.ds(start, 2 * ROWS), :] + add).reshape(2, 128 * ROWS)
 
 
-def patch_kernel(ints, flts, source, place, targets, turned, out, maps, sem, *, final):
+def patch_kernel(ints, flts, source, place, targets, maps, out, *, final):
     slots = place.shape[0]
-    copy = pltpu.make_async_copy(turned, maps, sem)
-    copy.start()
     parts = 2 if final else 1
     lanes = [place[pl.ds(8 * w, 8), :] & 127 for w in range(slots // 8)]
     rows = [place[pl.ds(8 * w, 8), :] >> 7 for w in range(slots // 8)]
@@ -278,7 +278,6 @@
         held = [jnp.where(iota((8, 128), 0) + 8 * w < live, vals[q][w], 0.0) for w in range(slots // 8)]
         full = jnp.concatenate(held + [jnp.zeros((128 - slots, 128), F32)], axis=0)
         columns.append(full.T)
-    copy.wait()
     left, right = [], [[] for _ in range(parts)]
     for s in range(slots):
         aim = targets[s : s + 1, :]
@@ -316,13 +315,13 @@
 
 
 def call(kernel, ins, outs, scratch=()):
-    where = {"s": SMEM, "v": VMEM, "h": pl.ANY}
+    where = {"s": SMEM, "v": VMEM}
     return pl.pallas_call(
         kernel,
         out_shape=[jax.ShapeDtypeStruct(s, d) for s, d, _ in outs],
         in_specs=[pl.BlockSpec(memory_space=where[i]) for i in ins],
         out_specs=[pl.BlockSpec(memory_space=where[o]) for _, _, o in outs],
-        scratch_shapes=[pltpu.VMEM(s, F32) if s else pltpu.SemaphoreType.DMA for s in scratch],
+        scratch_shapes=[pltpu.VMEM(s, F32) for s in scratch],
         compiler_params=pltpu.CompilerParams(vmem_limit_bytes=16 * 1024 * 1024),
     )
 
@@ -346,13 +345,12 @@
     slots = patch_maps.shape[1]
     planes, cells = initial_field.shape[1:]
 
-    (payload,) = call(pack_kernel, "vvvvv", [((1032, 128), F32, "v")])(
-        *(a.reshape(planes, cells) for a in (initial_field, conduct, velocity, heat_release)),
-        surface_cell,
-    )
+    fields = jnp.concatenate([initial_field, conduct, velocity, heat_release], axis=0)
+    (payload,) = call(pack_kernel, "vv", [((1032, 128), F32, "v")])(fields, surface_cell)
     up = [(i, i + 2) for i in range(subs - 2)]
     down = [(i + 2, i) for i in range(subs - 2)]
     swap = [(i, i ^ 1) for i in range(subs)]
+    cross = [(i, i + 1 if i % 2 else i - 1) for i in range(1, subs - 1)]
     left = lax.ppermute(payload, "sub", up)
     right = lax.ppermute(payload, "sub", down)
     mate = lax.ppermute(payload, "sub", swap)
@@ -374,25 +372,28 @@
     half_out = ((groups * subs, 4, 128), F32, "v")
     full_out = ((groups * subs, 8, 128), F32, "v")
     coef_shape = (3, WIDE - 2, ROWS, 128)
-    work = [(WIDE, ROWS, 128), (WIDE, ROWS, 128), (2 * ROWS, 128), coef_shape, None]
+    work = [(WIDE, ROWS, 128), (WIDE, ROWS, 128), (2 * ROWS, 128)]
     keep, send, coef, surf = call(
         first_kernel,
         "ssvvvvvv",
-        [keep_out, half_out, (coef_shape, F32, "h"), ((6, 4, 128), jnp.int32, "v")],
+        [keep_out, half_out, (coef_shape, F32, "v"), ((6, 4, 128), jnp.int32, "v")],
         work,
     )(ints, flts, payload, mate, left, left_mate, right, right_mate)
     for iteration in range(COUPLE):
         final = iteration == COUPLE - 1
         if not final:
-            left = lax.ppermute(keep, "sub", up)
-            right = lax.ppermute(keep, "sub", down)
+            beside = lax.ppermute(keep, "sub", cross)
         source = lax.all_to_all(send, ("grp", "sub"), 0, 0, tiled=True)
+        if not final:
+            source, beside = lax.optimization_barrier((source, beside))
+            other = lax.ppermute(beside, "sub", swap)
         (parts,) = call(
             functools.partial(patch_kernel, final=final),
-            "ssvvvh",
+            "ssvvvv",
             [((subs, 8 if final else 24, 128), F32, "v")],
-            [(slots, 128, 128), None],
         )(ints, flts, source, place, targets, turned)
+        if not final:
+            parts, other = lax.optimization_barrier((parts, other))
         parts = lax.all_to_all(parts, "sub", 0, 0, tiled=True)
         if final:
             field, interface = call(
@@ -402,10 +403,10 @@
             full = iteration == COUPLE - 2
             keep, send = call(
                 functools.partial(middle_kernel, full=full),
-                "ssvvvvvh",
+                "ssvvvvvv",
                 [keep_out, full_out if full else half_out],
                 work,
-            )(ints, flts, parts, keep, left, right, surf, coef)
+            )(ints, flts, parts, keep, beside, other, surf, coef)
     return field[None], interface[None]
 
 

time: 233 us -> 192 us (0.82)
  blocking collectives: 95.4 us -> 128 us
  local copies, waits for them, and re-layouts: 28.9 us -> 2.66 us
  waiting for transfers between devices: 31.9 us -> 8.73 us
  starting transfers between devices: 41.4 us -> 20.8 us
  Pallas kernels: 32.8 us -> 29.4 us
    all_to_all x1 -> x4, blocking collectives: 12.1 us -> 53 us  [local(): parts = lax.all_to_all(parts, 'sub', 0, 0, tiled=True)]
    unnamed x88 -> x14, local copies, waits for them, and re-layouts: 28.9 us -> 2.66 us
    ppermute x6, waiting for transfers between devices: 23.2 us -> 0.02 us  [the longest x3 0.01 us: local(): beside = lax.ppermute(keep, 'sub', cross)]
    all_to_all x3 -> x0, starting transfers between devices: 15.7 us -> none  [local(): parts = lax.all_to_all(parts, 'sub', 0, 0, tiled=True)]
    all_to_all x4, blocking collectives: 83.4 us -> 74.8 us  [local(): source = lax.all_to_all(send, ('grp', 'sub'), 0, 0, tiled=True)]
    ppermute x6, starting transfers between devices: 15.9 us -> 11 us  [the longest x3 7.84 us: local(): beside = lax.ppermute(keep, 'sub', cross)]
    pallas_call x9, Pallas kernels: 30 us -> 26.6 us  [the longest x3 14.7 us: local(): call(functools.partial(middle_kernel, full=full), 'ssvvvvvv', [keep_out,...]
  transfers between devices with their start and end apart: 14 -> 11, of which waited for: 4 -> 1; matrix products, arithmetic and copies ran while one was open for 0% -> 0% of each run, Pallas kernels for 1% -> 3%
where the time goes in v2:
time: 192 us
  blocking collectives  128 us (67%)
  Pallas kernels  29.4 us (15%)
  starting transfers between devices  20.8 us (11%)
  waiting for transfers between devices  8.73 us (5%)
  local copies, waits for them, and re-layouts  2.66 us (1%)
    all_to_all x4, blocking collectives, local(): source = lax.all_to_all(send, ('grp', 'sub'), 0, 0, tiled=True)  74.8 us
    all_to_all x4, blocking collectives, local(): parts = lax.all_to_all(parts, 'sub', 0, 0, tiled=True)  53 us
    pallas_call x3, Pallas kernels, local(): call(functools.partial(middle_kernel, full=full), 'ssvvvvvv', [keep_out,...  14.7 us
    ppermute x1, waiting for transfers between devices, local(): right = lax.ppermute(payload, 'sub', down)  8.71 us
    ppermute x3, starting transfers between devices, local(): beside = lax.ppermute(keep, 'sub', cross)  7.84 us
    pallas_call x4, Pallas kernels, local(): call(functools.partial(patch_kernel, final=final), 'ssvvvv', [((subs, 8 i...  7.48 us
    ppermute x1, starting transfers between devices, local(): left = lax.ppermute(payload, 'sub', up)  5.02 us
    pallas_call x1, Pallas kernels, local(): call(first_kernel, 'ssvvvvvv', [keep_out, half_out, (coef_shape, F32, 'v'...  4.37 us
  transfers between devices with their start and end apart: 11, of which 1 were waited for; matrix products, arithmetic and copies ran while one was open for 0% of the time, Pallas kernels for 3%

profile of v2, /device:TPU:1, one launch (start us, length us, event | category | flops | bytes accessed | tf_op | source)
XLA Modules:
  0.0 191.7 jit_solution(9713449419056820872)
XLA Ops:
  0.6 0.0 copy-start
  0.6 0.0 copy-start.2
  0.7 1.4 pad_maximum_fusion.fields
  2.1 0.0 copy-start.3
  2.1 0.7 copy-done.3
  2.8 0.1 shard_map.123.own
  2.8 1.3 collective-permute-start.3
  4.1 5.0 %collective-permute-start.1 = (f32[1032,128]{1,0:T(8,128)S(1)}, f32[1032,128]{1,0:T(8,128)S(1)}, u32[]{:S(2)}, u32[]{:S(2)}) collective-permute-start(f32[1032,128]{1,0:T(8,128)S(1)} %shard_map.123.own), channel_id=1, source_target_pairs={{0,2},{1,3},{2,4},{3,5},{4,6},{5,7},{6,8},{7,9},{8,10},{9,11},{10,... | collective-permute-start | bytes 1585160 | tf_op jit(solution)/shard_map/ppermute | solution.py:354
  9.2 1.0 collective-permute-start
  10.2 8.7 %collective-permute-done.3.right = f32[1032,128]{1,0:T(8,128)S(1)} collective-permute-done((f32[1032,128]{1,0:T(8,128)S(1)}, f32[1032,128]{1,0:T(8,128)S(1)}, u32[]{:S(2)}, u32[]{:S(2)}) %collective-permute-start.3) | collective-permute-done | bytes 528416 | tf_op jit(solution)/shard_map/ppermute | solution.py:355
  18.9 1.3 collective-permute-start.4
  20.2 0.0 collective-permute-done.1.left
  20.2 1.2 collective-permute-start.2
  21.3 0.0 copy-done
  21.4 0.0 copy-done.2
  21.4 0.0 copy-start.4
  21.4 0.7 copy-done.4
  22.0 0.0 copy-start.5
  22.0 0.7 copy-done.5
  22.7 0.0 copy-start.6
  22.7 0.7 copy-done.6
  23.3 1.3 shard_map.122
  24.7 0.0 collective-permute-done.mate
  24.7 0.0 collective-permute-done.4.right_mate
  24.7 0.0 collective-permute-done.2.left_mate
  24.7 0.0 copy-start.1
  24.7 4.4 %shard_map.124 = (f32[520,128]{1,0:T(8,128)S(1)}, f32[128,4,128]{2,1,0:T(4,128)S(1)}, f32[3,10,128,128]{3,2,1,0:T(8,128)S(1)}, s32[6,4,128]{2,1,0:T(4,128)S(1)}) custom-call(s32[6]{0:T(128)S(1)} %get-tuple-element.30.ints, f32[5]{0:T(128)S(1)} %get-tuple-element.31.flts, f32[1032,128]{1,0:T(8,128)S(1)} %shard_map.123.own, ...), custom_call_target="tpu_custom_call" | custom-call | tf_op jit(solution)/shard_map/pallas_call | solution.py:376
  29.1 4.0 %collective-permute-start.5 = (f32[520,128]{1,0:T(8,128)S(1)}, f32[520,128]{1,0:T(8,128)S(1)}, u32[]{:S(2)}, u32[]{:S(2)}) collective-permute-start(f32[520,128]{1,0:T(8,128)S(1)} %get-tuple-element.33.own), channel_id=1, source_target_pairs={{1,2},{2,1},{3,4},{4,3},{5,6},{6,5},{7,8},{8,7},{9,10},{10,9},{11,... | collective-permute-start | bytes 798728 | tf_op jit(solution)/shard_map/ppermute | solution.py:385
  33.1 24.9 %all_to_all.40.source = f32[128,4,128]{2,1,0:T(4,128)S(1)} all-to-all(f32[128,4,128]{2,1,0:T(4,128)S(1)} %get-tuple-element.32), channel_id=1, replica_groups=mesh['grp'=4,'sub'=32] {'grp','sub'}, dimensions={0} | all-to-all | bytes 524288 | tf_op jit(solution)/shard_map/all_to_all | solution.py:386
  57.9 0.0 collective-permute-done.5.beside
  57.9 1.1 collective-permute-start.6
  59.0 0.0 copy-done.1
  59.0 1.7 shard_map.125
  60.7 0.0 collective-permute-done.6.other
  60.7 13.6 %all_to_all.41.parts = f32[32,24,128]{2,1,0:T(8,128)S(1)} all-to-all(f32[32,24,128]{2,1,0:T(8,128)S(1)} %shard_map.125), channel_id=1, replica_groups=mesh['grp'=4,'sub'=32] {'sub'}, dimensions={0} | all-to-all | bytes 786432 | tf_op jit(solution)/shard_map/all_to_all | solution.py:397
  74.4 4.9 %shard_map.126 = (f32[520,128]{1,0:T(8,128)S(1)}, f32[128,4,128]{2,1,0:T(4,128)S(1)}) custom-call(s32[6]{0:T(128)S(1)} %get-tuple-element.30.ints, f32[5]{0:T(128)S(1)} %get-tuple-element.31.flts, f32[32,24,128]{2,1,0:T(8,128)S(1)} %all_to_all.41.parts, f32[520,128]{1,0:T(8,128)S(1)} %get-tuple-element.33.own, f32[520,128]{1,0:T(8,128)S(1)} %collective-permute-done.5.beside, ...), custom_call_target="tpu_custom_call" | custom-call | tf_op jit(solution)/shard_map/pallas_call | solution.py:404
  79.3 1.9 %collective-permute-start.7 = (f32[520,128]{1,0:T(8,128)S(1)}, f32[520,128]{1,0:T(8,128)S(1)}, u32[]{:S(2)}, u32[]{:S(2)}) collective-permute-start(f32[520,128]{1,0:T(8,128)S(1)} %get-tuple-element.43.own), channel_id=1, source_target_pairs={{1,2},{2,1},{3,4},{4,3},{5,6},{6,5},{7,8},{8,7},{9,10},{10,9},{11,... | collective-permute-start | bytes 798728 | tf_op jit(solution)/shard_map/ppermute | solution.py:385
  81.2 16.5 %all_to_all.42.source = f32[128,4,128]{2,1,0:T(4,128)S(1)} all-to-all(f32[128,4,128]{2,1,0:T(4,128)S(1)} %get-tuple-element.42), channel_id=1, replica_groups=mesh['grp'=4,'sub'=32] {'grp','sub'}, dimensions={0} | all-to-all | bytes 524288 | tf_op jit(solution)/shard_map/all_to_all | solution.py:386
  97.8 0.0 collective-permute-done.7.beside
  97.8 1.1 collective-permute-start.8
  98.8 1.7 shard_map.127
  100.5 0.0 collective-permute-done.8.other
  100.6 13.6 %all_to_all.43.parts = f32[32,24,128]{2,1,0:T(8,128)S(1)} all-to-all(f32[32,24,128]{2,1,0:T(8,128)S(1)} %shard_map.127), channel_id=1, replica_groups=mesh['grp'=4,'sub'=32] {'sub'}, dimensions={0} | all-to-all | bytes 786432 | tf_op jit(solution)/shard_map/all_to_all | solution.py:397
  114.2 4.9 %shard_map.128 = (f32[520,128]{1,0:T(8,128)S(1)}, f32[128,4,128]{2,1,0:T(4,128)S(1)}) custom-call(s32[6]{0:T(128)S(1)} %get-tuple-element.30.ints, f32[5]{0:T(128)S(1)} %get-tuple-element.31.flts, f32[32,24,128]{2,1,0:T(8,128)S(1)} %all_to_all.43.parts, f32[520,128]{1,0:T(8,128)S(1)} %get-tuple-element.43.own, f32[520,128]{1,0:T(8,128)S(1)} %collective-permute-done.7.beside, ...), custom_call_target="tpu_custom_call" | custom-call | tf_op jit(solution)/shard_map/pallas_call | solution.py:404
  119.1 1.9 %collective-permute-start.9 = (f32[520,128]{1,0:T(8,128)S(1)}, f32[520,128]{1,0:T(8,128)S(1)}, u32[]{:S(2)}, u32[]{:S(2)}) collective-permute-start(f32[520,128]{1,0:T(8,128)S(1)} %get-tuple-element.49.own), channel_id=1, source_target_pairs={{1,2},{2,1},{3,4},{4,3},{5,6},{6,5},{7,8},{8,7},{9,10},{10,9},{11,... | collective-permute-start | bytes 798728 | tf_op jit(solution)/shard_map/ppermute | solution.py:385
  121.0 16.5 %all_to_all.44.source = f32[128,4,128]{2,1,0:T(4,128)S(1)} all-to-all(f32[128,4,128]{2,1,0:T(4,128)S(1)} %get-tuple-element.48), channel_id=1, replica_groups=mesh['grp'=4,'sub'=32] {'grp','sub'}, dimensions={0} | all-to-all | bytes 524288 | tf_op jit(solution)/shard_map/all_to_all | solution.py:386
  137.6 0.0 collective-permute-done.9.beside
  137.6 1.1 collective-permute-start.10
  138.6 1.7 shard_map.129
  140.4 0.0 collective-permute-done.10.other
  140.4 13.6 %all_to_all.45.parts = f32[32,24,128]{2,1,0:T(8,128)S(1)} all-to-all(f32[32,24,128]{2,1,0:T(8,128)S(1)} %shard_map.129), channel_id=1, replica_groups=mesh['grp'=4,'sub'=32] {'sub'}, dimensions={0} | all-to-all | bytes 786432 | tf_op jit(solution)/shard_map/all_to_all | solution.py:397
  154.0 4.9 %shard_map.130 = (f32[520,128]{1,0:T(8,128)S(1)}, f32[128,8,128]{2,1,0:T(8,128)S(1)}) custom-call(s32[6]{0:T(128)S(1)} %get-tuple-element.30.ints, f32[5]{0:T(128)S(1)} %get-tuple-element.31.flts, f32[32,24,128]{2,1,0:T(8,128)S(1)} %all_to_all.45.parts, f32[520,128]{1,0:T(8,128)S(1)} %get-tuple-element.49.own, f32[520,128]{1,0:T(8,128)S(1)} %collective-permute-done.9.beside, ...), custom_call_target="tpu_custom_call" | custom-call | tf_op jit(solution)/shard_map/pallas_call | solution.py:404
  158.9 16.9 %all_to_all.46.source = f32[128,8,128]{2,1,0:T(8,128)S(1)} all-to-all(f32[128,8,128]{2,1,0:T(8,128)S(1)} %get-tuple-element.54), channel_id=1, replica_groups=mesh['grp'=4,'sub'=32] {'grp','sub'}, dimensions={0} | all-to-all | bytes 1048576 | tf_op jit(solution)/shard_map/all_to_all | solution.py:386
  175.8 2.3 %shard_map.131 = f32[32,8,128]{2,1,0:T(8,128)S(1)} custom-call(s32[6]{0:T(128)S(1)} %get-tuple-element.30.ints, f32[5]{0:T(128)S(1)} %get-tuple-element.31.flts, f32[128,8,128]{2,1,0:T(8,128)S(1)} %all_to_all.46.source, s32[24,128]{1,0:T(8,128)S(1)} %get-tuple-element.35.place, s32[24,128]{1,0:T(8,128)S(1)} %bitcast.9, ...), custom_call_target="tpu_custom_call" | custom-call | tf_op jit(solution)/shard_map/pallas_call | solution.py:390
  178.1 12.1 %all_to_all.47.parts = f32[32,8,128]{2,1,0:T(8,128)S(1)} all-to-all(f32[32,8,128]{2,1,0:T(8,128)S(1)} %shard_map.131), channel_id=1, replica_groups=mesh['grp'=4,'sub'=32] {'sub'}, dimensions={0} | all-to-all | bytes 262144 | tf_op jit(solution)/shard_map/all_to_all | solution.py:397
  190.2 1.5 shard_map.132
Async XLA Ops:
  0.6 20.7 %copy-start = (f32[1,24,128,128]{3,2,1,0:T(8,128)S(1)}, f32[1,24,128,128]{3,2,1,0:T(8,128)}, u32[]{:S(2)}) copy-start(f32[1,24,128,128]{3,2,1,0:T(8,128)} %param.21) | copy-start | bytes 4718596
  0.6 20.7 %copy-start.2 = (s32[1,24,128]{2,1,0:T(8,128)S(1)}, s32[1,24,128]{2,1,0:T(8,128)}, u32[]{:S(2)}) copy-start(s32[1,24,128]{2,1,0:T(8,128)} %param.19) | copy-start | bytes 36868
  2.1 0.7 copy-start.3
  2.8 16.1 %collective-permute-start.3 = (f32[1032,128]{1,0:T(8,128)S(1)}, f32[1032,128]{1,0:T(8,128)S(1)}, u32[]{:S(2)}, u32[]{:S(2)}) collective-permute-start(f32[1032,128]{1,0:T(8,128)S(1)} %shard_map.123.own), channel_id=1, source_target_pairs={{2,0},{3,1},{4,2},{5,3},{6,4},{7,5},{8,6},{9,7},{10,8},{11,9},{12,... | collective-permute-start | bytes 1585160 | tf_op jit(solution)/shard_map/ppermute | solution.py:355
  4.1 16.0 %collective-permute-start.1 = (f32[1032,128]{1,0:T(8,128)S(1)}, f32[1032,128]{1,0:T(8,128)S(1)}, u32[]{:S(2)}, u32[]{:S(2)}) collective-permute-start(f32[1032,128]{1,0:T(8,128)S(1)} %shard_map.123.own), channel_id=1, source_target_pairs={{0,2},{1,3},{2,4},{3,5},{4,6},{5,7},{6,8},{7,9},{8,10},{9,11},{10,... | collective-permute-start | bytes 1585160 | tf_op jit(solution)/shard_map/ppermute | solution.py:354
  9.2 15.5 %collective-permute-start = (f32[1032,128]{1,0:T(8,128)S(1)}, f32[1032,128]{1,0:T(8,128)S(1)}, u32[]{:S(2)}, u32[]{:S(2)}) collective-permute-start(f32[1032,128]{1,0:T(8,128)S(1)} %shard_map.123.own), channel_id=1, source_target_pairs={{0,1},{1,0},{2,3},{3,2},{4,5},{5,4},{6,7},{7,6},{8,9},{9,8},{10,11... | collective-permute-start | bytes 1585160 | tf_op jit(solution)/shard_map/ppermute | solution.py:356
  18.9 5.7 %collective-permute-start.4 = (f32[1032,128]{1,0:T(8,128)S(1)}, f32[1032,128]{1,0:T(8,128)S(1)}, u32[]{:S(2)}, u32[]{:S(2)}) collective-permute-start(f32[1032,128]{1,0:T(8,128)S(1)} %collective-permute-done.3.right), channel_id=1, source_target_pairs={{0,1},{1,0},{2,3},{3,2},{4,5},{5,4},{6,7},{7,6},{8,9},{9,8},{10,11... | collective-permute-start | bytes 1585160 | tf_op jit(solution)/shard_map/ppermute | solution.py:369
  20.2 4.5 %collective-permute-start.2 = (f32[1032,128]{1,0:T(8,128)S(1)}, f32[1032,128]{1,0:T(8,128)S(1)}, u32[]{:S(2)}, u32[]{:S(2)}) collective-permute-start(f32[1032,128]{1,0:T(8,128)S(1)} %collective-permute-done.1.left), channel_id=1, source_target_pairs={{0,1},{1,0},{2,3},{3,2},{4,5},{5,4},{6,7},{7,6},{8,9},{9,8},{10,11... | collective-permute-start | bytes 1585160 | tf_op jit(solution)/shard_map/ppermute | solution.py:368
  21.4 0.7 copy-start.4
  22.0 0.7 copy-start.5
  22.7 0.7 copy-start.6
  24.7 34.3 %copy-start.1 = (s32[1,24,128]{2,1,0:T(8,128)S(1)}, s32[1,24,128]{2,1,0:T(8,128)}, u32[]{:S(2)}) copy-start(s32[1,24,128]{2,1,0:T(8,128)} %param.20) | copy-start | bytes 36868
  29.1 28.9 %collective-permute-start.5 = (f32[520,128]{1,0:T(8,128)S(1)}, f32[520,128]{1,0:T(8,128)S(1)}, u32[]{:S(2)}, u32[]{:S(2)}) collective-permute-start(f32[520,128]{1,0:T(8,128)S(1)} %get-tuple-element.33.own), channel_id=1, source_target_pairs={{1,2},{2,1},{3,4},{4,3},{5,6},{6,5},{7,8},{8,7},{9,10},{10,9},{11,... | collective-permute-start | bytes 798728 | tf_op jit(solution)/shard_map/ppermute | solution.py:385
  57.9 2.8 %collective-permute-start.6 = (f32[520,128]{1,0:T(8,128)S(1)}, f32[520,128]{1,0:T(8,128)S(1)}, u32[]{:S(2)}, u32[]{:S(2)}) collective-permute-start(f32[520,128]{1,0:T(8,128)S(1)} %collective-permute-done.5.beside), channel_id=1, source_target_pairs={{0,1},{1,0},{2,3},{3,2},{4,5},{5,4},{6,7},{7,6},{8,9},{9,8},{10,11... | collective-permute-start | bytes 798728 | tf_op jit(solution)/shard_map/ppermute | solution.py:389
  79.3 18.5 %collective-permute-start.7 = (f32[520,128]{1,0:T(8,128)S(1)}, f32[520,128]{1,0:T(8,128)S(1)}, u32[]{:S(2)}, u32[]{:S(2)}) collective-permute-start(f32[520,128]{1,0:T(8,128)S(1)} %get-tuple-element.43.own), channel_id=1, source_target_pairs={{1,2},{2,1},{3,4},{4,3},{5,6},{6,5},{7,8},{8,7},{9,10},{10,9},{11,... | collective-permute-start | bytes 798728 | tf_op jit(solution)/shard_map/ppermute | solution.py:385
  97.8 2.8 %collective-permute-start.8 = (f32[520,128]{1,0:T(8,128)S(1)}, f32[520,128]{1,0:T(8,128)S(1)}, u32[]{:S(2)}, u32[]{:S(2)}) collective-permute-start(f32[520,128]{1,0:T(8,128)S(1)} %collective-permute-done.7.beside), channel_id=1, source_target_pairs={{0,1},{1,0},{2,3},{3,2},{4,5},{5,4},{6,7},{7,6},{8,9},{9,8},{10,11... | collective-permute-start | bytes 798728 | tf_op jit(solution)/shard_map/ppermute | solution.py:389
  119.1 18.5 %collective-permute-start.9 = (f32[520,128]{1,0:T(8,128)S(1)}, f32[520,128]{1,0:T(8,128)S(1)}, u32[]{:S(2)}, u32[]{:S(2)}) collective-permute-start(f32[520,128]{1,0:T(8,128)S(1)} %get-tuple-element.49.own), channel_id=1, source_target_pairs={{1,2},{2,1},{3,4},{4,3},{5,6},{6,5},{7,8},{8,7},{9,10},{10,9},{11,... | collective-permute-start | bytes 798728 | tf_op jit(solution)/shard_map/ppermute | solution.py:385
  137.6 2.8 %collective-permute-start.10 = (f32[520,128]{1,0:T(8,128)S(1)}, f32[520,128]{1,0:T(8,128)S(1)}, u32[]{:S(2)}, u32[]{:S(2)}) collective-permute-start(f32[520,128]{1,0:T(8,128)S(1)} %collective-permute-done.9.beside), channel_id=1, source_target_pairs={{0,1},{1,0},{2,3},{3,2},{4,5},{5,4},{6,7},{7,6},{8,9},{9,8},{10,11... | collective-permute-start | bytes 798728 | tf_op jit(solution)/shard_map/ppermute | solution.py:389

commit v3 on v2

--- a/solution.py
+++ b/solution.py
@@ -76,20 +76,25 @@
     ]
 
 
-def scatter_block(surf, inc):
-    left, right = [], []
-    for g in range(4):
-        lane = surf[g : g + 1] & 127
-        row = surf[g : g + 1] >> 7
-        left.append(jnp.where(iota((256, 128), 0) == row, 1.0, 0.0).astype(BF16))
-        hit = iota((128, 128), 0) == lane
-        value = inc[g : g + 1]
-        top = value.astype(BF16).astype(F32)
-        right.append(
-            jnp.concatenate(
-                [jnp.where(hit, top, 0.0).astype(BF16), jnp.where(hit, value - top, 0.0).astype(BF16)], axis=0
-            )
-        )
+def halves(x):
+    high = x.astype(BF16)
+    return high, (x - high.astype(F32)).astype(BF16)
+
+
+def rows_at(index, count):
+    return iota((count, 128), 0).astype(F32).astype(BF16) == index.astype(F32).astype(BF16)
+
+
+def one_hot(index, count):
+    return jnp.where(rows_at(index, count), jnp.bfloat16(1), jnp.bfloat16(0))
+
+
+def spread(index, value):
+    hit = rows_at(index, 128)
+    return jnp.concatenate([jnp.where(hit, part, jnp.bfloat16(0)) for part in halves(value)], axis=0)
+
+
+def product(left, right):
     out = lax.dot_general(
         jnp.concatenate(left, axis=1),
         jnp.concatenate(right, axis=1),
@@ -99,8 +104,15 @@
     return out[:, :128] + out[:, 128:]
 
 
-def finish(ints, flts, cur, coef, surf_ref, flux, keep, export, full):
-    core = ints[0]
+def scatter_block(surf, inc):
+    groups = [slice(g, g + 1) for g in range(4)]
+    return product(
+        [one_hot(surf[g] >> 7, 256) for g in groups], [spread(surf[g] & 127, inc[g]) for g in groups]
+    )
+
+
+def finish(flts, cur, coef, surf_ref, flux, keep, export, full):
+    core = lax.axis_index("sub") & 1
     for p in range(4):
         keep[pl.ds(p * ROWS, ROWS), :] = cur[HALO + p]
     for p in range(2):
@@ -129,7 +141,7 @@
     if full:
         block = jnp.concatenate([own, own_flux], axis=0)
     else:
-        block = flts[3] * own + flts[4] * own_flux
+        block = flts[3:4, :] * own + flts[4:5, :] * own_flux
     export[...] = jnp.broadcast_to(block[None], export.shape)
 
 
@@ -154,25 +166,18 @@
     lowest = jnp.min(apart.astype(F32)).astype(jnp.int32)
     start = (jnp.max(anchor.astype(F32)).astype(jnp.int32) + lowest) & (nodes - 1)
     first = start >> 9
-    place[...] = (at - first * 512) & (nodes - 1)
-    ints[0] = me & 1
-    ints[1] = live
-    ints[2] = kind
-    for i in range(3):
-        ints[3 + i] = partners[group] * subs + ((first + i) & (subs - 1))
+    place[...] = jnp.where(iota(at.shape, 0) < live, (at - first * 512) & (nodes - 1), -1)
+    ints[...] = jnp.full(ints.shape, partners[group] * subs + first, jnp.int32)
     is_gas = kind == 0
-    flts[0] = jnp.where(is_gas, 0.5, 0.25)
-    flts[1] = jnp.where(is_gas, -0.25, 0.25)
-    flts[2] = jnp.where(is_gas, 1.0, 0.0)
-    flts[3] = jnp.where(is_gas, 0.25, 0.5)
-    flts[4] = jnp.where(is_gas, 0.25, -0.25)
+    for row, (gas, solid) in enumerate(((0.5, 0.25), (-0.25, 0.25), (1.0, 0.0), (0.25, 0.5), (0.25, -0.25))):
+        flts[pl.ds(row, 1), :] = jnp.full((1, 128), jnp.where(is_gas, gas, solid), F32)
     for s in range(maps.shape[0]):
         turned[s] = maps[s].T
 
 
-def first_kernel(ints, flts, own, mate, left, left_mate, right, right_mate,
+def first_kernel(flts, own, mate, left, left_mate, right, right_mate,
                  keep, export, coef, surf, cur, nxt, flux):
-    core = ints[0]
+    core = lax.axis_index("sub") & 1
     other = 1 - core
     for base, mine, its in ((0, left, left_mate), (4, own, mate), (8, right, right_mate)):
         for p in range(2):
@@ -182,7 +187,7 @@
         tail_mate = its[pl.ds(1024, 8), :].astype(jnp.int32)
         surf[pl.ds(base // 2 + core, 1)] = tail[:4][None]
         surf[pl.ds(base // 2 + other, 1)] = tail_mate[:4][None]
-    gas = flts[2]
+    gas = flts[2:3, :]
 
     def store(p, ref, half):
         got = [ref[pl.ds(256 * (w + 1) + half * ROWS, ROWS), :] for w in range(3)]
@@ -213,12 +218,12 @@
         store(9, right, 0)
 
     run_steps(cur, nxt, coef)
-    finish(ints, flts, cur, coef, surf, flux, keep, export, False)
-
-
-def middle_kernel(ints, flts, parts, own, beside, other, surf, coef, keep, export,
+    finish(flts, cur, coef, surf, flux, keep, export, False)
+
+
+def middle_kernel(flts, parts, own, beside, other, surf, coef, keep, export,
                   cur, nxt, flux, *, full):
-    first = ints[0] == 0
+    first = (lax.axis_index("sub") & 1) == 0
     total = sum_parts(parts)
 
     def sides(start, size):
@@ -227,7 +232,7 @@
         return jnp.where(first, near, far), own[pl.ds(start, size), :], jnp.where(first, far, near)
 
     temps = sides(4 * ROWS, 8)
-    incs = [total[8 * side : 8 * side + 8] - flts[0] * temps[side] for side in range(3)]
+    incs = [total[8 * side : 8 * side + 8] - flts[0:1, :] * temps[side] for side in range(3)]
     for half in range(2):
         planes = sides(2 * half * ROWS, 2 * ROWS)
         for side in range(3):
@@ -236,7 +241,7 @@
             cur[2 * block] = out[:ROWS]
             cur[2 * block + 1] = out[ROWS:]
     run_steps(cur, nxt, coef)
-    finish(ints, flts, cur, coef, surf, flux, keep, export, full)
+    finish(flts, cur, coef, surf, flux, keep, export, full)
 
 
 def sum_parts(parts):
@@ -246,60 +251,47 @@
     return (lanes[0] + lanes[1]) + (lanes[2] + lanes[3])
 
 
-def last_kernel(ints, flts, parts, own, surf, field, interface):
-    core = ints[0]
+def last_kernel(flts, parts, own, surf, field, interface):
+    core = lax.axis_index("sub") & 1
     total = sum_parts(parts)
     interface[...] = total.reshape(2, 512)
     temps = own[pl.ds(4 * ROWS, 8), :]
     temps = jnp.where(core == 0, temps[:4], temps[4:])
-    inc = flts[0] * (total[:4] - temps) + flts[1] * total[4:]
+    inc = flts[0:1, :] * (total[:4] - temps) + flts[1:2, :] * total[4:]
     add = scatter_block(surf[pl.ds(2 + core, 1)][0], inc)
     start = pl.multiple_of(core * 2 * ROWS, 2 * ROWS)
     field[...] = (own[pl.ds(start, 2 * ROWS), :] + add).reshape(2, 128 * ROWS)
 
 
-def patch_kernel(ints, flts, source, place, targets, maps, out, *, final):
+def patch_kernel(ints, source, place, targets, maps, out, *, final):
     slots = place.shape[0]
+    subs = out.shape[0]
     parts = 2 if final else 1
     lanes = [place[pl.ds(8 * w, 8), :] & 127 for w in range(slots // 8)]
     rows = [place[pl.ds(8 * w, 8), :] >> 7 for w in range(slots // 8)]
     vals = [[jnp.zeros((8, 128), F32) for _ in rows] for _ in range(parts)]
+    at = jnp.max(ints[0:1, :].astype(F32)).astype(jnp.int32)
     for i in range(3):
-        tile = source[ints[3 + i]]
+        tile = source[(at & -subs) + ((at + i) & (subs - 1))]
         for q in range(parts):
             for j in range(4):
                 line = jnp.broadcast_to(tile[4 * q + j : 4 * q + j + 1], (8, 128))
                 for w in range(slots // 8):
                     got = jnp.take_along_axis(line, lanes[w], axis=1, mode="promise_in_bounds")
                     vals[q][w] = jnp.where(rows[w] == 4 * i + j, got, vals[q][w])
-    live = ints[1]
     columns = []
     for q in range(parts):
-        held = [jnp.where(iota((8, 128), 0) + 8 * w < live, vals[q][w], 0.0) for w in range(slots // 8)]
-        full = jnp.concatenate(held + [jnp.zeros((128 - slots, 128), F32)], axis=0)
+        full = jnp.concatenate(vals[q] + [jnp.zeros((128 - slots, 128), F32)], axis=0)
         columns.append(full.T)
     left, right = [], [[] for _ in range(parts)]
     for s in range(slots):
         aim = targets[s : s + 1, :]
-        left.append(jnp.where(iota((128, 128), 0) == aim >> 7, 1.0, 0.0).astype(BF16))
-        hit = iota((128, 128), 0) == (aim & 127)
+        left.append(one_hot(aim >> 7, 128))
         table = maps[s]
         for q in range(parts):
             value = jnp.sum(table * columns[q][:, s : s + 1], axis=0, keepdims=True)
-            top = value.astype(BF16).astype(F32)
-            right[q].append(
-                jnp.concatenate(
-                    [jnp.where(hit, top, 0.0).astype(BF16), jnp.where(hit, value - top, 0.0).astype(BF16)],
-                    axis=0,
-                )
-            )
-    lhs = jnp.concatenate(left, axis=1)
-    sums = []
-    for q in range(parts):
-        both = lax.dot_general(
-            lhs, jnp.concatenate(right[q], axis=1), (((1,), (1,)), ((), ())), preferred_element_type=F32
-        )
-        sums.append(both[:, :128] + both[:, 128:])
+            right[q].append(spread(aim & 127, value))
+    sums = [product(left, right[q]) for q in range(parts)]
     chips = out.shape[0] // 2
     for c in range(chips):
         if final:
@@ -358,8 +350,8 @@
         prepare_kernel,
         "sssvv",
         [
-            ((6,), jnp.int32, "s"),
-            ((5,), F32, "s"),
+            ((8, 128), jnp.int32, "v"),
+            ((8, 128), F32, "v"),
             ((slots, 128), jnp.int32, "v"),
             ((slots, 128, 128), F32, "v"),
         ],
@@ -375,10 +367,10 @@
     work = [(WIDE, ROWS, 128), (WIDE, ROWS, 128), (2 * ROWS, 128)]
     keep, send, coef, surf = call(
         first_kernel,
-        "ssvvvvvv",
+        "vvvvvvv",
         [keep_out, half_out, (coef_shape, F32, "v"), ((6, 4, 128), jnp.int32, "v")],
         work,
-    )(ints, flts, payload, mate, left, left_mate, right, right_mate)
+    )(flts, payload, mate, left, left_mate, right, right_mate)
     for iteration in range(COUPLE):
         final = iteration == COUPLE - 1
         if not final:
@@ -389,24 +381,24 @@
             other = lax.ppermute(beside, "sub", swap)
         (parts,) = call(
             functools.partial(patch_kernel, final=final),
-            "ssvvvv",
+            "vvvvv",
             [((subs, 8 if final else 24, 128), F32, "v")],
-        )(ints, flts, source, place, targets, turned)
+        )(ints, source, place, targets, turned)
         if not final:
             parts, other = lax.optimization_barrier((parts, other))
         parts = lax.all_to_all(parts, "sub", 0, 0, tiled=True)
         if final:
             field, interface = call(
-                last_kernel, "ssvvv", [((planes, cells), F32, "v"), ((2, block), F32, "v")]
-            )(ints, flts, parts, keep, surf)
+                last_kernel, "vvvv", [((planes, cells), F32, "v"), ((2, block), F32, "v")]
+            )(flts, parts, keep, surf)
         else:
             full = iteration == COUPLE - 2
             keep, send = call(
                 functools.partial(middle_kernel, full=full),
-                "ssvvvvvv",
+                "vvvvvvv",
                 [keep_out, full_out if full else half_out],
                 work,
-            )(ints, flts, parts, keep, beside, other, surf, coef)
+            )(flts, parts, keep, beside, other, surf, coef)
     return field[None], interface[None]
 
 

time: 192 us -> 188 us (0.979)
  Pallas kernels: 29.4 us -> 25.7 us
    pallas_call x10, Pallas kernels: 29.4 us -> 25.6 us  [the longest x3 13.4 us: local(): call(functools.partial(middle_kernel, full=full), 'vvvvvvv', [keep_out, f...]
where the time goes in v3:
time: 188 us
  blocking collectives  128 us (68%)
  Pallas kernels  25.7 us (14%)
  starting transfers between devices  20.8 us (11%)
  waiting for transfers between devices  8.73 us (5%)
  local copies, waits for them, and re-layouts  2.66 us (1%)
    all_to_all x4, blocking collectives, local(): source = lax.all_to_all(send, ('grp', 'sub'), 0, 0, tiled=True)  74.8 us
    all_to_all x4, blocking collectives, local(): parts = lax.all_to_all(parts, 'sub', 0, 0, tiled=True)  53 us
    pallas_call x3, Pallas kernels, local(): call(functools.partial(middle_kernel, full=full), 'vvvvvvv', [keep_out, f...  13.4 us
    ppermute x1, waiting for transfers between devices, local(): right = lax.ppermute(payload, 'sub', down)  8.71 us
    ppermute x3, starting transfers between devices, local(): beside = lax.ppermute(keep, 'sub', cross)  7.84 us
    pallas_call x4, Pallas kernels, local(): call(functools.partial(patch_kernel, final=final), 'vvvvv', [((subs, 8 if...  6.1 us
    ppermute x1, starting transfers between devices, local(): left = lax.ppermute(payload, 'sub', up)  5.02 us
    pallas_call x1, Pallas kernels, local(): call(first_kernel, 'vvvvvvv', [keep_out, half_out, (coef_shape, F32, 'v')...  4.03 us
  transfers between devices with their start and end apart: 11, of which 1 were waited for; matrix products, arithmetic and copies ran while one was open for 0% of the time, Pallas kernels for 3%

profile of v3, /device:TPU:1, one launch (start us, length us, event | category | flops | bytes accessed | tf_op | source)
XLA Modules:
  0.0 188.0 jit_solution(11664877719680626500)
XLA Ops:
  0.6 0.0 copy-start
  0.6 0.0 copy-start.2
  0.7 1.4 pad_maximum_fusion.fields
  2.1 0.0 copy-start.3
  2.1 0.7 copy-done.3
  2.8 0.1 shard_map.123.own
  2.8 1.3 collective-permute-start.3
  4.1 5.0 %collective-permute-start.1 = (f32[1032,128]{1,0:T(8,128)S(1)}, f32[1032,128]{1,0:T(8,128)S(1)}, u32[]{:S(2)}, u32[]{:S(2)}) collective-permute-start(f32[1032,128]{1,0:T(8,128)S(1)} %shard_map.123.own), channel_id=1, source_target_pairs={{0,2},{1,3},{2,4},{3,5},{4,6},{5,7},{6,8},{7,9},{8,10},{9,11},{10,... | collective-permute-start | bytes 1585160 | tf_op jit(solution)/shard_map/ppermute | solution.py:346
  9.2 1.0 collective-permute-start
  10.2 8.7 %collective-permute-done.3.right = f32[1032,128]{1,0:T(8,128)S(1)} collective-permute-done((f32[1032,128]{1,0:T(8,128)S(1)}, f32[1032,128]{1,0:T(8,128)S(1)}, u32[]{:S(2)}, u32[]{:S(2)}) %collective-permute-start.3) | collective-permute-done | bytes 528416 | tf_op jit(solution)/shard_map/ppermute | solution.py:347
  18.9 1.3 collective-permute-start.4
  20.2 0.0 collective-permute-done.1.left
  20.2 1.2 collective-permute-start.2
  21.3 0.0 copy-done
  21.4 0.0 copy-done.2
  21.4 0.0 copy-start.4
  21.4 0.7 copy-done.4
  22.0 0.0 copy-start.5
  22.0 0.7 copy-done.5
  22.7 0.0 copy-start.6
  22.7 0.7 copy-done.6
  23.3 1.1 shard_map.122
  24.4 0.0 collective-permute-done.mate
  24.4 0.0 collective-permute-done.4.right_mate
  24.4 0.0 collective-permute-done.2.left_mate
  24.4 0.0 copy-start.1
  24.5 4.0 %shard_map.124 = (f32[520,128]{1,0:T(8,128)S(1)}, f32[128,4,128]{2,1,0:T(4,128)S(1)}, f32[3,10,128,128]{3,2,1,0:T(8,128)S(1)}, s32[6,4,128]{2,1,0:T(4,128)S(1)}) custom-call(f32[8,128]{1,0:T(8,128)S(1)} %get-tuple-element.30.flts, f32[1032,128]{1,0:T(8,128)S(1)} %shard_map.123.own, f32[1032,128]{1,0:T(8,128)S(1)} %collective-permute-done.mate, ...), custom_call_target="tpu_custom_call" | custom-call | tf_op jit(solution)/shard_map/pallas_call | solution.py:368
  28.5 4.0 %collective-permute-start.5 = (f32[520,128]{1,0:T(8,128)S(1)}, f32[520,128]{1,0:T(8,128)S(1)}, u32[]{:S(2)}, u32[]{:S(2)}) collective-permute-start(f32[520,128]{1,0:T(8,128)S(1)} %get-tuple-element.33.own), channel_id=1, source_target_pairs={{1,2},{2,1},{3,4},{4,3},{5,6},{6,5},{7,8},{8,7},{9,10},{10,9},{11,... | collective-permute-start | bytes 798728 | tf_op jit(solution)/shard_map/ppermute | solution.py:377
  32.5 24.9 %all_to_all.40.source = f32[128,4,128]{2,1,0:T(4,128)S(1)} all-to-all(f32[128,4,128]{2,1,0:T(4,128)S(1)} %get-tuple-element.32), channel_id=1, replica_groups=mesh['grp'=4,'sub'=32] {'grp','sub'}, dimensions={0} | all-to-all | bytes 524288 | tf_op jit(solution)/shard_map/all_to_all | solution.py:378
  57.4 0.0 collective-permute-done.5.beside
  57.4 1.1 collective-permute-start.6
  58.4 0.0 copy-done.1
  58.4 1.4 shard_map.125
  59.8 0.0 collective-permute-done.6.other
  59.8 13.7 %all_to_all.41.parts = f32[32,24,128]{2,1,0:T(8,128)S(1)} all-to-all(f32[32,24,128]{2,1,0:T(8,128)S(1)} %shard_map.125), channel_id=1, replica_groups=mesh['grp'=4,'sub'=32] {'sub'}, dimensions={0} | all-to-all | bytes 786432 | tf_op jit(solution)/shard_map/all_to_all | solution.py:389
  73.5 4.5 %shard_map.126 = (f32[520,128]{1,0:T(8,128)S(1)}, f32[128,4,128]{2,1,0:T(4,128)S(1)}) custom-call(f32[8,128]{1,0:T(8,128)S(1)} %get-tuple-element.30.flts, f32[32,24,128]{2,1,0:T(8,128)S(1)} %all_to_all.41.parts, f32[520,128]{1,0:T(8,128)S(1)} %get-tuple-element.33.own, f32[520,128]{1,0:T(8,128)S(1)} %collective-permute-done.5.beside, ...), custom_call_target="tpu_custom_call" | custom-call | tf_op jit(solution)/shard_map/pallas_call | solution.py:396
  78.0 1.9 %collective-permute-start.7 = (f32[520,128]{1,0:T(8,128)S(1)}, f32[520,128]{1,0:T(8,128)S(1)}, u32[]{:S(2)}, u32[]{:S(2)}) collective-permute-start(f32[520,128]{1,0:T(8,128)S(1)} %get-tuple-element.43.own), channel_id=1, source_target_pairs={{1,2},{2,1},{3,4},{4,3},{5,6},{6,5},{7,8},{8,7},{9,10},{10,9},{11,... | collective-permute-start | bytes 798728 | tf_op jit(solution)/shard_map/ppermute | solution.py:377
  79.9 16.5 %all_to_all.42.source = f32[128,4,128]{2,1,0:T(4,128)S(1)} all-to-all(f32[128,4,128]{2,1,0:T(4,128)S(1)} %get-tuple-element.42), channel_id=1, replica_groups=mesh['grp'=4,'sub'=32] {'grp','sub'}, dimensions={0} | all-to-all | bytes 524288 | tf_op jit(solution)/shard_map/all_to_all | solution.py:378
  96.4 0.0 collective-permute-done.7.beside
  96.4 1.1 collective-permute-start.8
  97.5 1.4 shard_map.127
  98.9 0.0 collective-permute-done.8.other
  98.9 13.7 %all_to_all.43.parts = f32[32,24,128]{2,1,0:T(8,128)S(1)} all-to-all(f32[32,24,128]{2,1,0:T(8,128)S(1)} %shard_map.127), channel_id=1, replica_groups=mesh['grp'=4,'sub'=32] {'sub'}, dimensions={0} | all-to-all | bytes 786432 | tf_op jit(solution)/shard_map/all_to_all | solution.py:389
  112.6 4.5 %shard_map.128 = (f32[520,128]{1,0:T(8,128)S(1)}, f32[128,4,128]{2,1,0:T(4,128)S(1)}) custom-call(f32[8,128]{1,0:T(8,128)S(1)} %get-tuple-element.30.flts, f32[32,24,128]{2,1,0:T(8,128)S(1)} %all_to_all.43.parts, f32[520,128]{1,0:T(8,128)S(1)} %get-tuple-element.43.own, f32[520,128]{1,0:T(8,128)S(1)} %collective-permute-done.7.beside, ...), custom_call_target="tpu_custom_call" | custom-call | tf_op jit(solution)/shard_map/pallas_call | solution.py:396
  117.1 1.9 %collective-permute-start.9 = (f32[520,128]{1,0:T(8,128)S(1)}, f32[520,128]{1,0:T(8,128)S(1)}, u32[]{:S(2)}, u32[]{:S(2)}) collective-permute-start(f32[520,128]{1,0:T(8,128)S(1)} %get-tuple-element.49.own), channel_id=1, source_target_pairs={{1,2},{2,1},{3,4},{4,3},{5,6},{6,5},{7,8},{8,7},{9,10},{10,9},{11,... | collective-permute-start | bytes 798728 | tf_op jit(solution)/shard_map/ppermute | solution.py:377
  119.0 16.5 %all_to_all.44.source = f32[128,4,128]{2,1,0:T(4,128)S(1)} all-to-all(f32[128,4,128]{2,1,0:T(4,128)S(1)} %get-tuple-element.48), channel_id=1, replica_groups=mesh['grp'=4,'sub'=32] {'grp','sub'}, dimensions={0} | all-to-all | bytes 524288 | tf_op jit(solution)/shard_map/all_to_all | solution.py:378
  135.5 0.0 collective-permute-done.9.beside
  135.5 1.1 collective-permute-start.10
  136.6 1.4 shard_map.129
  138.0 0.0 collective-permute-done.10.other
  138.0 13.7 %all_to_all.45.parts = f32[32,24,128]{2,1,0:T(8,128)S(1)} all-to-all(f32[32,24,128]{2,1,0:T(8,128)S(1)} %shard_map.129), channel_id=1, replica_groups=mesh['grp'=4,'sub'=32] {'sub'}, dimensions={0} | all-to-all | bytes 786432 | tf_op jit(solution)/shard_map/all_to_all | solution.py:389
  151.6 4.5 %shard_map.130 = (f32[520,128]{1,0:T(8,128)S(1)}, f32[128,8,128]{2,1,0:T(8,128)S(1)}) custom-call(f32[8,128]{1,0:T(8,128)S(1)} %get-tuple-element.30.flts, f32[32,24,128]{2,1,0:T(8,128)S(1)} %all_to_all.45.parts, f32[520,128]{1,0:T(8,128)S(1)} %get-tuple-element.49.own, f32[520,128]{1,0:T(8,128)S(1)} %collective-permute-done.9.beside, ...), custom_call_target="tpu_custom_call" | custom-call | tf_op jit(solution)/shard_map/pallas_call | solution.py:396
  156.1 16.9 %all_to_all.46.source = f32[128,8,128]{2,1,0:T(8,128)S(1)} all-to-all(f32[128,8,128]{2,1,0:T(8,128)S(1)} %get-tuple-element.54), channel_id=1, replica_groups=mesh['grp'=4,'sub'=32] {'grp','sub'}, dimensions={0} | all-to-all | bytes 1048576 | tf_op jit(solution)/shard_map/all_to_all | solution.py:378
  173.0 2.0 %shard_map.131 = f32[32,8,128]{2,1,0:T(8,128)S(1)} custom-call(s32[8,128]{1,0:T(8,128)S(1)} %get-tuple-element.31.ints, f32[128,8,128]{2,1,0:T(8,128)S(1)} %all_to_all.46.source, s32[24,128]{1,0:T(8,128)S(1)} %get-tuple-element.35.place, s32[24,128]{1,0:T(8,128)S(1)} %bitcast.9, f32[24,128,128]{2,1,0:T(8,128)S(1)} %get-tuple-element.36.maps), custom_call_target="tpu_custom_call" | custom-call | tf_op jit(solution)/shard_map/pallas_call | solution.py:382
  175.0 12.1 %all_to_all.47.parts = f32[32,8,128]{2,1,0:T(8,128)S(1)} all-to-all(f32[32,8,128]{2,1,0:T(8,128)S(1)} %shard_map.131), channel_id=1, replica_groups=mesh['grp'=4,'sub'=32] {'sub'}, dimensions={0} | all-to-all | bytes 262144 | tf_op jit(solution)/shard_map/all_to_all | solution.py:389
  187.0 0.9 shard_map.132
Async XLA Ops:
  0.6 20.7 %copy-start = (f32[1,24,128,128]{3,2,1,0:T(8,128)S(1)}, f32[1,24,128,128]{3,2,1,0:T(8,128)}, u32[]{:S(2)}) copy-start(f32[1,24,128,128]{3,2,1,0:T(8,128)} %param.21) | copy-start | bytes 4718596
  0.6 20.7 %copy-start.2 = (s32[1,24,128]{2,1,0:T(8,128)S(1)}, s32[1,24,128]{2,1,0:T(8,128)}, u32[]{:S(2)}) copy-start(s32[1,24,128]{2,1,0:T(8,128)} %param.19) | copy-start | bytes 36868
  2.1 0.7 copy-start.3
  2.8 16.1 %collective-permute-start.3 = (f32[1032,128]{1,0:T(8,128)S(1)}, f32[1032,128]{1,0:T(8,128)S(1)}, u32[]{:S(2)}, u32[]{:S(2)}) collective-permute-start(f32[1032,128]{1,0:T(8,128)S(1)} %shard_map.123.own), channel_id=1, source_target_pairs={{2,0},{3,1},{4,2},{5,3},{6,4},{7,5},{8,6},{9,7},{10,8},{11,9},{12,... | collective-permute-start | bytes 1585160 | tf_op jit(solution)/shard_map/ppermute | solution.py:347
  4.1 16.0 %collective-permute-start.1 = (f32[1032,128]{1,0:T(8,128)S(1)}, f32[1032,128]{1,0:T(8,128)S(1)}, u32[]{:S(2)}, u32[]{:S(2)}) collective-permute-start(f32[1032,128]{1,0:T(8,128)S(1)} %shard_map.123.own), channel_id=1, source_target_pairs={{0,2},{1,3},{2,4},{3,5},{4,6},{5,7},{6,8},{7,9},{8,10},{9,11},{10,... | collective-permute-start | bytes 1585160 | tf_op jit(solution)/shard_map/ppermute | solution.py:346
  9.2 15.2 %collective-permute-start = (f32[1032,128]{1,0:T(8,128)S(1)}, f32[1032,128]{1,0:T(8,128)S(1)}, u32[]{:S(2)}, u32[]{:S(2)}) collective-permute-start(f32[1032,128]{1,0:T(8,128)S(1)} %shard_map.123.own), channel_id=1, source_target_pairs={{0,1},{1,0},{2,3},{3,2},{4,5},{5,4},{6,7},{7,6},{8,9},{9,8},{10,11... | collective-permute-start | bytes 1585160 | tf_op jit(solution)/shard_map/ppermute | solution.py:348
  18.9 5.5 %collective-permute-start.4 = (f32[1032,128]{1,0:T(8,128)S(1)}, f32[1032,128]{1,0:T(8,128)S(1)}, u32[]{:S(2)}, u32[]{:S(2)}) collective-permute-start(f32[1032,128]{1,0:T(8,128)S(1)} %collective-permute-done.3.right), channel_id=1, source_target_pairs={{0,1},{1,0},{2,3},{3,2},{4,5},{5,4},{6,7},{7,6},{8,9},{9,8},{10,11... | collective-permute-start | bytes 1585160 | tf_op jit(solution)/shard_map/ppermute | solution.py:361
  20.2 4.3 %collective-permute-start.2 = (f32[1032,128]{1,0:T(8,128)S(1)}, f32[1032,128]{1,0:T(8,128)S(1)}, u32[]{:S(2)}, u32[]{:S(2)}) collective-permute-start(f32[1032,128]{1,0:T(8,128)S(1)} %collective-permute-done.1.left), channel_id=1, source_target_pairs={{0,1},{1,0},{2,3},{3,2},{4,5},{5,4},{6,7},{7,6},{8,9},{9,8},{10,11... | collective-permute-start | bytes 1585160 | tf_op jit(solution)/shard_map/ppermute | solution.py:360
  21.4 0.7 copy-start.4
  22.0 0.7 copy-start.5
  22.7 0.7 copy-start.6
  24.4 34.0 %copy-start.1 = (s32[1,24,128]{2,1,0:T(8,128)S(1)}, s32[1,24,128]{2,1,0:T(8,128)}, u32[]{:S(2)}) copy-start(s32[1,24,128]{2,1,0:T(8,128)} %param.20) | copy-start | bytes 36868
  28.5 28.9 %collective-permute-start.5 = (f32[520,128]{1,0:T(8,128)S(1)}, f32[520,128]{1,0:T(8,128)S(1)}, u32[]{:S(2)}, u32[]{:S(2)}) collective-permute-start(f32[520,128]{1,0:T(8,128)S(1)} %get-tuple-element.33.own), channel_id=1, source_target_pairs={{1,2},{2,1},{3,4},{4,3},{5,6},{6,5},{7,8},{8,7},{9,10},{10,9},{11,... | collective-permute-start | bytes 798728 | tf_op jit(solution)/shard_map/ppermute | solution.py:377
  57.4 2.5 %collective-permute-start.6 = (f32[520,128]{1,0:T(8,128)S(1)}, f32[520,128]{1,0:T(8,128)S(1)}, u32[]{:S(2)}, u32[]{:S(2)}) collective-permute-start(f32[520,128]{1,0:T(8,128)S(1)} %collective-permute-done.5.beside), channel_id=1, source_target_pairs={{0,1},{1,0},{2,3},{3,2},{4,5},{5,4},{6,7},{7,6},{8,9},{9,8},{10,11... | collective-permute-start | bytes 798728 | tf_op jit(solution)/shard_map/ppermute | solution.py:381
  78.0 18.5 %collective-permute-start.7 = (f32[520,128]{1,0:T(8,128)S(1)}, f32[520,128]{1,0:T(8,128)S(1)}, u32[]{:S(2)}, u32[]{:S(2)}) collective-permute-start(f32[520,128]{1,0:T(8,128)S(1)} %get-tuple-element.43.own), channel_id=1, source_target_pairs={{1,2},{2,1},{3,4},{4,3},{5,6},{6,5},{7,8},{8,7},{9,10},{10,9},{11,... | collective-permute-start | bytes 798728 | tf_op jit(solution)/shard_map/ppermute | solution.py:377
  96.4 2.5 %collective-permute-start.8 = (f32[520,128]{1,0:T(8,128)S(1)}, f32[520,128]{1,0:T(8,128)S(1)}, u32[]{:S(2)}, u32[]{:S(2)}) collective-permute-start(f32[520,128]{1,0:T(8,128)S(1)} %collective-permute-done.7.beside), channel_id=1, source_target_pairs={{0,1},{1,0},{2,3},{3,2},{4,5},{5,4},{6,7},{7,6},{8,9},{9,8},{10,11... | collective-permute-start | bytes 798728 | tf_op jit(solution)/shard_map/ppermute | solution.py:381
  117.1 18.5 %collective-permute-start.9 = (f32[520,128]{1,0:T(8,128)S(1)}, f32[520,128]{1,0:T(8,128)S(1)}, u32[]{:S(2)}, u32[]{:S(2)}) collective-permute-start(f32[520,128]{1,0:T(8,128)S(1)} %get-tuple-element.49.own), channel_id=1, source_target_pairs={{1,2},{2,1},{3,4},{4,3},{5,6},{6,5},{7,8},{8,7},{9,10},{10,9},{11,... | collective-permute-start | bytes 798728 | tf_op jit(solution)/shard_map/ppermute | solution.py:377
  135.5 2.5 %collective-permute-start.10 = (f32[520,128]{1,0:T(8,128)S(1)}, f32[520,128]{1,0:T(8,128)S(1)}, u32[]{:S(2)}, u32[]{:S(2)}) collective-permute-start(f32[520,128]{1,0:T(8,128)S(1)} %collective-permute-done.9.beside), channel_id=1, source_target_pairs={{0,1},{1,0},{2,3},{3,2},{4,5},{5,4},{6,7},{7,6},{8,9},{9,8},{10,11... | collective-permute-start | bytes 798728 | tf_op jit(solution)/shard_map/ppermute | solution.py:381

commit v4 on v3

--- a/solution.py
+++ b/solution.py
@@ -24,12 +24,9 @@
 
 
 def in_plane(x):
-    return (
-        pltpu.roll(x, 1, 0)
-        + pltpu.roll(x, ROWS - 1, 0)
-        + pltpu.roll(x, 1, 1)
-        + pltpu.roll(x, 127, 1)
-    )
+    above = jnp.concatenate([pltpu.roll(x[ROWS - 8 :], 1, 0), x[: ROWS - 8]], axis=0)
+    below = jnp.concatenate([x[8:], pltpu.roll(x[:8], 7, 0)], axis=0)
+    return (above + below) + (pltpu.roll(x, 1, 1) + pltpu.roll(x, 127, 1))
 
 
 def run_steps(cur, nxt, coef):
@@ -47,7 +44,7 @@
             )
             return carry
 
-        lax.fori_loop(step + 1, WIDE - 1 - step, body, 0, unroll=2)
+        lax.fori_loop(step + 1, WIDE - 1 - step, body, 0, unroll=True)
 
 
 def pick_nodes(jobs):
@@ -147,8 +144,15 @@
 
 def pack_kernel(fields, surface, payload):
     for i in range(4):
-        payload[pl.ds(256 * i, 256), :] = fields[i].reshape(2 * ROWS, 128)
-    cells = surface[...].reshape(4, 128).astype(F32)
+        rows = fields[i].reshape(2 * ROWS, 128)
+        for p in range(2):
+            for lane in range(8):
+                start = p * ROWS + 16 * lane
+                payload[pl.ds(256 * i + p * ROWS + lane, 16, stride=8), :] = rows[start : start + 16]
+    cells = surface[...].reshape(4, 128)
+    row = (cells >> 7) & (ROWS - 1)
+    kept = ((row & 15) << 3) | (row >> 4)
+    cells = ((cells & ~(127 << 7)) | (kept << 7)).astype(F32)
     payload[pl.ds(1024, 8), :] = jnp.concatenate([cells, cells], axis=0)
 
 
@@ -251,7 +255,7 @@
     return (lanes[0] + lanes[1]) + (lanes[2] + lanes[3])
 
 
-def last_kernel(flts, parts, own, surf, field, interface):
+def last_kernel(flts, parts, own, surf, field, interface, work):
     core = lax.axis_index("sub") & 1
     total = sum_parts(parts)
     interface[...] = total.reshape(2, 512)
@@ -260,7 +264,9 @@
     inc = flts[0:1, :] * (total[:4] - temps) + flts[1:2, :] * total[4:]
     add = scatter_block(surf[pl.ds(2 + core, 1)][0], inc)
     start = pl.multiple_of(core * 2 * ROWS, 2 * ROWS)
-    field[...] = (own[pl.ds(start, 2 * ROWS), :] + add).reshape(2, 128 * ROWS)
+    work[...] = own[pl.ds(start, 2 * ROWS), :] + add
+    rows = [work[pl.ds(p * ROWS + lane, 16, stride=8), :] for p in range(2) for lane in range(8)]
+    field[...] = jnp.concatenate(rows, axis=0).reshape(2, 128 * ROWS)
 
 
 def patch_kernel(ints, source, place, targets, maps, out, *, final):
@@ -389,7 +395,10 @@
         parts = lax.all_to_all(parts, "sub", 0, 0, tiled=True)
         if final:
             field, interface = call(
-                last_kernel, "vvvv", [((planes, cells), F32, "v"), ((2, block), F32, "v")]
+                last_kernel,
+                "vvvv",
+                [((planes, cells), F32, "v"), ((2, block), F32, "v")],
+                [(2 * ROWS, 128)],
             )(flts, parts, keep, surf)
         else:
             full = iteration == COUPLE - 2

time: 188 us -> 184 us (0.979)
  Pallas kernels: 25.7 us -> 21.7 us
    pallas_call x3, Pallas kernels: 13.4 us -> 10.1 us  [local(): call(functools.partial(middle_kernel, full=full), 'vvvvvvv', [keep_out, f...]
where the time goes in v4:
time: 184 us
  blocking collectives  128 us (70%)
  Pallas kernels  21.7 us (12%)
  starting transfers between devices  20.8 us (11%)
  waiting for transfers between devices  8.73 us (5%)
  local copies, waits for them, and re-layouts  2.66 us (1%)
    all_to_all x4, blocking collectives, local(): source = lax.all_to_all(send, ('grp', 'sub'), 0, 0, tiled=True)  74.8 us
    all_to_all x4, blocking collectives, local(): parts = lax.all_to_all(parts, 'sub', 0, 0, tiled=True)  53 us
    pallas_call x3, Pallas kernels, local(): call(functools.partial(middle_kernel, full=full), 'vvvvvvv', [keep_out, f...  10.1 us
    ppermute x1, waiting for transfers between devices, local(): right = lax.ppermute(payload, 'sub', down)  8.71 us
    ppermute x3, starting transfers between devices, local(): beside = lax.ppermute(keep, 'sub', cross)  7.84 us
    pallas_call x4, Pallas kernels, local(): call(functools.partial(patch_kernel, final=final), 'vvvvv', [((subs, 8 if...  6.1 us
    ppermute x1, starting transfers between devices, local(): left = lax.ppermute(payload, 'sub', up)  5.02 us
  transfers between devices with their start and end apart: 11, of which 1 were waited for; matrix products, arithmetic and copies ran while one was open for 0% of the time, Pallas kernels for 3%

profile of v4, /device:TPU:1, one launch (start us, length us, event | category | flops | bytes accessed | tf_op | source)
XLA Modules:
  0.0 184.0 jit_solution(6471464749720200921)
XLA Ops:
  0.6 0.0 copy-start
  0.6 0.0 copy-start.2
  0.7 1.4 pad_maximum_fusion.fields
  2.1 0.0 copy-start.3
  2.1 0.7 copy-done.3
  2.8 0.1 shard_map.123.own
  2.9 1.3 collective-permute-start.3
  4.2 5.0 %collective-permute-start.1 = (f32[1032,128]{1,0:T(8,128)S(1)}, f32[1032,128]{1,0:T(8,128)S(1)}, u32[]{:S(2)}, u32[]{:S(2)}) collective-permute-start(f32[1032,128]{1,0:T(8,128)S(1)} %shard_map.123.own), channel_id=1, source_target_pairs={{0,2},{1,3},{2,4},{3,5},{4,6},{5,7},{6,8},{7,9},{8,10},{9,11},{10,... | collective-permute-start | bytes 1585160 | tf_op jit(solution)/shard_map/ppermute | solution.py:352
  9.2 1.0 collective-permute-start
  10.3 8.7 %collective-permute-done.3.right = f32[1032,128]{1,0:T(8,128)S(1)} collective-permute-done((f32[1032,128]{1,0:T(8,128)S(1)}, f32[1032,128]{1,0:T(8,128)S(1)}, u32[]{:S(2)}, u32[]{:S(2)}) %collective-permute-start.3) | collective-permute-done | bytes 528416 | tf_op jit(solution)/shard_map/ppermute | solution.py:353
  19.0 1.3 collective-permute-start.4
  20.2 0.0 collective-permute-done.1.left
  20.2 1.2 collective-permute-start.2
  21.4 0.0 copy-done
  21.4 0.0 copy-done.2
  21.4 0.0 copy-start.4
  21.4 0.7 copy-done.4
  22.1 0.0 copy-start.5
  22.1 0.7 copy-done.5
  22.7 0.0 copy-start.6
  22.7 0.7 copy-done.6
  23.4 1.1 shard_map.122
  24.5 0.0 collective-permute-done.mate
  24.5 0.0 collective-permute-done.4.right_mate
  24.5 0.0 collective-permute-done.2.left_mate
  24.5 0.0 copy-start.1
  24.5 3.3 %shard_map.124 = (f32[520,128]{1,0:T(8,128)S(1)}, f32[128,4,128]{2,1,0:T(4,128)S(1)}, f32[3,10,128,128]{3,2,1,0:T(8,128)S(1)}, s32[6,4,128]{2,1,0:T(4,128)S(1)}) custom-call(f32[8,128]{1,0:T(8,128)S(1)} %get-tuple-element.30.flts, f32[1032,128]{1,0:T(8,128)S(1)} %shard_map.123.own, f32[1032,128]{1,0:T(8,128)S(1)} %collective-permute-done.mate, ...), custom_call_target="tpu_custom_call" | custom-call | tf_op jit(solution)/shard_map/pallas_call | solution.py:374
  27.9 4.0 %collective-permute-start.5 = (f32[520,128]{1,0:T(8,128)S(1)}, f32[520,128]{1,0:T(8,128)S(1)}, u32[]{:S(2)}, u32[]{:S(2)}) collective-permute-start(f32[520,128]{1,0:T(8,128)S(1)} %get-tuple-element.33.own), channel_id=1, source_target_pairs={{1,2},{2,1},{3,4},{4,3},{5,6},{6,5},{7,8},{8,7},{9,10},{10,9},{11,... | collective-permute-start | bytes 798728 | tf_op jit(solution)/shard_map/ppermute | solution.py:383
  31.9 24.9 %all_to_all.40.source = f32[128,4,128]{2,1,0:T(4,128)S(1)} all-to-all(f32[128,4,128]{2,1,0:T(4,128)S(1)} %get-tuple-element.32), channel_id=1, replica_groups=mesh['grp'=4,'sub'=32] {'grp','sub'}, dimensions={0} | all-to-all | bytes 524288 | tf_op jit(solution)/shard_map/all_to_all | solution.py:384
  56.7 0.0 collective-permute-done.5.beside
  56.7 1.1 collective-permute-start.6
  57.8 0.0 copy-done.1
  57.8 1.4 shard_map.125
  59.2 0.0 collective-permute-done.6.other
  59.2 13.7 %all_to_all.41.parts = f32[32,24,128]{2,1,0:T(8,128)S(1)} all-to-all(f32[32,24,128]{2,1,0:T(8,128)S(1)} %shard_map.125), channel_id=1, replica_groups=mesh['grp'=4,'sub'=32] {'sub'}, dimensions={0} | all-to-all | bytes 786432 | tf_op jit(solution)/shard_map/all_to_all | solution.py:395
  72.8 3.4 %shard_map.126 = (f32[520,128]{1,0:T(8,128)S(1)}, f32[128,4,128]{2,1,0:T(4,128)S(1)}) custom-call(f32[8,128]{1,0:T(8,128)S(1)} %get-tuple-element.30.flts, f32[32,24,128]{2,1,0:T(8,128)S(1)} %all_to_all.41.parts, f32[520,128]{1,0:T(8,128)S(1)} %get-tuple-element.33.own, f32[520,128]{1,0:T(8,128)S(1)} %collective-permute-done.5.beside, ...), custom_call_target="tpu_custom_call" | custom-call | tf_op jit(solution)/shard_map/pallas_call | solution.py:405
  76.2 1.9 %collective-permute-start.7 = (f32[520,128]{1,0:T(8,128)S(1)}, f32[520,128]{1,0:T(8,128)S(1)}, u32[]{:S(2)}, u32[]{:S(2)}) collective-permute-start(f32[520,128]{1,0:T(8,128)S(1)} %get-tuple-element.43.own), channel_id=1, source_target_pairs={{1,2},{2,1},{3,4},{4,3},{5,6},{6,5},{7,8},{8,7},{9,10},{10,9},{11,... | collective-permute-start | bytes 798728 | tf_op jit(solution)/shard_map/ppermute | solution.py:383
  78.1 16.5 %all_to_all.42.source = f32[128,4,128]{2,1,0:T(4,128)S(1)} all-to-all(f32[128,4,128]{2,1,0:T(4,128)S(1)} %get-tuple-element.42), channel_id=1, replica_groups=mesh['grp'=4,'sub'=32] {'grp','sub'}, dimensions={0} | all-to-all | bytes 524288 | tf_op jit(solution)/shard_map/all_to_all | solution.py:384
  94.7 0.0 collective-permute-done.7.beside
  94.7 1.1 collective-permute-start.8
  95.7 1.4 shard_map.127
  97.1 0.0 collective-permute-done.8.other
  97.1 13.7 %all_to_all.43.parts = f32[32,24,128]{2,1,0:T(8,128)S(1)} all-to-all(f32[32,24,128]{2,1,0:T(8,128)S(1)} %shard_map.127), channel_id=1, replica_groups=mesh['grp'=4,'sub'=32] {'sub'}, dimensions={0} | all-to-all | bytes 786432 | tf_op jit(solution)/shard_map/all_to_all | solution.py:395
  110.8 3.3 %shard_map.128 = (f32[520,128]{1,0:T(8,128)S(1)}, f32[128,4,128]{2,1,0:T(4,128)S(1)}) custom-call(f32[8,128]{1,0:T(8,128)S(1)} %get-tuple-element.30.flts, f32[32,24,128]{2,1,0:T(8,128)S(1)} %all_to_all.43.parts, f32[520,128]{1,0:T(8,128)S(1)} %get-tuple-element.43.own, f32[520,128]{1,0:T(8,128)S(1)} %collective-permute-done.7.beside, ...), custom_call_target="tpu_custom_call" | custom-call | tf_op jit(solution)/shard_map/pallas_call | solution.py:405
  114.1 1.9 %collective-permute-start.9 = (f32[520,128]{1,0:T(8,128)S(1)}, f32[520,128]{1,0:T(8,128)S(1)}, u32[]{:S(2)}, u32[]{:S(2)}) collective-permute-start(f32[520,128]{1,0:T(8,128)S(1)} %get-tuple-element.49.own), channel_id=1, source_target_pairs={{1,2},{2,1},{3,4},{4,3},{5,6},{6,5},{7,8},{8,7},{9,10},{10,9},{11,... | collective-permute-start | bytes 798728 | tf_op jit(solution)/shard_map/ppermute | solution.py:383
  116.1 16.5 %all_to_all.44.source = f32[128,4,128]{2,1,0:T(4,128)S(1)} all-to-all(f32[128,4,128]{2,1,0:T(4,128)S(1)} %get-tuple-element.48), channel_id=1, replica_groups=mesh['grp'=4,'sub'=32] {'grp','sub'}, dimensions={0} | all-to-all | bytes 524288 | tf_op jit(solution)/shard_map/all_to_all | solution.py:384
  132.6 0.0 collective-permute-done.9.beside
  132.6 1.1 collective-permute-start.10
  133.7 1.4 shard_map.129
  135.1 0.0 collective-permute-done.10.other
  135.1 13.7 %all_to_all.45.parts = f32[32,24,128]{2,1,0:T(8,128)S(1)} all-to-all(f32[32,24,128]{2,1,0:T(8,128)S(1)} %shard_map.129), channel_id=1, replica_groups=mesh['grp'=4,'sub'=32] {'sub'}, dimensions={0} | all-to-all | bytes 786432 | tf_op jit(solution)/shard_map/all_to_all | solution.py:395
  148.7 3.4 %shard_map.130 = (f32[520,128]{1,0:T(8,128)S(1)}, f32[128,8,128]{2,1,0:T(8,128)S(1)}) custom-call(f32[8,128]{1,0:T(8,128)S(1)} %get-tuple-element.30.flts, f32[32,24,128]{2,1,0:T(8,128)S(1)} %all_to_all.45.parts, f32[520,128]{1,0:T(8,128)S(1)} %get-tuple-element.49.own, f32[520,128]{1,0:T(8,128)S(1)} %collective-permute-done.9.beside, ...), custom_call_target="tpu_custom_call" | custom-call | tf_op jit(solution)/shard_map/pallas_call | solution.py:405
  152.1 16.9 %all_to_all.46.source = f32[128,8,128]{2,1,0:T(8,128)S(1)} all-to-all(f32[128,8,128]{2,1,0:T(8,128)S(1)} %get-tuple-element.54), channel_id=1, replica_groups=mesh['grp'=4,'sub'=32] {'grp','sub'}, dimensions={0} | all-to-all | bytes 1048576 | tf_op jit(solution)/shard_map/all_to_all | solution.py:384
  169.0 2.0 %shard_map.131 = f32[32,8,128]{2,1,0:T(8,128)S(1)} custom-call(s32[8,128]{1,0:T(8,128)S(1)} %get-tuple-element.31.ints, f32[128,8,128]{2,1,0:T(8,128)S(1)} %all_to_all.46.source, s32[24,128]{1,0:T(8,128)S(1)} %get-tuple-element.35.place, s32[24,128]{1,0:T(8,128)S(1)} %bitcast.9, f32[24,128,128]{2,1,0:T(8,128)S(1)} %get-tuple-element.36.maps), custom_call_target="tpu_custom_call" | custom-call | tf_op jit(solution)/shard_map/pallas_call | solution.py:388
  170.9 12.1 %all_to_all.47.parts = f32[32,8,128]{2,1,0:T(8,128)S(1)} all-to-all(f32[32,8,128]{2,1,0:T(8,128)S(1)} %shard_map.131), channel_id=1, replica_groups=mesh['grp'=4,'sub'=32] {'sub'}, dimensions={0} | all-to-all | bytes 262144 | tf_op jit(solution)/shard_map/all_to_all | solution.py:395
  183.0 1.0 shard_map.132
Async XLA Ops:
  0.6 20.8 %copy-start = (f32[1,24,128,128]{3,2,1,0:T(8,128)S(1)}, f32[1,24,128,128]{3,2,1,0:T(8,128)}, u32[]{:S(2)}) copy-start(f32[1,24,128,128]{3,2,1,0:T(8,128)} %param.21) | copy-start | bytes 4718596
  0.6 20.8 %copy-start.2 = (s32[1,24,128]{2,1,0:T(8,128)S(1)}, s32[1,24,128]{2,1,0:T(8,128)}, u32[]{:S(2)}) copy-start(s32[1,24,128]{2,1,0:T(8,128)} %param.19) | copy-start | bytes 36868
  2.1 0.7 copy-start.3
  2.9 16.1 %collective-permute-start.3 = (f32[1032,128]{1,0:T(8,128)S(1)}, f32[1032,128]{1,0:T(8,128)S(1)}, u32[]{:S(2)}, u32[]{:S(2)}) collective-permute-start(f32[1032,128]{1,0:T(8,128)S(1)} %shard_map.123.own), channel_id=1, source_target_pairs={{2,0},{3,1},{4,2},{5,3},{6,4},{7,5},{8,6},{9,7},{10,8},{11,9},{12,... | collective-permute-start | bytes 1585160 | tf_op jit(solution)/shard_map/ppermute | solution.py:353
  4.2 16.0 %collective-permute-start.1 = (f32[1032,128]{1,0:T(8,128)S(1)}, f32[1032,128]{1,0:T(8,128)S(1)}, u32[]{:S(2)}, u32[]{:S(2)}) collective-permute-start(f32[1032,128]{1,0:T(8,128)S(1)} %shard_map.123.own), channel_id=1, source_target_pairs={{0,2},{1,3},{2,4},{3,5},{4,6},{5,7},{6,8},{7,9},{8,10},{9,11},{10,... | collective-permute-start | bytes 1585160 | tf_op jit(solution)/shard_map/ppermute | solution.py:352
  9.2 15.2 %collective-permute-start = (f32[1032,128]{1,0:T(8,128)S(1)}, f32[1032,128]{1,0:T(8,128)S(1)}, u32[]{:S(2)}, u32[]{:S(2)}) collective-permute-start(f32[1032,128]{1,0:T(8,128)S(1)} %shard_map.123.own), channel_id=1, source_target_pairs={{0,1},{1,0},{2,3},{3,2},{4,5},{5,4},{6,7},{7,6},{8,9},{9,8},{10,11... | collective-permute-start | bytes 1585160 | tf_op jit(solution)/shard_map/ppermute | solution.py:354
  19.0 5.5 %collective-permute-start.4 = (f32[1032,128]{1,0:T(8,128)S(1)}, f32[1032,128]{1,0:T(8,128)S(1)}, u32[]{:S(2)}, u32[]{:S(2)}) collective-permute-start(f32[1032,128]{1,0:T(8,128)S(1)} %collective-permute-done.3.right), channel_id=1, source_target_pairs={{0,1},{1,0},{2,3},{3,2},{4,5},{5,4},{6,7},{7,6},{8,9},{9,8},{10,11... | collective-permute-start | bytes 1585160 | tf_op jit(solution)/shard_map/ppermute | solution.py:367
  20.2 4.3 %collective-permute-start.2 = (f32[1032,128]{1,0:T(8,128)S(1)}, f32[1032,128]{1,0:T(8,128)S(1)}, u32[]{:S(2)}, u32[]{:S(2)}) collective-permute-start(f32[1032,128]{1,0:T(8,128)S(1)} %collective-permute-done.1.left), channel_id=1, source_target_pairs={{0,1},{1,0},{2,3},{3,2},{4,5},{5,4},{6,7},{7,6},{8,9},{9,8},{10,11... | collective-permute-start | bytes 1585160 | tf_op jit(solution)/shard_map/ppermute | solution.py:366
  21.4 0.7 copy-start.4
  22.1 0.7 copy-start.5
  22.7 0.7 copy-start.6
  24.5 33.3 %copy-start.1 = (s32[1,24,128]{2,1,0:T(8,128)S(1)}, s32[1,24,128]{2,1,0:T(8,128)}, u32[]{:S(2)}) copy-start(s32[1,24,128]{2,1,0:T(8,128)} %param.20) | copy-start | bytes 36868
  27.9 28.9 %collective-permute-start.5 = (f32[520,128]{1,0:T(8,128)S(1)}, f32[520,128]{1,0:T(8,128)S(1)}, u32[]{:S(2)}, u32[]{:S(2)}) collective-permute-start(f32[520,128]{1,0:T(8,128)S(1)} %get-tuple-element.33.own), channel_id=1, source_target_pairs={{1,2},{2,1},{3,4},{4,3},{5,6},{6,5},{7,8},{8,7},{9,10},{10,9},{11,... | collective-permute-start | bytes 798728 | tf_op jit(solution)/shard_map/ppermute | solution.py:383
  56.7 2.5 %collective-permute-start.6 = (f32[520,128]{1,0:T(8,128)S(1)}, f32[520,128]{1,0:T(8,128)S(1)}, u32[]{:S(2)}, u32[]{:S(2)}) collective-permute-start(f32[520,128]{1,0:T(8,128)S(1)} %collective-permute-done.5.beside), channel_id=1, source_target_pairs={{0,1},{1,0},{2,3},{3,2},{4,5},{5,4},{6,7},{7,6},{8,9},{9,8},{10,11... | collective-permute-start | bytes 798728 | tf_op jit(solution)/shard_map/ppermute | solution.py:387
  76.2 18.5 %collective-permute-start.7 = (f32[520,128]{1,0:T(8,128)S(1)}, f32[520,128]{1,0:T(8,128)S(1)}, u32[]{:S(2)}, u32[]{:S(2)}) collective-permute-start(f32[520,128]{1,0:T(8,128)S(1)} %get-tuple-element.43.own), channel_id=1, source_target_pairs={{1,2},{2,1},{3,4},{4,3},{5,6},{6,5},{7,8},{8,7},{9,10},{10,9},{11,... | collective-permute-start | bytes 798728 | tf_op jit(solution)/shard_map/ppermute | solution.py:383
  94.7 2.5 %collective-permute-start.8 = (f32[520,128]{1,0:T(8,128)S(1)}, f32[520,128]{1,0:T(8,128)S(1)}, u32[]{:S(2)}, u32[]{:S(2)}) collective-permute-start(f32[520,128]{1,0:T(8,128)S(1)} %collective-permute-done.7.beside), channel_id=1, source_target_pairs={{0,1},{1,0},{2,3},{3,2},{4,5},{5,4},{6,7},{7,6},{8,9},{9,8},{10,11... | collective-permute-start | bytes 798728 | tf_op jit(solution)/shard_map/ppermute | solution.py:387
  114.1 18.5 %collective-permute-start.9 = (f32[520,128]{1,0:T(8,128)S(1)}, f32[520,128]{1,0:T(8,128)S(1)}, u32[]{:S(2)}, u32[]{:S(2)}) collective-permute-start(f32[520,128]{1,0:T(8,128)S(1)} %get-tuple-element.49.own), channel_id=1, source_target_pairs={{1,2},{2,1},{3,4},{4,3},{5,6},{6,5},{7,8},{8,7},{9,10},{10,9},{11,... | collective-permute-start | bytes 798728 | tf_op jit(solution)/shard_map/ppermute | solution.py:383
  132.6 2.5 %collective-permute-start.10 = (f32[520,128]{1,0:T(8,128)S(1)}, f32[520,128]{1,0:T(8,128)S(1)}, u32[]{:S(2)}, u32[]{:S(2)}) collective-permute-start(f32[520,128]{1,0:T(8,128)S(1)} %collective-permute-done.9.beside), channel_id=1, source_target_pairs={{0,1},{1,0},{2,3},{3,2},{4,5},{5,4},{6,7},{7,6},{8,9},{9,8},{10,11... | collective-permute-start | bytes 798728 | tf_op jit(solution)/shard_map/ppermute | solution.py:387

commit v5 on v4

--- a/solution.py
+++ b/solution.py
@@ -179,48 +179,47 @@
         turned[s] = maps[s].T
 
 
-def first_kernel(flts, own, mate, left, left_mate, right, right_mate,
+def far_kernel(mate, far):
+    skip = jnp.where((lax.axis_index("sub") & 1) == 0, 0, ROWS)
+    far[pl.ds(0, 2 * ROWS), :] = mate[pl.ds(0, 2 * ROWS), :]
+    for which in range(3):
+        start = pl.multiple_of(256 * (which + 1) + skip, ROWS)
+        far[pl.ds((2 + which) * ROWS, ROWS), :] = mate[pl.ds(start, ROWS), :]
+    far[pl.ds(5 * ROWS, 8), :] = mate[pl.ds(1024, 8), :]
+
+
+def first_kernel(flts, own, mate, near, near_other, far, far_other,
                  keep, export, coef, surf, cur, nxt, flux):
-    core = lax.axis_index("sub") & 1
-    other = 1 - core
-    for base, mine, its in ((0, left, left_mate), (4, own, mate), (8, right, right_mate)):
-        for p in range(2):
-            cur[base + 2 * core + p] = mine[pl.ds(p * ROWS, ROWS), :]
-            cur[base + 2 * other + p] = its[pl.ds(p * ROWS, ROWS), :]
-        tail = mine[pl.ds(1024, 8), :].astype(jnp.int32)
-        tail_mate = its[pl.ds(1024, 8), :].astype(jnp.int32)
-        surf[pl.ds(base // 2 + core, 1)] = tail[:4][None]
-        surf[pl.ds(base // 2 + other, 1)] = tail_mate[:4][None]
+    first = (lax.axis_index("sub") & 1) == 0
     gas = flts[2:3, :]
 
-    def store(p, ref, half):
-        got = [ref[pl.ds(256 * (w + 1) + half * ROWS, ROWS), :] for w in range(3)]
-        coef[0, p] = got[0]
-        coef[1, p] = got[0] + gas * got[1]
-        coef[2, p] = (0.5 * gas) * got[2]
+    def pick(one, other, start, size):
+        x = one[pl.ds(start, size), :]
+        y = other[pl.ds(start, size), :]
+        return jnp.where(first, x, y), jnp.where(first, y, x)
+
+    pairs = ((far, far_other, 5 * ROWS, (0, 5)), (near, near_other, 1024, (1, 4)), (own, mate, 1024, (2, 3)))
+    for one, other, tail, blocks in pairs:
+        both = pick(one, other, 0, 2 * ROWS)
+        cells = pick(one, other, tail, 8)
+        for side, block in enumerate(blocks):
+            cur[2 * block] = both[side][:ROWS]
+            cur[2 * block + 1] = both[side][ROWS:]
+            surf[block] = cells[side][:4].astype(jnp.int32)
+
+    def store(one, other, starts, planes):
+        got = [pick(one, other, start, ROWS) for start in starts]
+        for side, plane in enumerate(planes):
+            conduct, velocity, heat = (g[side] for g in got)
+            coef[0, plane - 1] = conduct
+            coef[1, plane - 1] = conduct + gas * velocity
+            coef[2, plane - 1] = (0.5 * gas) * heat
 
     for half in range(2):
-        store(3 + 2 * core + half, own, half)
-        store(3 + 2 * other + half, mate, half)
-
-    @pl.when(core == 0)
-    def _():
-        store(0, left, 1)
-        store(1, left_mate, 0)
-        store(2, left_mate, 1)
-        store(7, right, 0)
-        store(8, right, 1)
-        store(9, right_mate, 0)
-
-    @pl.when(core == 1)
-    def _():
-        store(0, left_mate, 1)
-        store(1, left, 0)
-        store(2, left, 1)
-        store(7, right_mate, 0)
-        store(8, right_mate, 1)
-        store(9, right, 0)
-
+        starts = [256 * (w + 1) + half * ROWS for w in range(3)]
+        store(own, mate, starts, (4 + half, 6 + half))
+        store(near, near_other, starts, (2 + half, 8 + half))
+    store(far, far_other, [(2 + w) * ROWS for w in range(3)], (1, 10))
     run_steps(cur, nxt, coef)
     finish(flts, cur, coef, surf, flux, keep, export, False)
 
@@ -345,13 +344,12 @@
 
     fields = jnp.concatenate([initial_field, conduct, velocity, heat_release], axis=0)
     (payload,) = call(pack_kernel, "vv", [((1032, 128), F32, "v")])(fields, surface_cell)
-    up = [(i, i + 2) for i in range(subs - 2)]
-    down = [(i + 2, i) for i in range(subs - 2)]
     swap = [(i, i ^ 1) for i in range(subs)]
     cross = [(i, i + 1 if i % 2 else i - 1) for i in range(1, subs - 1)]
-    left = lax.ppermute(payload, "sub", up)
-    right = lax.ppermute(payload, "sub", down)
+    near = lax.ppermute(payload, "sub", cross)
     mate = lax.ppermute(payload, "sub", swap)
+    (far,) = call(far_kernel, "v", [((5 * ROWS + 8, 128), F32, "v")])(mate)
+    far = lax.ppermute(far, "sub", cross)
     ints, flts, place, turned = call(
         prepare_kernel,
         "sssvv",
@@ -363,8 +361,8 @@
         ],
     )(group_kind, partner, patch_count, patch_centres[0], patch_maps[0])
     targets = patch_targets[0]
-    left_mate = lax.ppermute(left, "sub", swap)
-    right_mate = lax.ppermute(right, "sub", swap)
+    near_other = lax.ppermute(near, "sub", swap)
+    far_other = lax.ppermute(far, "sub", swap)
 
     keep_out = ((4 * ROWS + 8, 128), F32, "v")
     half_out = ((groups * subs, 4, 128), F32, "v")
@@ -376,7 +374,7 @@
         "vvvvvvv",
         [keep_out, half_out, (coef_shape, F32, "v"), ((6, 4, 128), jnp.int32, "v")],
         work,
-    )(flts, payload, mate, left, left_mate, right, right_mate)
+    )(flts, payload, mate, near, near_other, far, far_other)
     for iteration in range(COUPLE):
         final = iteration == COUPLE - 1
         if not final:

time: 184 us -> 177 us (0.962)
  starting transfers between devices: 20.8 us -> 17.7 us
  blocking collectives: 128 us -> 125 us
  local copies, waits for them, and re-layouts: 2.66 us -> 0.7 us
    ppermute x4, starting transfers between devices: 8.74 us -> 5.56 us  [the longest x1 3.56 us: local(): near = lax.ppermute(payload, 'sub', cross)]
    all_to_all x4, blocking collectives: 74.8 us -> 72.4 us  [local(): source = lax.all_to_all(send, ('grp', 'sub'), 0, 0, tiled=True)]
    unnamed x14, local copies, waits for them, and re-layouts: 2.66 us -> 0.7 us
  transfers between devices with their start and end apart: 11 -> 11, of which waited for: 1 -> 3; matrix products, arithmetic and copies ran while one was open for 0% -> 0% of each run, Pallas kernels for 3% -> 3%
where the time goes in v5:
time: 177 us
  blocking collectives  125 us (71%)
  Pallas kernels  21.4 us (12%)
  starting transfers between devices  17.7 us (10%)
  waiting for transfers between devices  8.99 us (5%)
    all_to_all x4, blocking collectives, local(): source = lax.all_to_all(send, ('grp', 'sub'), 0, 0, tiled=True)  72.4 us
    all_to_all x4, blocking collectives, local(): parts = lax.all_to_all(parts, 'sub', 0, 0, tiled=True)  53 us
    pallas_call x3, Pallas kernels, local(): call(functools.partial(middle_kernel, full=full), 'vvvvvvv', [keep_out, f...  10.1 us
    ppermute x3, starting transfers between devices, local(): beside = lax.ppermute(keep, 'sub', cross)  7.52 us
    pallas_call x4, Pallas kernels, local(): call(functools.partial(patch_kernel, final=final), 'vvvvv', [((subs, 8 if...  6.09 us
    ppermute x1, waiting for transfers between devices, local(): near = lax.ppermute(payload, 'sub', cross)  4.92 us
    ppermute x1, starting transfers between devices, local(): near = lax.ppermute(payload, 'sub', cross)  3.56 us
    ppermute x1, waiting for transfers between devices, local(): far = lax.ppermute(far, 'sub', cross)  3.55 us
  transfers between devices with their start and end apart: 11, of which 3 were waited for; matrix products, arithmetic and copies ran while one was open for 0% of the time, Pallas kernels for 3%

profile of v5, /device:TPU:1, one launch (start us, length us, event | category | flops | bytes accessed | tf_op | source)
XLA Modules:
  0.0 176.5 jit_solution(6077066127654727633)
XLA Ops:
  0.6 0.0 copy-start
  0.6 0.0 copy-start.2
  0.7 1.4 pad_maximum_fusion.fields
  2.1 0.0 copy-start.3
  2.1 0.7 copy-done.3
  2.8 0.0 copy-start.4
  2.8 0.0 copy-start.5
  2.8 0.0 copy-start.6
  2.8 0.1 shard_map.123.own
  2.9 1.5 collective-permute-start
  4.4 3.6 %collective-permute-start.1 = (f32[1032,128]{1,0:T(8,128)S(1)}, f32[1032,128]{1,0:T(8,128)S(1)}, u32[]{:S(2)}, u32[]{:S(2)}) collective-permute-start(f32[1032,128]{1,0:T(8,128)S(1)} %shard_map.123.own), channel_id=1, source_target_pairs={{1,2},{2,1},{3,4},{4,3},{5,6},{6,5},{7,8},{8,7},{9,10},{10,9},{11,... | collective-permute-start | bytes 1585160 | tf_op jit(solution)/shard_map/ppermute | solution.py:349
  7.9 0.0 collective-permute-done.mate
  8.0 2.0 %collective-permute-start.3 = (f32[648,128]{1,0:T(8,128)S(1)}, f32[648,128]{1,0:T(8,128)S(1)}, u32[]{:S(2)}, u32[]{:S(2)}) collective-permute-start(f32[648,128]{1,0:T(8,128)S(1)} %shard_map.124), channel_id=1, source_target_pairs={{1,2},{2,1},{3,4},{4,3},{5,6},{6,5},{7,8},{8,7},{9,10},{10,9},{11,... | collective-permute-start | bytes 995336 | tf_op jit(solution)/shard_map/ppermute | solution.py:352
  10.0 4.9 %collective-permute-done.1.near = f32[1032,128]{1,0:T(8,128)S(1)} collective-permute-done((f32[1032,128]{1,0:T(8,128)S(1)}, f32[1032,128]{1,0:T(8,128)S(1)}, u32[]{:S(2)}, u32[]{:S(2)}) %collective-permute-start.1) | collective-permute-done | bytes 528416 | tf_op jit(solution)/shard_map/ppermute | solution.py:349
  14.9 0.0 collective-permute-start.2
  14.9 3.6 %collective-permute-done.3.far = f32[648,128]{1,0:T(8,128)S(1)} collective-permute-done((f32[648,128]{1,0:T(8,128)S(1)}, f32[648,128]{1,0:T(8,128)S(1)}, u32[]{:S(2)}, u32[]{:S(2)}) %collective-permute-start.3) | collective-permute-done | bytes 331808 | tf_op jit(solution)/shard_map/ppermute | solution.py:352
  18.5 0.0 collective-permute-start.4
  18.5 0.0 copy-done
  18.5 0.0 copy-done.2
  18.5 0.0 copy-done.4
  18.5 0.0 copy-done.5
  18.5 0.0 copy-done.6
  18.5 1.1 shard_map.122
  19.6 0.0 collective-permute-done.2.near_other
  19.6 0.5 collective-permute-done.4.far_other
  20.1 0.0 copy-start.1
  20.1 3.0 %shard_map.125 = (f32[520,128]{1,0:T(8,128)S(1)}, f32[128,4,128]{2,1,0:T(4,128)S(1)}, f32[3,10,128,128]{3,2,1,0:T(8,128)S(1)}, s32[6,4,128]{2,1,0:T(4,128)S(1)}) custom-call(f32[8,128]{1,0:T(8,128)S(1)} %get-tuple-element.30.flts, f32[1032,128]{1,0:T(8,128)S(1)} %shard_map.123.own, f32[1032,128]{1,0:T(8,128)S(1)} %collective-permute-done.mate, ...), custom_call_target="tpu_custom_call" | custom-call | tf_op jit(solution)/shard_map/pallas_call | solution.py:372
  23.1 3.7 %collective-permute-start.5 = (f32[520,128]{1,0:T(8,128)S(1)}, f32[520,128]{1,0:T(8,128)S(1)}, u32[]{:S(2)}, u32[]{:S(2)}) collective-permute-start(f32[520,128]{1,0:T(8,128)S(1)} %get-tuple-element.33.own), channel_id=1, source_target_pairs={{1,2},{2,1},{3,4},{4,3},{5,6},{6,5},{7,8},{8,7},{9,10},{10,9},{11,... | collective-permute-start | bytes 798728 | tf_op jit(solution)/shard_map/ppermute | solution.py:381
  26.8 22.5 %all_to_all.40.source = f32[128,4,128]{2,1,0:T(4,128)S(1)} all-to-all(f32[128,4,128]{2,1,0:T(4,128)S(1)} %get-tuple-element.32), channel_id=1, replica_groups=mesh['grp'=4,'sub'=32] {'grp','sub'}, dimensions={0} | all-to-all | bytes 524288 | tf_op jit(solution)/shard_map/all_to_all | solution.py:382
  49.3 0.0 collective-permute-done.5.beside
  49.3 1.1 collective-permute-start.6
  50.4 0.0 copy-done.1
  50.4 1.4 shard_map.126
  51.8 0.0 collective-permute-done.6.other
  51.8 13.7 %all_to_all.41.parts = f32[32,24,128]{2,1,0:T(8,128)S(1)} all-to-all(f32[32,24,128]{2,1,0:T(8,128)S(1)} %shard_map.126), channel_id=1, replica_groups=mesh['grp'=4,'sub'=32] {'sub'}, dimensions={0} | all-to-all | bytes 786432 | tf_op jit(solution)/shard_map/all_to_all | solution.py:393
  65.4 3.3 %shard_map.127 = (f32[520,128]{1,0:T(8,128)S(1)}, f32[128,4,128]{2,1,0:T(4,128)S(1)}) custom-call(f32[8,128]{1,0:T(8,128)S(1)} %get-tuple-element.30.flts, f32[32,24,128]{2,1,0:T(8,128)S(1)} %all_to_all.41.parts, f32[520,128]{1,0:T(8,128)S(1)} %get-tuple-element.33.own, f32[520,128]{1,0:T(8,128)S(1)} %collective-permute-done.5.beside, ...), custom_call_target="tpu_custom_call" | custom-call | tf_op jit(solution)/shard_map/pallas_call | solution.py:403
  68.8 1.9 %collective-permute-start.7 = (f32[520,128]{1,0:T(8,128)S(1)}, f32[520,128]{1,0:T(8,128)S(1)}, u32[]{:S(2)}, u32[]{:S(2)}) collective-permute-start(f32[520,128]{1,0:T(8,128)S(1)} %get-tuple-element.43.own), channel_id=1, source_target_pairs={{1,2},{2,1},{3,4},{4,3},{5,6},{6,5},{7,8},{8,7},{9,10},{10,9},{11,... | collective-permute-start | bytes 798728 | tf_op jit(solution)/shard_map/ppermute | solution.py:381
  70.7 16.5 %all_to_all.42.source = f32[128,4,128]{2,1,0:T(4,128)S(1)} all-to-all(f32[128,4,128]{2,1,0:T(4,128)S(1)} %get-tuple-element.42), channel_id=1, replica_groups=mesh['grp'=4,'sub'=32] {'grp','sub'}, dimensions={0} | all-to-all | bytes 524288 | tf_op jit(solution)/shard_map/all_to_all | solution.py:382
  87.2 0.0 collective-permute-done.7.beside
  87.3 1.1 collective-permute-start.8
  88.3 1.4 shard_map.128
  89.7 0.0 collective-permute-done.8.other
  89.7 13.7 %all_to_all.43.parts = f32[32,24,128]{2,1,0:T(8,128)S(1)} all-to-all(f32[32,24,128]{2,1,0:T(8,128)S(1)} %shard_map.128), channel_id=1, replica_groups=mesh['grp'=4,'sub'=32] {'sub'}, dimensions={0} | all-to-all | bytes 786432 | tf_op jit(solution)/shard_map/all_to_all | solution.py:393
  103.4 3.4 %shard_map.129 = (f32[520,128]{1,0:T(8,128)S(1)}, f32[128,4,128]{2,1,0:T(4,128)S(1)}) custom-call(f32[8,128]{1,0:T(8,128)S(1)} %get-tuple-element.30.flts, f32[32,24,128]{2,1,0:T(8,128)S(1)} %all_to_all.43.parts, f32[520,128]{1,0:T(8,128)S(1)} %get-tuple-element.43.own, f32[520,128]{1,0:T(8,128)S(1)} %collective-permute-done.7.beside, ...), custom_call_target="tpu_custom_call" | custom-call | tf_op jit(solution)/shard_map/pallas_call | solution.py:403
  106.7 1.9 %collective-permute-start.9 = (f32[520,128]{1,0:T(8,128)S(1)}, f32[520,128]{1,0:T(8,128)S(1)}, u32[]{:S(2)}, u32[]{:S(2)}) collective-permute-start(f32[520,128]{1,0:T(8,128)S(1)} %get-tuple-element.49.own), channel_id=1, source_target_pairs={{1,2},{2,1},{3,4},{4,3},{5,6},{6,5},{7,8},{8,7},{9,10},{10,9},{11,... | collective-permute-start | bytes 798728 | tf_op jit(solution)/shard_map/ppermute | solution.py:381
  108.7 16.5 %all_to_all.44.source = f32[128,4,128]{2,1,0:T(4,128)S(1)} all-to-all(f32[128,4,128]{2,1,0:T(4,128)S(1)} %get-tuple-element.48), channel_id=1, replica_groups=mesh['grp'=4,'sub'=32] {'grp','sub'}, dimensions={0} | all-to-all | bytes 524288 | tf_op jit(solution)/shard_map/all_to_all | solution.py:382
  125.2 0.0 collective-permute-done.9.beside
  125.2 1.1 collective-permute-start.10
  126.3 1.4 shard_map.130
  127.7 0.0 collective-permute-done.10.other
  127.7 13.7 %all_to_all.45.parts = f32[32,24,128]{2,1,0:T(8,128)S(1)} all-to-all(f32[32,24,128]{2,1,0:T(8,128)S(1)} %shard_map.130), channel_id=1, replica_groups=mesh['grp'=4,'sub'=32] {'sub'}, dimensions={0} | all-to-all | bytes 786432 | tf_op jit(solution)/shard_map/all_to_all | solution.py:393
  141.3 3.4 %shard_map.131 = (f32[520,128]{1,0:T(8,128)S(1)}, f32[128,8,128]{2,1,0:T(8,128)S(1)}) custom-call(f32[8,128]{1,0:T(8,128)S(1)} %get-tuple-element.30.flts, f32[32,24,128]{2,1,0:T(8,128)S(1)} %all_to_all.45.parts, f32[520,128]{1,0:T(8,128)S(1)} %get-tuple-element.49.own, f32[520,128]{1,0:T(8,128)S(1)} %collective-permute-done.9.beside, ...), custom_call_target="tpu_custom_call" | custom-call | tf_op jit(solution)/shard_map/pallas_call | solution.py:403
  144.7 16.9 %all_to_all.46.source = f32[128,8,128]{2,1,0:T(8,128)S(1)} all-to-all(f32[128,8,128]{2,1,0:T(8,128)S(1)} %get-tuple-element.54), channel_id=1, replica_groups=mesh['grp'=4,'sub'=32] {'grp','sub'}, dimensions={0} | all-to-all | bytes 1048576 | tf_op jit(solution)/shard_map/all_to_all | solution.py:382
  161.5 2.0 %shard_map.132 = f32[32,8,128]{2,1,0:T(8,128)S(1)} custom-call(s32[8,128]{1,0:T(8,128)S(1)} %get-tuple-element.31.ints, f32[128,8,128]{2,1,0:T(8,128)S(1)} %all_to_all.46.source, s32[24,128]{1,0:T(8,128)S(1)} %get-tuple-element.35.place, s32[24,128]{1,0:T(8,128)S(1)} %bitcast.9, f32[24,128,128]{2,1,0:T(8,128)S(1)} %get-tuple-element.36.maps), custom_call_target="tpu_custom_call" | custom-call | tf_op jit(solution)/shard_map/pallas_call | solution.py:386
  163.5 12.1 %all_to_all.47.parts = f32[32,8,128]{2,1,0:T(8,128)S(1)} all-to-all(f32[32,8,128]{2,1,0:T(8,128)S(1)} %shard_map.132), channel_id=1, replica_groups=mesh['grp'=4,'sub'=32] {'sub'}, dimensions={0} | all-to-all | bytes 262144 | tf_op jit(solution)/shard_map/all_to_all | solution.py:393
  175.6 1.0 shard_map.133
  (1 shorter events, 0.0 us)
Async XLA Ops:
  0.6 17.8 %copy-start = (f32[1,24,128,128]{3,2,1,0:T(8,128)S(1)}, f32[1,24,128,128]{3,2,1,0:T(8,128)}, u32[]{:S(2)}) copy-start(f32[1,24,128,128]{3,2,1,0:T(8,128)} %param.21) | copy-start | bytes 4718596
  0.6 17.8 %copy-start.2 = (s32[1,24,128]{2,1,0:T(8,128)S(1)}, s32[1,24,128]{2,1,0:T(8,128)}, u32[]{:S(2)}) copy-start(s32[1,24,128]{2,1,0:T(8,128)} %param.19) | copy-start | bytes 36868
  2.1 0.7 copy-start.3
  2.8 15.7 %copy-start.4 = (s32[4]{0:T(128)S(1)}, s32[4]{0:T(128)}, u32[]{:S(2)}) copy-start(s32[4]{0:T(128)} %kinds.1) | copy-start | bytes 52
  2.8 15.7 %copy-start.5 = (s32[4]{0:T(128)S(1)}, s32[4]{0:T(128)}, u32[]{:S(2)}) copy-start(s32[4]{0:T(128)} %partners.1) | copy-start | bytes 52
  2.8 15.7 %copy-start.6 = (s32[1,32]{1,0:T(1,128)S(1)}, s32[1,32]{1,0:T(1,128)}, u32[]{:S(2)}) copy-start(s32[1,32]{1,0:T(1,128)} %counts.1) | copy-start | bytes 388
  2.9 5.0 %collective-permute-start = (f32[1032,128]{1,0:T(8,128)S(1)}, f32[1032,128]{1,0:T(8,128)S(1)}, u32[]{:S(2)}, u32[]{:S(2)}) collective-permute-start(f32[1032,128]{1,0:T(8,128)S(1)} %shard_map.123.own), channel_id=1, source_target_pairs={{0,1},{1,0},{2,3},{3,2},{4,5},{5,4},{6,7},{7,6},{8,9},{9,8},{10,11... | collective-permute-start | bytes 1585160 | tf_op jit(solution)/shard_map/ppermute | solution.py:350
  4.4 10.5 %collective-permute-start.1 = (f32[1032,128]{1,0:T(8,128)S(1)}, f32[1032,128]{1,0:T(8,128)S(1)}, u32[]{:S(2)}, u32[]{:S(2)}) collective-permute-start(f32[1032,128]{1,0:T(8,128)S(1)} %shard_map.123.own), channel_id=1, source_target_pairs={{1,2},{2,1},{3,4},{4,3},{5,6},{6,5},{7,8},{8,7},{9,10},{10,9},{11,... | collective-permute-start | bytes 1585160 | tf_op jit(solution)/shard_map/ppermute | solution.py:349
  8.0 10.5 %collective-permute-start.3 = (f32[648,128]{1,0:T(8,128)S(1)}, f32[648,128]{1,0:T(8,128)S(1)}, u32[]{:S(2)}, u32[]{:S(2)}) collective-permute-start(f32[648,128]{1,0:T(8,128)S(1)} %shard_map.124), channel_id=1, source_target_pairs={{1,2},{2,1},{3,4},{4,3},{5,6},{6,5},{7,8},{8,7},{9,10},{10,9},{11,... | collective-permute-start | bytes 995336 | tf_op jit(solution)/shard_map/ppermute | solution.py:352
  14.9 4.7 %collective-permute-start.2 = (f32[1032,128]{1,0:T(8,128)S(1)}, f32[1032,128]{1,0:T(8,128)S(1)}, u32[]{:S(2)}, u32[]{:S(2)}) collective-permute-start(f32[1032,128]{1,0:T(8,128)S(1)} %collective-permute-done.1.near), channel_id=1, source_target_pairs={{0,1},{1,0},{2,3},{3,2},{4,5},{5,4},{6,7},{7,6},{8,9},{9,8},{10,11... | collective-permute-start | bytes 1585160 | tf_op jit(solution)/shard_map/ppermute | solution.py:364
  18.5 1.6 collective-permute-start.4
  20.1 30.3 %copy-start.1 = (s32[1,24,128]{2,1,0:T(8,128)S(1)}, s32[1,24,128]{2,1,0:T(8,128)}, u32[]{:S(2)}) copy-start(s32[1,24,128]{2,1,0:T(8,128)} %param.20) | copy-start | bytes 36868
  23.1 26.2 %collective-permute-start.5 = (f32[520,128]{1,0:T(8,128)S(1)}, f32[520,128]{1,0:T(8,128)S(1)}, u32[]{:S(2)}, u32[]{:S(2)}) collective-permute-start(f32[520,128]{1,0:T(8,128)S(1)} %get-tuple-element.33.own), channel_id=1, source_target_pairs={{1,2},{2,1},{3,4},{4,3},{5,6},{6,5},{7,8},{8,7},{9,10},{10,9},{11,... | collective-permute-start | bytes 798728 | tf_op jit(solution)/shard_map/ppermute | solution.py:381
  49.3 2.5 %collective-permute-start.6 = (f32[520,128]{1,0:T(8,128)S(1)}, f32[520,128]{1,0:T(8,128)S(1)}, u32[]{:S(2)}, u32[]{:S(2)}) collective-permute-start(f32[520,128]{1,0:T(8,128)S(1)} %collective-permute-done.5.beside), channel_id=1, source_target_pairs={{0,1},{1,0},{2,3},{3,2},{4,5},{5,4},{6,7},{7,6},{8,9},{9,8},{10,11... | collective-permute-start | bytes 798728 | tf_op jit(solution)/shard_map/ppermute | solution.py:385
  68.8 18.5 %collective-permute-start.7 = (f32[520,128]{1,0:T(8,128)S(1)}, f32[520,128]{1,0:T(8,128)S(1)}, u32[]{:S(2)}, u32[]{:S(2)}) collective-permute-start(f32[520,128]{1,0:T(8,128)S(1)} %get-tuple-element.43.own), channel_id=1, source_target_pairs={{1,2},{2,1},{3,4},{4,3},{5,6},{6,5},{7,8},{8,7},{9,10},{10,9},{11,... | collective-permute-start | bytes 798728 | tf_op jit(solution)/shard_map/ppermute | solution.py:381
  87.3 2.5 %collective-permute-start.8 = (f32[520,128]{1,0:T(8,128)S(1)}, f32[520,128]{1,0:T(8,128)S(1)}, u32[]{:S(2)}, u32[]{:S(2)}) collective-permute-start(f32[520,128]{1,0:T(8,128)S(1)} %collective-permute-done.7.beside), channel_id=1, source_target_pairs={{0,1},{1,0},{2,3},{3,2},{4,5},{5,4},{6,7},{7,6},{8,9},{9,8},{10,11... | collective-permute-start | bytes 798728 | tf_op jit(solution)/shard_map/ppermute | solution.py:385
  106.7 18.5 %collective-permute-start.9 = (f32[520,128]{1,0:T(8,128)S(1)}, f32[520,128]{1,0:T(8,128)S(1)}, u32[]{:S(2)}, u32[]{:S(2)}) collective-permute-start(f32[520,128]{1,0:T(8,128)S(1)} %get-tuple-element.49.own), channel_id=1, source_target_pairs={{1,2},{2,1},{3,4},{4,3},{5,6},{6,5},{7,8},{8,7},{9,10},{10,9},{11,... | collective-permute-start | bytes 798728 | tf_op jit(solution)/shard_map/ppermute | solution.py:381
  125.2 2.5 %collective-permute-start.10 = (f32[520,128]{1,0:T(8,128)S(1)}, f32[520,128]{1,0:T(8,128)S(1)}, u32[]{:S(2)}, u32[]{:S(2)}) collective-permute-start(f32[520,128]{1,0:T(8,128)S(1)} %collective-permute-done.9.beside), channel_id=1, source_target_pairs={{0,1},{1,0},{2,3},{3,2},{4,5},{5,4},{6,7},{7,6},{8,9},{9,8},{10,11... | collective-permute-start | bytes 798728 | tf_op jit(solution)/shard_map/ppermute | solution.py:385

commit v6 on v5

--- a/solution.py
+++ b/solution.py
@@ -36,11 +36,9 @@
 
         def body(p, carry, src=src, dst=dst):
             x = src[p]
-            dst[p] = (
-                x
-                + coef[0, p - 1] * (src[p + 1] + in_plane(x) - 5.0 * x)
-                + coef[1, p - 1] * (src[p - 1] - x)
-                + coef[2, p - 1] * (1.0 + jnp.tanh(x))
+            near = src[p + 1] + in_plane(x)
+            dst[p] = (coef[3, p - 1] * x + coef[0, p - 1] * near) + (
+                coef[1, p - 1] * src[p - 1] + coef[2, p - 1] * (1.0 + jnp.tanh(x))
             )
             return carry
 
@@ -212,7 +210,9 @@
         for side, plane in enumerate(planes):
             conduct, velocity, heat = (g[side] for g in got)
             coef[0, plane - 1] = conduct
-            coef[1, plane - 1] = conduct + gas * velocity
+            flow = conduct + gas * velocity
+            coef[1, plane - 1] = flow
+            coef[3, plane - 1] = 1.0 - 5.0 * conduct - flow
             coef[2, plane - 1] = (0.5 * gas) * heat
 
     for half in range(2):
@@ -367,7 +367,7 @@
     keep_out = ((4 * ROWS + 8, 128), F32, "v")
     half_out = ((groups * subs, 4, 128), F32, "v")
     full_out = ((groups * subs, 8, 128), F32, "v")
-    coef_shape = (3, WIDE - 2, ROWS, 128)
+    coef_shape = (4, WIDE - 2, ROWS, 128)
     work = [(WIDE, ROWS, 128), (WIDE, ROWS, 128), (2 * ROWS, 128)]
     keep, send, coef, surf = call(
         first_kernel,

time: 177 us -> 177 us (level)
  no operation moved by 1% of the time
where the time goes in v6:
time: 177 us
  blocking collectives  125 us (71%)
  Pallas kernels  21.6 us (12%)
  starting transfers between devices  17.7 us (10%)
  waiting for transfers between devices  8.99 us (5%)
    all_to_all x4, blocking collectives, local(): source = lax.all_to_all(send, ('grp', 'sub'), 0, 0, tiled=True)  72.4 us
    all_to_all x4, blocking collectives, local(): parts = lax.all_to_all(parts, 'sub', 0, 0, tiled=True)  53 us
    pallas_call x3, Pallas kernels, local(): call(functools.partial(middle_kernel, full=full), 'vvvvvvv', [keep_out, f...  10.1 us
    ppermute x3, starting transfers between devices, local(): beside = lax.ppermute(keep, 'sub', cross)  7.52 us
    pallas_call x4, Pallas kernels, local(): call(functools.partial(patch_kernel, final=final), 'vvvvv', [((subs, 8 if...  6.11 us
    ppermute x1, waiting for transfers between devices, local(): near = lax.ppermute(payload, 'sub', cross)  4.92 us
    ppermute x1, starting transfers between devices, local(): near = lax.ppermute(payload, 'sub', cross)  3.56 us
    ppermute x1, waiting for transfers between devices, local(): far = lax.ppermute(far, 'sub', cross)  3.55 us
  transfers between devices with their start and end apart: 11, of which 3 were waited for; matrix products, arithmetic and copies ran while one was open for 0% of the time, Pallas kernels for 3%

profile of v6, /device:TPU:1, one launch (start us, length us, event | category | flops | bytes accessed | tf_op | source)
XLA Modules:
  0.0 176.7 jit_solution(1136127260928187073)
XLA Ops:
  0.6 0.0 copy-start
  0.6 0.0 copy-start.2
  0.7 1.4 pad_maximum_fusion.fields
  2.1 0.0 copy-start.3
  2.1 0.7 copy-done.3
  2.8 0.0 copy-start.4
  2.8 0.0 copy-start.5
  2.8 0.0 copy-start.6
  2.8 0.1 shard_map.123.own
  2.9 1.5 collective-permute-start
  4.4 3.6 %collective-permute-start.1 = (f32[1032,128]{1,0:T(8,128)S(1)}, f32[1032,128]{1,0:T(8,128)S(1)}, u32[]{:S(2)}, u32[]{:S(2)}) collective-permute-start(f32[1032,128]{1,0:T(8,128)S(1)} %shard_map.123.own), channel_id=1, source_target_pairs={{1,2},{2,1},{3,4},{4,3},{5,6},{6,5},{7,8},{8,7},{9,10},{10,9},{11,... | collective-permute-start | bytes 1585160 | tf_op jit(solution)/shard_map/ppermute | solution.py:349
  7.9 0.0 collective-permute-done.mate
  8.0 2.0 %collective-permute-start.3 = (f32[648,128]{1,0:T(8,128)S(1)}, f32[648,128]{1,0:T(8,128)S(1)}, u32[]{:S(2)}, u32[]{:S(2)}) collective-permute-start(f32[648,128]{1,0:T(8,128)S(1)} %shard_map.124), channel_id=1, source_target_pairs={{1,2},{2,1},{3,4},{4,3},{5,6},{6,5},{7,8},{8,7},{9,10},{10,9},{11,... | collective-permute-start | bytes 995336 | tf_op jit(solution)/shard_map/ppermute | solution.py:352
  10.0 4.9 %collective-permute-done.1.near = f32[1032,128]{1,0:T(8,128)S(1)} collective-permute-done((f32[1032,128]{1,0:T(8,128)S(1)}, f32[1032,128]{1,0:T(8,128)S(1)}, u32[]{:S(2)}, u32[]{:S(2)}) %collective-permute-start.1) | collective-permute-done | bytes 528416 | tf_op jit(solution)/shard_map/ppermute | solution.py:349
  14.9 0.0 collective-permute-start.2
  14.9 3.6 %collective-permute-done.3.far = f32[648,128]{1,0:T(8,128)S(1)} collective-permute-done((f32[648,128]{1,0:T(8,128)S(1)}, f32[648,128]{1,0:T(8,128)S(1)}, u32[]{:S(2)}, u32[]{:S(2)}) %collective-permute-start.3) | collective-permute-done | bytes 331808 | tf_op jit(solution)/shard_map/ppermute | solution.py:352
  18.5 0.0 collective-permute-start.4
  18.5 0.0 copy-done
  18.5 0.0 copy-done.2
  18.5 0.0 copy-done.4
  18.5 0.0 copy-done.5
  18.5 0.0 copy-done.6
  18.5 1.1 shard_map.122
  19.6 0.0 collective-permute-done.2.near_other
  19.6 0.5 collective-permute-done.4.far_other
  20.1 0.0 copy-start.1
  20.1 3.2 %shard_map.125 = (f32[520,128]{1,0:T(8,128)S(1)}, f32[128,4,128]{2,1,0:T(4,128)S(1)}, f32[4,10,128,128]{3,2,1,0:T(8,128)S(1)}, s32[6,4,128]{2,1,0:T(4,128)S(1)}) custom-call(f32[8,128]{1,0:T(8,128)S(1)} %get-tuple-element.30.flts, f32[1032,128]{1,0:T(8,128)S(1)} %shard_map.123.own, f32[1032,128]{1,0:T(8,128)S(1)} %collective-permute-done.mate, ...), custom_call_target="tpu_custom_call" | custom-call | tf_op jit(solution)/shard_map/pallas_call | solution.py:372
  23.3 3.7 %collective-permute-start.5 = (f32[520,128]{1,0:T(8,128)S(1)}, f32[520,128]{1,0:T(8,128)S(1)}, u32[]{:S(2)}, u32[]{:S(2)}) collective-permute-start(f32[520,128]{1,0:T(8,128)S(1)} %get-tuple-element.33.own), channel_id=1, source_target_pairs={{1,2},{2,1},{3,4},{4,3},{5,6},{6,5},{7,8},{8,7},{9,10},{10,9},{11,... | collective-permute-start | bytes 798728 | tf_op jit(solution)/shard_map/ppermute | solution.py:381
  27.0 22.5 %all_to_all.40.source = f32[128,4,128]{2,1,0:T(4,128)S(1)} all-to-all(f32[128,4,128]{2,1,0:T(4,128)S(1)} %get-tuple-element.32), channel_id=1, replica_groups=mesh['grp'=4,'sub'=32] {'grp','sub'}, dimensions={0} | all-to-all | bytes 524288 | tf_op jit(solution)/shard_map/all_to_all | solution.py:382
  49.5 0.0 collective-permute-done.5.beside
  49.5 1.1 collective-permute-start.6
  50.5 0.0 copy-done.1
  50.5 1.4 shard_map.126
  51.9 0.0 collective-permute-done.6.other
  51.9 13.7 %all_to_all.41.parts = f32[32,24,128]{2,1,0:T(8,128)S(1)} all-to-all(f32[32,24,128]{2,1,0:T(8,128)S(1)} %shard_map.126), channel_id=1, replica_groups=mesh['grp'=4,'sub'=32] {'sub'}, dimensions={0} | all-to-all | bytes 786432 | tf_op jit(solution)/shard_map/all_to_all | solution.py:393
  65.6 3.4 %shard_map.127 = (f32[520,128]{1,0:T(8,128)S(1)}, f32[128,4,128]{2,1,0:T(4,128)S(1)}) custom-call(f32[8,128]{1,0:T(8,128)S(1)} %get-tuple-element.30.flts, f32[32,24,128]{2,1,0:T(8,128)S(1)} %all_to_all.41.parts, f32[520,128]{1,0:T(8,128)S(1)} %get-tuple-element.33.own, f32[520,128]{1,0:T(8,128)S(1)} %collective-permute-done.5.beside, ...), custom_call_target="tpu_custom_call" | custom-call | tf_op jit(solution)/shard_map/pallas_call | solution.py:403
  68.9 1.9 %collective-permute-start.7 = (f32[520,128]{1,0:T(8,128)S(1)}, f32[520,128]{1,0:T(8,128)S(1)}, u32[]{:S(2)}, u32[]{:S(2)}) collective-permute-start(f32[520,128]{1,0:T(8,128)S(1)} %get-tuple-element.43.own), channel_id=1, source_target_pairs={{1,2},{2,1},{3,4},{4,3},{5,6},{6,5},{7,8},{8,7},{9,10},{10,9},{11,... | collective-permute-start | bytes 798728 | tf_op jit(solution)/shard_map/ppermute | solution.py:381
  70.9 16.5 %all_to_all.42.source = f32[128,4,128]{2,1,0:T(4,128)S(1)} all-to-all(f32[128,4,128]{2,1,0:T(4,128)S(1)} %get-tuple-element.42), channel_id=1, replica_groups=mesh['grp'=4,'sub'=32] {'grp','sub'}, dimensions={0} | all-to-all | bytes 524288 | tf_op jit(solution)/shard_map/all_to_all | solution.py:382
  87.4 0.0 collective-permute-done.7.beside
  87.4 1.1 collective-permute-start.8
  88.5 1.4 shard_map.128
  89.9 0.0 collective-permute-done.8.other
  89.9 13.7 %all_to_all.43.parts = f32[32,24,128]{2,1,0:T(8,128)S(1)} all-to-all(f32[32,24,128]{2,1,0:T(8,128)S(1)} %shard_map.128), channel_id=1, replica_groups=mesh['grp'=4,'sub'=32] {'sub'}, dimensions={0} | all-to-all | bytes 786432 | tf_op jit(solution)/shard_map/all_to_all | solution.py:393
  103.5 3.3 %shard_map.129 = (f32[520,128]{1,0:T(8,128)S(1)}, f32[128,4,128]{2,1,0:T(4,128)S(1)}) custom-call(f32[8,128]{1,0:T(8,128)S(1)} %get-tuple-element.30.flts, f32[32,24,128]{2,1,0:T(8,128)S(1)} %all_to_all.43.parts, f32[520,128]{1,0:T(8,128)S(1)} %get-tuple-element.43.own, f32[520,128]{1,0:T(8,128)S(1)} %collective-permute-done.7.beside, ...), custom_call_target="tpu_custom_call" | custom-call | tf_op jit(solution)/shard_map/pallas_call | solution.py:403
  106.9 1.9 %collective-permute-start.9 = (f32[520,128]{1,0:T(8,128)S(1)}, f32[520,128]{1,0:T(8,128)S(1)}, u32[]{:S(2)}, u32[]{:S(2)}) collective-permute-start(f32[520,128]{1,0:T(8,128)S(1)} %get-tuple-element.49.own), channel_id=1, source_target_pairs={{1,2},{2,1},{3,4},{4,3},{5,6},{6,5},{7,8},{8,7},{9,10},{10,9},{11,... | collective-permute-start | bytes 798728 | tf_op jit(solution)/shard_map/ppermute | solution.py:381
  108.8 16.5 %all_to_all.44.source = f32[128,4,128]{2,1,0:T(4,128)S(1)} all-to-all(f32[128,4,128]{2,1,0:T(4,128)S(1)} %get-tuple-element.48), channel_id=1, replica_groups=mesh['grp'=4,'sub'=32] {'grp','sub'}, dimensions={0} | all-to-all | bytes 524288 | tf_op jit(solution)/shard_map/all_to_all | solution.py:382
  125.4 0.0 collective-permute-done.9.beside
  125.4 1.1 collective-permute-start.10
  126.4 1.4 shard_map.130
  127.8 0.0 collective-permute-done.10.other
  127.8 13.7 %all_to_all.45.parts = f32[32,24,128]{2,1,0:T(8,128)S(1)} all-to-all(f32[32,24,128]{2,1,0:T(8,128)S(1)} %shard_map.130), channel_id=1, replica_groups=mesh['grp'=4,'sub'=32] {'sub'}, dimensions={0} | all-to-all | bytes 786432 | tf_op jit(solution)/shard_map/all_to_all | solution.py:393
  141.5 3.4 %shard_map.131 = (f32[520,128]{1,0:T(8,128)S(1)}, f32[128,8,128]{2,1,0:T(8,128)S(1)}) custom-call(f32[8,128]{1,0:T(8,128)S(1)} %get-tuple-element.30.flts, f32[32,24,128]{2,1,0:T(8,128)S(1)} %all_to_all.45.parts, f32[520,128]{1,0:T(8,128)S(1)} %get-tuple-element.49.own, f32[520,128]{1,0:T(8,128)S(1)} %collective-permute-done.9.beside, ...), custom_call_target="tpu_custom_call" | custom-call | tf_op jit(solution)/shard_map/pallas_call | solution.py:403
  144.8 16.9 %all_to_all.46.source = f32[128,8,128]{2,1,0:T(8,128)S(1)} all-to-all(f32[128,8,128]{2,1,0:T(8,128)S(1)} %get-tuple-element.54), channel_id=1, replica_groups=mesh['grp'=4,'sub'=32] {'grp','sub'}, dimensions={0} | all-to-all | bytes 1048576 | tf_op jit(solution)/shard_map/all_to_all | solution.py:382
  161.7 2.0 %shard_map.132 = f32[32,8,128]{2,1,0:T(8,128)S(1)} custom-call(s32[8,128]{1,0:T(8,128)S(1)} %get-tuple-element.31.ints, f32[128,8,128]{2,1,0:T(8,128)S(1)} %all_to_all.46.source, s32[24,128]{1,0:T(8,128)S(1)} %get-tuple-element.35.place, s32[24,128]{1,0:T(8,128)S(1)} %bitcast.9, f32[24,128,128]{2,1,0:T(8,128)S(1)} %get-tuple-element.36.maps), custom_call_target="tpu_custom_call" | custom-call | tf_op jit(solution)/shard_map/pallas_call | solution.py:386
  163.7 12.1 %all_to_all.47.parts = f32[32,8,128]{2,1,0:T(8,128)S(1)} all-to-all(f32[32,8,128]{2,1,0:T(8,128)S(1)} %shard_map.132), channel_id=1, replica_groups=mesh['grp'=4,'sub'=32] {'sub'}, dimensions={0} | all-to-all | bytes 262144 | tf_op jit(solution)/shard_map/all_to_all | solution.py:393
  175.7 1.0 shard_map.133
  (1 shorter events, 0.0 us)
Async XLA Ops:
  0.6 17.8 %copy-start = (f32[1,24,128,128]{3,2,1,0:T(8,128)S(1)}, f32[1,24,128,128]{3,2,1,0:T(8,128)}, u32[]{:S(2)}) copy-start(f32[1,24,128,128]{3,2,1,0:T(8,128)} %param.21) | copy-start | bytes 4718596
  0.6 17.8 %copy-start.2 = (s32[1,24,128]{2,1,0:T(8,128)S(1)}, s32[1,24,128]{2,1,0:T(8,128)}, u32[]{:S(2)}) copy-start(s32[1,24,128]{2,1,0:T(8,128)} %param.19) | copy-start | bytes 36868
  2.1 0.7 copy-start.3
  2.8 15.7 %copy-start.4 = (s32[4]{0:T(128)S(1)}, s32[4]{0:T(128)}, u32[]{:S(2)}) copy-start(s32[4]{0:T(128)} %kinds.1) | copy-start | bytes 52
  2.8 15.7 %copy-start.5 = (s32[4]{0:T(128)S(1)}, s32[4]{0:T(128)}, u32[]{:S(2)}) copy-start(s32[4]{0:T(128)} %partners.1) | copy-start | bytes 52
  2.8 15.7 %copy-start.6 = (s32[1,32]{1,0:T(1,128)S(1)}, s32[1,32]{1,0:T(1,128)}, u32[]{:S(2)}) copy-start(s32[1,32]{1,0:T(1,128)} %counts.1) | copy-start | bytes 388
  2.9 5.0 %collective-permute-start = (f32[1032,128]{1,0:T(8,128)S(1)}, f32[1032,128]{1,0:T(8,128)S(1)}, u32[]{:S(2)}, u32[]{:S(2)}) collective-permute-start(f32[1032,128]{1,0:T(8,128)S(1)} %shard_map.123.own), channel_id=1, source_target_pairs={{0,1},{1,0},{2,3},{3,2},{4,5},{5,4},{6,7},{7,6},{8,9},{9,8},{10,11... | collective-permute-start | bytes 1585160 | tf_op jit(solution)/shard_map/ppermute | solution.py:350
  4.4 10.5 %collective-permute-start.1 = (f32[1032,128]{1,0:T(8,128)S(1)}, f32[1032,128]{1,0:T(8,128)S(1)}, u32[]{:S(2)}, u32[]{:S(2)}) collective-permute-start(f32[1032,128]{1,0:T(8,128)S(1)} %shard_map.123.own), channel_id=1, source_target_pairs={{1,2},{2,1},{3,4},{4,3},{5,6},{6,5},{7,8},{8,7},{9,10},{10,9},{11,... | collective-permute-start | bytes 1585160 | tf_op jit(solution)/shard_map/ppermute | solution.py:349
  8.0 10.5 %collective-permute-start.3 = (f32[648,128]{1,0:T(8,128)S(1)}, f32[648,128]{1,0:T(8,128)S(1)}, u32[]{:S(2)}, u32[]{:S(2)}) collective-permute-start(f32[648,128]{1,0:T(8,128)S(1)} %shard_map.124), channel_id=1, source_target_pairs={{1,2},{2,1},{3,4},{4,3},{5,6},{6,5},{7,8},{8,7},{9,10},{10,9},{11,... | collective-permute-start | bytes 995336 | tf_op jit(solution)/shard_map/ppermute | solution.py:352
  14.9 4.7 %collective-permute-start.2 = (f32[1032,128]{1,0:T(8,128)S(1)}, f32[1032,128]{1,0:T(8,128)S(1)}, u32[]{:S(2)}, u32[]{:S(2)}) collective-permute-start(f32[1032,128]{1,0:T(8,128)S(1)} %collective-permute-done.1.near), channel_id=1, source_target_pairs={{0,1},{1,0},{2,3},{3,2},{4,5},{5,4},{6,7},{7,6},{8,9},{9,8},{10,11... | collective-permute-start | bytes 1585160 | tf_op jit(solution)/shard_map/ppermute | solution.py:364
  18.5 1.6 collective-permute-start.4
  20.1 30.4 %copy-start.1 = (s32[1,24,128]{2,1,0:T(8,128)S(1)}, s32[1,24,128]{2,1,0:T(8,128)}, u32[]{:S(2)}) copy-start(s32[1,24,128]{2,1,0:T(8,128)} %param.20) | copy-start | bytes 36868
  23.3 26.2 %collective-permute-start.5 = (f32[520,128]{1,0:T(8,128)S(1)}, f32[520,128]{1,0:T(8,128)S(1)}, u32[]{:S(2)}, u32[]{:S(2)}) collective-permute-start(f32[520,128]{1,0:T(8,128)S(1)} %get-tuple-element.33.own), channel_id=1, source_target_pairs={{1,2},{2,1},{3,4},{4,3},{5,6},{6,5},{7,8},{8,7},{9,10},{10,9},{11,... | collective-permute-start | bytes 798728 | tf_op jit(solution)/shard_map/ppermute | solution.py:381
  49.5 2.5 %collective-permute-start.6 = (f32[520,128]{1,0:T(8,128)S(1)}, f32[520,128]{1,0:T(8,128)S(1)}, u32[]{:S(2)}, u32[]{:S(2)}) collective-permute-start(f32[520,128]{1,0:T(8,128)S(1)} %collective-permute-done.5.beside), channel_id=1, source_target_pairs={{0,1},{1,0},{2,3},{3,2},{4,5},{5,4},{6,7},{7,6},{8,9},{9,8},{10,11... | collective-permute-start | bytes 798728 | tf_op jit(solution)/shard_map/ppermute | solution.py:385
  68.9 18.5 %collective-permute-start.7 = (f32[520,128]{1,0:T(8,128)S(1)}, f32[520,128]{1,0:T(8,128)S(1)}, u32[]{:S(2)}, u32[]{:S(2)}) collective-permute-start(f32[520,128]{1,0:T(8,128)S(1)} %get-tuple-element.43.own), channel_id=1, source_target_pairs={{1,2},{2,1},{3,4},{4,3},{5,6},{6,5},{7,8},{8,7},{9,10},{10,9},{11,... | collective-permute-start | bytes 798728 | tf_op jit(solution)/shard_map/ppermute | solution.py:381
  87.4 2.5 %collective-permute-start.8 = (f32[520,128]{1,0:T(8,128)S(1)}, f32[520,128]{1,0:T(8,128)S(1)}, u32[]{:S(2)}, u32[]{:S(2)}) collective-permute-start(f32[520,128]{1,0:T(8,128)S(1)} %collective-permute-done.7.beside), channel_id=1, source_target_pairs={{0,1},{1,0},{2,3},{3,2},{4,5},{5,4},{6,7},{7,6},{8,9},{9,8},{10,11... | collective-permute-start | bytes 798728 | tf_op jit(solution)/shard_map/ppermute | solution.py:385
  106.9 18.5 %collective-permute-start.9 = (f32[520,128]{1,0:T(8,128)S(1)}, f32[520,128]{1,0:T(8,128)S(1)}, u32[]{:S(2)}, u32[]{:S(2)}) collective-permute-start(f32[520,128]{1,0:T(8,128)S(1)} %get-tuple-element.49.own), channel_id=1, source_target_pairs={{1,2},{2,1},{3,4},{4,3},{5,6},{6,5},{7,8},{8,7},{9,10},{10,9},{11,... | collective-permute-start | bytes 798728 | tf_op jit(solution)/shard_map/ppermute | solution.py:381
  125.4 2.5 %collective-permute-start.10 = (f32[520,128]{1,0:T(8,128)S(1)}, f32[520,128]{1,0:T(8,128)S(1)}, u32[]{:S(2)}, u32[]{:S(2)}) collective-permute-start(f32[520,128]{1,0:T(8,128)S(1)} %collective-permute-done.9.beside), channel_id=1, source_target_pairs={{0,1},{1,0},{2,3},{3,2},{4,5},{5,4},{6,7},{7,6},{8,9},{9,8},{10,11... | collective-permute-start | bytes 798728 | tf_op jit(solution)/shard_map/ppermute | solution.py:385

commit v7 on v6

--- a/solution.py
+++ b/solution.py
@@ -174,7 +174,7 @@
     for row, (gas, solid) in enumerate(((0.5, 0.25), (-0.25, 0.25), (1.0, 0.0), (0.25, 0.5), (0.25, -0.25))):
         flts[pl.ds(row, 1), :] = jnp.full((1, 128), jnp.where(is_gas, gas, solid), F32)
     for s in range(maps.shape[0]):
-        turned[s] = maps[s].T
+        turned[pl.ds(128 * s, 128), :] = jnp.concatenate(halves(maps[s].T), axis=1)
 
 
 def far_kernel(mate, far):
@@ -284,18 +284,23 @@
                 for w in range(slots // 8):
                     got = jnp.take_along_axis(line, lanes[w], axis=1, mode="promise_in_bounds")
                     vals[q][w] = jnp.where(rows[w] == 4 * i + j, got, vals[q][w])
-    columns = []
+    heads = []
     for q in range(parts):
-        full = jnp.concatenate(vals[q] + [jnp.zeros((128 - slots, 128), F32)], axis=0)
-        columns.append(full.T)
+        heads.extend(halves(jnp.concatenate(vals[q] + [jnp.zeros((32 - slots, 128), F32)], axis=0)))
+    head = jnp.concatenate(heads, axis=0)
+    blocks = []
+    for s in range(slots):
+        mine = iota((32, 128), 0).astype(F32).astype(BF16) == jnp.bfloat16(s)
+        blocks.append(jnp.where(jnp.concatenate([mine] * (2 * parts), axis=0), head, jnp.bfloat16(0)))
+    out_rows = jnp.dot(jnp.concatenate(blocks, axis=1), maps[...], preferred_element_type=F32)
+    out_rows = out_rows[:, :128] + out_rows[:, 128:]
+    values = [out_rows[64 * q : 64 * q + 32] + out_rows[64 * q + 32 : 64 * q + 64] for q in range(parts)]
     left, right = [], [[] for _ in range(parts)]
     for s in range(slots):
         aim = targets[s : s + 1, :]
         left.append(one_hot(aim >> 7, 128))
-        table = maps[s]
         for q in range(parts):
-            value = jnp.sum(table * columns[q][:, s : s + 1], axis=0, keepdims=True)
-            right[q].append(spread(aim & 127, value))
+            right[q].append(spread(aim & 127, values[q][s : s + 1]))
     sums = [product(left, right[q]) for q in range(parts)]
     chips = out.shape[0] // 2
     for c in range(chips):
@@ -357,7 +362,7 @@
             ((8, 128), jnp.int32, "v"),
             ((8, 128), F32, "v"),
             ((slots, 128), jnp.int32, "v"),
-            ((slots, 128, 128), F32, "v"),
+            ((slots * 128, 256), BF16, "v"),
         ],
     )(group_kind, partner, patch_count, patch_centres[0], patch_maps[0])
     targets = patch_targets[0]

time: 177 us -> 178 us (level)
  no operation moved by 1% of the time
where the time goes in v7:
time: 178 us; the launch traced here: 177 us
  blocking collectives  125 us (70%)
  Pallas kernels  22.3 us (13%)
  starting transfers between devices  17.7 us (10%)
  waiting for transfers between devices  8.98 us (5%)
    all_to_all x4, blocking collectives, local(): source = lax.all_to_all(send, ('grp', 'sub'), 0, 0, tiled=True)  72.4 us
    all_to_all x4, blocking collectives, local(): parts = lax.all_to_all(parts, 'sub', 0, 0, tiled=True)  53 us
    pallas_call x3, Pallas kernels, local(): call(functools.partial(middle_kernel, full=full), 'vvvvvvv', [keep_out, f...  10.1 us
    ppermute x3, starting transfers between devices, local(): beside = lax.ppermute(keep, 'sub', cross)  7.52 us
    pallas_call x4, Pallas kernels, local(): call(functools.partial(patch_kernel, final=final), 'vvvvv', [((subs, 8 if...  6.85 us
    ppermute x1, waiting for transfers between devices, local(): near = lax.ppermute(payload, 'sub', cross)  4.92 us
  transfers between devices with their start and end apart: 11, of which 3 were waited for; matrix products, arithmetic and copies ran while one was open for 0% of the time, Pallas kernels for 3%

profile of v7, /device:TPU:1, one launch (start us, length us, event | category | flops | bytes accessed | tf_op | source)
XLA Modules:
  0.0 177.4 jit_solution(2586113165501666513)
XLA Ops:
  0.6 0.0 copy-start
  0.6 0.0 copy-start.2
  0.7 1.4 pad_maximum_fusion.fields
  2.1 0.0 copy-start.3
  2.1 0.7 copy-done.3
  2.8 0.0 copy-start.4
  2.8 0.0 copy-start.5
  2.8 0.0 copy-start.6
  2.8 0.1 shard_map.123.own
  2.9 1.5 collective-permute-start
  4.4 3.6 %collective-permute-start.1 = (f32[1032,128]{1,0:T(8,128)S(1)}, f32[1032,128]{1,0:T(8,128)S(1)}, u32[]{:S(2)}, u32[]{:S(2)}) collective-permute-start(f32[1032,128]{1,0:T(8,128)S(1)} %shard_map.123.own), channel_id=1, source_target_pairs={{1,2},{2,1},{3,4},{4,3},{5,6},{6,5},{7,8},{8,7},{9,10},{10,9},{11,... | collective-permute-start | bytes 1585160 | tf_op jit(solution)/shard_map/ppermute | solution.py:354
  7.9 0.0 collective-permute-done.mate
  8.0 2.0 %collective-permute-start.3 = (f32[648,128]{1,0:T(8,128)S(1)}, f32[648,128]{1,0:T(8,128)S(1)}, u32[]{:S(2)}, u32[]{:S(2)}) collective-permute-start(f32[648,128]{1,0:T(8,128)S(1)} %shard_map.124), channel_id=1, source_target_pairs={{1,2},{2,1},{3,4},{4,3},{5,6},{6,5},{7,8},{8,7},{9,10},{10,9},{11,... | collective-permute-start | bytes 995336 | tf_op jit(solution)/shard_map/ppermute | solution.py:357
  10.0 4.9 %collective-permute-done.1.near = f32[1032,128]{1,0:T(8,128)S(1)} collective-permute-done((f32[1032,128]{1,0:T(8,128)S(1)}, f32[1032,128]{1,0:T(8,128)S(1)}, u32[]{:S(2)}, u32[]{:S(2)}) %collective-permute-start.1) | collective-permute-done | bytes 528416 | tf_op jit(solution)/shard_map/ppermute | solution.py:354
  14.9 0.0 collective-permute-start.2
  14.9 3.6 %collective-permute-done.3.far = f32[648,128]{1,0:T(8,128)S(1)} collective-permute-done((f32[648,128]{1,0:T(8,128)S(1)}, f32[648,128]{1,0:T(8,128)S(1)}, u32[]{:S(2)}, u32[]{:S(2)}) %collective-permute-start.3) | collective-permute-done | bytes 331808 | tf_op jit(solution)/shard_map/ppermute | solution.py:357
  18.5 0.0 collective-permute-start.4
  18.5 0.0 copy-done
  18.5 0.0 copy-done.2
  18.5 0.0 copy-done.4
  18.5 0.0 copy-done.5
  18.5 0.0 copy-done.6
  18.5 1.1 shard_map.122
  19.6 0.0 collective-permute-done.2.near_other
  19.6 0.5 collective-permute-done.4.far_other
  20.1 0.0 copy-start.1
  20.1 3.2 %shard_map.125 = (f32[520,128]{1,0:T(8,128)S(1)}, f32[128,4,128]{2,1,0:T(4,128)S(1)}, f32[4,10,128,128]{3,2,1,0:T(8,128)S(1)}, s32[6,4,128]{2,1,0:T(4,128)S(1)}) custom-call(f32[8,128]{1,0:T(8,128)S(1)} %get-tuple-element.30.flts, f32[1032,128]{1,0:T(8,128)S(1)} %shard_map.123.own, f32[1032,128]{1,0:T(8,128)S(1)} %collective-permute-done.mate, ...), custom_call_target="tpu_custom_call" | custom-call | tf_op jit(solution)/shard_map/pallas_call | solution.py:377
  23.3 3.7 %collective-permute-start.5 = (f32[520,128]{1,0:T(8,128)S(1)}, f32[520,128]{1,0:T(8,128)S(1)}, u32[]{:S(2)}, u32[]{:S(2)}) collective-permute-start(f32[520,128]{1,0:T(8,128)S(1)} %get-tuple-element.33.own), channel_id=1, source_target_pairs={{1,2},{2,1},{3,4},{4,3},{5,6},{6,5},{7,8},{8,7},{9,10},{10,9},{11,... | collective-permute-start | bytes 798728 | tf_op jit(solution)/shard_map/ppermute | solution.py:386
  27.0 22.5 %all_to_all.40.source = f32[128,4,128]{2,1,0:T(4,128)S(1)} all-to-all(f32[128,4,128]{2,1,0:T(4,128)S(1)} %get-tuple-element.32), channel_id=1, replica_groups=mesh['grp'=4,'sub'=32] {'grp','sub'}, dimensions={0} | all-to-all | bytes 524288 | tf_op jit(solution)/shard_map/all_to_all | solution.py:387
  49.5 0.0 collective-permute-done.5.beside
  49.5 1.1 collective-permute-start.6
  50.5 0.0 copy-done.1
  50.5 1.6 shard_map.126
  52.1 0.0 collective-permute-done.6.other
  52.2 13.6 %all_to_all.41.parts = f32[32,24,128]{2,1,0:T(8,128)S(1)} all-to-all(f32[32,24,128]{2,1,0:T(8,128)S(1)} %shard_map.126), channel_id=1, replica_groups=mesh['grp'=4,'sub'=32] {'sub'}, dimensions={0} | all-to-all | bytes 786432 | tf_op jit(solution)/shard_map/all_to_all | solution.py:398
  65.8 3.4 %shard_map.127 = (f32[520,128]{1,0:T(8,128)S(1)}, f32[128,4,128]{2,1,0:T(4,128)S(1)}) custom-call(f32[8,128]{1,0:T(8,128)S(1)} %get-tuple-element.30.flts, f32[32,24,128]{2,1,0:T(8,128)S(1)} %all_to_all.41.parts, f32[520,128]{1,0:T(8,128)S(1)} %get-tuple-element.33.own, f32[520,128]{1,0:T(8,128)S(1)} %collective-permute-done.5.beside, ...), custom_call_target="tpu_custom_call" | custom-call | tf_op jit(solution)/shard_map/pallas_call | solution.py:408
  69.2 1.9 %collective-permute-start.7 = (f32[520,128]{1,0:T(8,128)S(1)}, f32[520,128]{1,0:T(8,128)S(1)}, u32[]{:S(2)}, u32[]{:S(2)}) collective-permute-start(f32[520,128]{1,0:T(8,128)S(1)} %get-tuple-element.43.own), channel_id=1, source_target_pairs={{1,2},{2,1},{3,4},{4,3},{5,6},{6,5},{7,8},{8,7},{9,10},{10,9},{11,... | collective-permute-start | bytes 798728 | tf_op jit(solution)/shard_map/ppermute | solution.py:386
  71.1 16.5 %all_to_all.42.source = f32[128,4,128]{2,1,0:T(4,128)S(1)} all-to-all(f32[128,4,128]{2,1,0:T(4,128)S(1)} %get-tuple-element.42), channel_id=1, replica_groups=mesh['grp'=4,'sub'=32] {'grp','sub'}, dimensions={0} | all-to-all | bytes 524288 | tf_op jit(solution)/shard_map/all_to_all | solution.py:387
  87.6 0.0 collective-permute-done.7.beside
  87.6 1.1 collective-permute-start.8
  88.7 1.6 shard_map.128
  90.3 0.0 collective-permute-done.8.other
  90.3 13.6 %all_to_all.43.parts = f32[32,24,128]{2,1,0:T(8,128)S(1)} all-to-all(f32[32,24,128]{2,1,0:T(8,128)S(1)} %shard_map.128), channel_id=1, replica_groups=mesh['grp'=4,'sub'=32] {'sub'}, dimensions={0} | all-to-all | bytes 786432 | tf_op jit(solution)/shard_map/all_to_all | solution.py:398
  104.0 3.4 %shard_map.129 = (f32[520,128]{1,0:T(8,128)S(1)}, f32[128,4,128]{2,1,0:T(4,128)S(1)}) custom-call(f32[8,128]{1,0:T(8,128)S(1)} %get-tuple-element.30.flts, f32[32,24,128]{2,1,0:T(8,128)S(1)} %all_to_all.43.parts, f32[520,128]{1,0:T(8,128)S(1)} %get-tuple-element.43.own, f32[520,128]{1,0:T(8,128)S(1)} %collective-permute-done.7.beside, ...), custom_call_target="tpu_custom_call" | custom-call | tf_op jit(solution)/shard_map/pallas_call | solution.py:408
  107.3 1.9 %collective-permute-start.9 = (f32[520,128]{1,0:T(8,128)S(1)}, f32[520,128]{1,0:T(8,128)S(1)}, u32[]{:S(2)}, u32[]{:S(2)}) collective-permute-start(f32[520,128]{1,0:T(8,128)S(1)} %get-tuple-element.49.own), channel_id=1, source_target_pairs={{1,2},{2,1},{3,4},{4,3},{5,6},{6,5},{7,8},{8,7},{9,10},{10,9},{11,... | collective-permute-start | bytes 798728 | tf_op jit(solution)/shard_map/ppermute | solution.py:386
  109.2 16.5 %all_to_all.44.source = f32[128,4,128]{2,1,0:T(4,128)S(1)} all-to-all(f32[128,4,128]{2,1,0:T(4,128)S(1)} %get-tuple-element.48), channel_id=1, replica_groups=mesh['grp'=4,'sub'=32] {'grp','sub'}, dimensions={0} | all-to-all | bytes 524288 | tf_op jit(solution)/shard_map/all_to_all | solution.py:387
  125.8 0.0 collective-permute-done.9.beside
  125.8 1.1 collective-permute-start.10
  126.8 1.6 shard_map.130
  128.5 0.0 collective-permute-done.10.other
  128.5 13.6 %all_to_all.45.parts = f32[32,24,128]{2,1,0:T(8,128)S(1)} all-to-all(f32[32,24,128]{2,1,0:T(8,128)S(1)} %shard_map.130), channel_id=1, replica_groups=mesh['grp'=4,'sub'=32] {'sub'}, dimensions={0} | all-to-all | bytes 786432 | tf_op jit(solution)/shard_map/all_to_all | solution.py:398
  142.1 3.3 %shard_map.131 = (f32[520,128]{1,0:T(8,128)S(1)}, f32[128,8,128]{2,1,0:T(8,128)S(1)}) custom-call(f32[8,128]{1,0:T(8,128)S(1)} %get-tuple-element.30.flts, f32[32,24,128]{2,1,0:T(8,128)S(1)} %all_to_all.45.parts, f32[520,128]{1,0:T(8,128)S(1)} %get-tuple-element.49.own, f32[520,128]{1,0:T(8,128)S(1)} %collective-permute-done.9.beside, ...), custom_call_target="tpu_custom_call" | custom-call | tf_op jit(solution)/shard_map/pallas_call | solution.py:408
  145.5 16.9 %all_to_all.46.source = f32[128,8,128]{2,1,0:T(8,128)S(1)} all-to-all(f32[128,8,128]{2,1,0:T(8,128)S(1)} %get-tuple-element.54), channel_id=1, replica_groups=mesh['grp'=4,'sub'=32] {'grp','sub'}, dimensions={0} | all-to-all | bytes 1048576 | tf_op jit(solution)/shard_map/all_to_all | solution.py:387
  162.3 2.0 %shard_map.132 = f32[32,8,128]{2,1,0:T(8,128)S(1)} custom-call(s32[8,128]{1,0:T(8,128)S(1)} %get-tuple-element.31.ints, f32[128,8,128]{2,1,0:T(8,128)S(1)} %all_to_all.46.source, s32[24,128]{1,0:T(8,128)S(1)} %get-tuple-element.35.place, s32[24,128]{1,0:T(8,128)S(1)} %bitcast.9, bf16[3072,256]{1,0:T(8,128)(2,1)S(1)} %get-tuple-element.36.maps), custom_call_target="tpu_custom_call" | custom-call | tf_op jit(solution)/shard_map/pallas_call | solution.py:391
  164.4 12.1 %all_to_all.47.parts = f32[32,8,128]{2,1,0:T(8,128)S(1)} all-to-all(f32[32,8,128]{2,1,0:T(8,128)S(1)} %shard_map.132), channel_id=1, replica_groups=mesh['grp'=4,'sub'=32] {'sub'}, dimensions={0} | all-to-all | bytes 262144 | tf_op jit(solution)/shard_map/all_to_all | solution.py:398
  176.4 1.0 shard_map.133
  (1 shorter events, 0.0 us)
Async XLA Ops:
  0.6 17.8 %copy-start = (f32[1,24,128,128]{3,2,1,0:T(8,128)S(1)}, f32[1,24,128,128]{3,2,1,0:T(8,128)}, u32[]{:S(2)}) copy-start(f32[1,24,128,128]{3,2,1,0:T(8,128)} %param.21) | copy-start | bytes 4718596
  0.6 17.8 %copy-start.2 = (s32[1,24,128]{2,1,0:T(8,128)S(1)}, s32[1,24,128]{2,1,0:T(8,128)}, u32[]{:S(2)}) copy-start(s32[1,24,128]{2,1,0:T(8,128)} %param.19) | copy-start | bytes 36868
  2.1 0.7 copy-start.3
  2.8 15.7 %copy-start.4 = (s32[4]{0:T(128)S(1)}, s32[4]{0:T(128)}, u32[]{:S(2)}) copy-start(s32[4]{0:T(128)} %kinds.1) | copy-start | bytes 52
  2.8 15.7 %copy-start.5 = (s32[4]{0:T(128)S(1)}, s32[4]{0:T(128)}, u32[]{:S(2)}) copy-start(s32[4]{0:T(128)} %partners.1) | copy-start | bytes 52
  2.8 15.7 %copy-start.6 = (s32[1,32]{1,0:T(1,128)S(1)}, s32[1,32]{1,0:T(1,128)}, u32[]{:S(2)}) copy-start(s32[1,32]{1,0:T(1,128)} %counts.1) | copy-start | bytes 388
  2.9 5.0 %collective-permute-start = (f32[1032,128]{1,0:T(8,128)S(1)}, f32[1032,128]{1,0:T(8,128)S(1)}, u32[]{:S(2)}, u32[]{:S(2)}) collective-permute-start(f32[1032,128]{1,0:T(8,128)S(1)} %shard_map.123.own), channel_id=1, source_target_pairs={{0,1},{1,0},{2,3},{3,2},{4,5},{5,4},{6,7},{7,6},{8,9},{9,8},{10,11... | collective-permute-start | bytes 1585160 | tf_op jit(solution)/shard_map/ppermute | solution.py:355
  4.4 10.5 %collective-permute-start.1 = (f32[1032,128]{1,0:T(8,128)S(1)}, f32[1032,128]{1,0:T(8,128)S(1)}, u32[]{:S(2)}, u32[]{:S(2)}) collective-permute-start(f32[1032,128]{1,0:T(8,128)S(1)} %shard_map.123.own), channel_id=1, source_target_pairs={{1,2},{2,1},{3,4},{4,3},{5,6},{6,5},{7,8},{8,7},{9,10},{10,9},{11,... | collective-permute-start | bytes 1585160 | tf_op jit(solution)/shard_map/ppermute | solution.py:354
  8.0 10.5 %collective-permute-start.3 = (f32[648,128]{1,0:T(8,128)S(1)}, f32[648,128]{1,0:T(8,128)S(1)}, u32[]{:S(2)}, u32[]{:S(2)}) collective-permute-start(f32[648,128]{1,0:T(8,128)S(1)} %shard_map.124), channel_id=1, source_target_pairs={{1,2},{2,1},{3,4},{4,3},{5,6},{6,5},{7,8},{8,7},{9,10},{10,9},{11,... | collective-permute-start | bytes 995336 | tf_op jit(solution)/shard_map/ppermute | solution.py:357
  14.9 4.7 %collective-permute-start.2 = (f32[1032,128]{1,0:T(8,128)S(1)}, f32[1032,128]{1,0:T(8,128)S(1)}, u32[]{:S(2)}, u32[]{:S(2)}) collective-permute-start(f32[1032,128]{1,0:T(8,128)S(1)} %collective-permute-done.1.near), channel_id=1, source_target_pairs={{0,1},{1,0},{2,3},{3,2},{4,5},{5,4},{6,7},{7,6},{8,9},{9,8},{10,11... | collective-permute-start | bytes 1585160 | tf_op jit(solution)/shard_map/ppermute | solution.py:369
  18.5 1.6 collective-permute-start.4
  20.1 30.4 %copy-start.1 = (s32[1,24,128]{2,1,0:T(8,128)S(1)}, s32[1,24,128]{2,1,0:T(8,128)}, u32[]{:S(2)}) copy-start(s32[1,24,128]{2,1,0:T(8,128)} %param.20) | copy-start | bytes 36868
  23.3 26.2 %collective-permute-start.5 = (f32[520,128]{1,0:T(8,128)S(1)}, f32[520,128]{1,0:T(8,128)S(1)}, u32[]{:S(2)}, u32[]{:S(2)}) collective-permute-start(f32[520,128]{1,0:T(8,128)S(1)} %get-tuple-element.33.own), channel_id=1, source_target_pairs={{1,2},{2,1},{3,4},{4,3},{5,6},{6,5},{7,8},{8,7},{9,10},{10,9},{11,... | collective-permute-start | bytes 798728 | tf_op jit(solution)/shard_map/ppermute | solution.py:386
  49.5 2.7 %collective-permute-start.6 = (f32[520,128]{1,0:T(8,128)S(1)}, f32[520,128]{1,0:T(8,128)S(1)}, u32[]{:S(2)}, u32[]{:S(2)}) collective-permute-start(f32[520,128]{1,0:T(8,128)S(1)} %collective-permute-done.5.beside), channel_id=1, source_target_pairs={{0,1},{1,0},{2,3},{3,2},{4,5},{5,4},{6,7},{7,6},{8,9},{9,8},{10,11... | collective-permute-start | bytes 798728 | tf_op jit(solution)/shard_map/ppermute | solution.py:390
  69.2 18.5 %collective-permute-start.7 = (f32[520,128]{1,0:T(8,128)S(1)}, f32[520,128]{1,0:T(8,128)S(1)}, u32[]{:S(2)}, u32[]{:S(2)}) collective-permute-start(f32[520,128]{1,0:T(8,128)S(1)} %get-tuple-element.43.own), channel_id=1, source_target_pairs={{1,2},{2,1},{3,4},{4,3},{5,6},{6,5},{7,8},{8,7},{9,10},{10,9},{11,... | collective-permute-start | bytes 798728 | tf_op jit(solution)/shard_map/ppermute | solution.py:386
  87.6 2.7 %collective-permute-start.8 = (f32[520,128]{1,0:T(8,128)S(1)}, f32[520,128]{1,0:T(8,128)S(1)}, u32[]{:S(2)}, u32[]{:S(2)}) collective-permute-start(f32[520,128]{1,0:T(8,128)S(1)} %collective-permute-done.7.beside), channel_id=1, source_target_pairs={{0,1},{1,0},{2,3},{3,2},{4,5},{5,4},{6,7},{7,6},{8,9},{9,8},{10,11... | collective-permute-start | bytes 798728 | tf_op jit(solution)/shard_map/ppermute | solution.py:390
  107.3 18.5 %collective-permute-start.9 = (f32[520,128]{1,0:T(8,128)S(1)}, f32[520,128]{1,0:T(8,128)S(1)}, u32[]{:S(2)}, u32[]{:S(2)}) collective-permute-start(f32[520,128]{1,0:T(8,128)S(1)} %get-tuple-element.49.own), channel_id=1, source_target_pairs={{1,2},{2,1},{3,4},{4,3},{5,6},{6,5},{7,8},{8,7},{9,10},{10,9},{11,... | collective-permute-start | bytes 798728 | tf_op jit(solution)/shard_map/ppermute | solution.py:386
  125.8 2.7 %collective-permute-start.10 = (f32[520,128]{1,0:T(8,128)S(1)}, f32[520,128]{1,0:T(8,128)S(1)}, u32[]{:S(2)}, u32[]{:S(2)}) collective-permute-start(f32[520,128]{1,0:T(8,128)S(1)} %collective-permute-done.9.beside), channel_id=1, source_target_pairs={{0,1},{1,0},{2,3},{3,2},{4,5},{5,4},{6,7},{7,6},{8,9},{9,8},{10,11... | collective-permute-start | bytes 798728 | tf_op jit(solution)/shard_map/ppermute | solution.py:390

commit v8 on v6

--- a/solution.py
+++ b/solution.py
@@ -11,6 +11,7 @@
 STEPS = 4
 COUPLE = 4
 ROWS = 128
+PIECE = 16
 HALO = 4
 WIDE = 12
 F32 = jnp.float32
@@ -35,11 +36,23 @@
         src, dst = bufs[step % 2], bufs[(step + 1) % 2]
 
         def body(p, carry, src=src, dst=dst):
-            x = src[p]
-            near = src[p + 1] + in_plane(x)
-            dst[p] = (coef[3, p - 1] * x + coef[0, p - 1] * near) + (
-                coef[1, p - 1] * src[p - 1] + coef[2, p - 1] * (1.0 + jnp.tanh(x))
-            )
+            for low in range(0, ROWS, PIECE):
+                high = low + PIECE
+                rows = pl.ds(low, PIECE)
+                if low:
+                    before = src[p, pl.ds(low - 8, 8)]
+                else:
+                    before = pltpu.roll(src[p, pl.ds(ROWS - 8, 8)], 1, 0)
+                if high < ROWS:
+                    after = src[p, pl.ds(high, 8)]
+                else:
+                    after = pltpu.roll(src[p, pl.ds(0, 8)], 7, 0)
+                x = src[p, rows]
+                beside = jnp.concatenate([before, x[:-8]], axis=0) + jnp.concatenate([x[8:], after], axis=0)
+                beside = beside + (pltpu.roll(x, 1, 1) + pltpu.roll(x, 127, 1))
+                dst[p, rows] = (coef[3, p - 1, rows] * x + coef[0, p - 1, rows] * (src[p + 1, rows] + beside)) + (
+                    coef[1, p - 1, rows] * src[p - 1, rows] + coef[2, p - 1, rows] * (1.0 + jnp.tanh(x))
+                )
             return carry
 
         lax.fori_loop(step + 1, WIDE - 1 - step, body, 0, unroll=True)

time: 177 us -> 177 us (level)
  no operation moved by 1% of the time
where the time goes in v8:
time: 177 us
  blocking collectives  125 us (71%)
  Pallas kernels  21.4 us (12%)
  starting transfers between devices  17.7 us (10%)
  waiting for transfers between devices  8.99 us (5%)
    all_to_all x4, blocking collectives, local(): source = lax.all_to_all(send, ('grp', 'sub'), 0, 0, tiled=True)  72.4 us
    all_to_all x4, blocking collectives, local(): parts = lax.all_to_all(parts, 'sub', 0, 0, tiled=True)  53 us
    pallas_call x3, Pallas kernels, local(): call(functools.partial(middle_kernel, full=full), 'vvvvvvv', [keep_out, f...  9.96 us
    ppermute x3, starting transfers between devices, local(): beside = lax.ppermute(keep, 'sub', cross)  7.52 us
    pallas_call x4, Pallas kernels, local(): call(functools.partial(patch_kernel, final=final), 'vvvvv', [((subs, 8 if...  6.1 us
    ppermute x1, waiting for transfers between devices, local(): near = lax.ppermute(payload, 'sub', cross)  4.92 us
    ppermute x1, starting transfers between devices, local(): near = lax.ppermute(payload, 'sub', cross)  3.56 us
    ppermute x1, waiting for transfers between devices, local(): far = lax.ppermute(far, 'sub', cross)  3.55 us
  transfers between devices with their start and end apart: 11, of which 3 were waited for; matrix products, arithmetic and copies ran while one was open for 0% of the time, Pallas kernels for 3%

profile of v8, /device:TPU:1, one launch (start us, length us, event | category | flops | bytes accessed | tf_op | source)
XLA Modules:
  0.0 176.5 jit_solution(13524991260263615385)
XLA Ops:
  0.6 0.0 copy-start
  0.6 0.0 copy-start.2
  0.7 1.4 pad_maximum_fusion.fields
  2.1 0.0 copy-start.3
  2.1 0.7 copy-done.3
  2.8 0.0 copy-start.4
  2.8 0.0 copy-start.5
  2.8 0.0 copy-start.6
  2.8 0.1 shard_map.123.own
  2.9 1.5 collective-permute-start
  4.4 3.6 %collective-permute-start.1 = (f32[1032,128]{1,0:T(8,128)S(1)}, f32[1032,128]{1,0:T(8,128)S(1)}, u32[]{:S(2)}, u32[]{:S(2)}) collective-permute-start(f32[1032,128]{1,0:T(8,128)S(1)} %shard_map.123.own), channel_id=1, source_target_pairs={{1,2},{2,1},{3,4},{4,3},{5,6},{6,5},{7,8},{8,7},{9,10},{10,9},{11,... | collective-permute-start | bytes 1585160 | tf_op jit(solution)/shard_map/ppermute | solution.py:362
  7.9 0.0 collective-permute-done.mate
  8.0 2.0 %collective-permute-start.3 = (f32[648,128]{1,0:T(8,128)S(1)}, f32[648,128]{1,0:T(8,128)S(1)}, u32[]{:S(2)}, u32[]{:S(2)}) collective-permute-start(f32[648,128]{1,0:T(8,128)S(1)} %shard_map.124), channel_id=1, source_target_pairs={{1,2},{2,1},{3,4},{4,3},{5,6},{6,5},{7,8},{8,7},{9,10},{10,9},{11,... | collective-permute-start | bytes 995336 | tf_op jit(solution)/shard_map/ppermute | solution.py:365
  10.0 4.9 %collective-permute-done.1.near = f32[1032,128]{1,0:T(8,128)S(1)} collective-permute-done((f32[1032,128]{1,0:T(8,128)S(1)}, f32[1032,128]{1,0:T(8,128)S(1)}, u32[]{:S(2)}, u32[]{:S(2)}) %collective-permute-start.1) | collective-permute-done | bytes 528416 | tf_op jit(solution)/shard_map/ppermute | solution.py:362
  14.9 0.0 collective-permute-start.2
  14.9 3.6 %collective-permute-done.3.far = f32[648,128]{1,0:T(8,128)S(1)} collective-permute-done((f32[648,128]{1,0:T(8,128)S(1)}, f32[648,128]{1,0:T(8,128)S(1)}, u32[]{:S(2)}, u32[]{:S(2)}) %collective-permute-start.3) | collective-permute-done | bytes 331808 | tf_op jit(solution)/shard_map/ppermute | solution.py:365
  18.5 0.0 collective-permute-start.4
  18.5 0.0 copy-done
  18.5 0.0 copy-done.2
  18.5 0.0 copy-done.4
  18.5 0.0 copy-done.5
  18.5 0.0 copy-done.6
  18.5 1.1 shard_map.122
  19.6 0.0 collective-permute-done.2.near_other
  19.6 0.5 collective-permute-done.4.far_other
  20.1 0.0 copy-start.1
  20.1 3.1 %shard_map.125 = (f32[520,128]{1,0:T(8,128)S(1)}, f32[128,4,128]{2,1,0:T(4,128)S(1)}, f32[4,10,128,128]{3,2,1,0:T(8,128)S(1)}, s32[6,4,128]{2,1,0:T(4,128)S(1)}) custom-call(f32[8,128]{1,0:T(8,128)S(1)} %get-tuple-element.30.flts, f32[1032,128]{1,0:T(8,128)S(1)} %shard_map.123.own, f32[1032,128]{1,0:T(8,128)S(1)} %collective-permute-done.mate, ...), custom_call_target="tpu_custom_call" | custom-call | tf_op jit(solution)/shard_map/pallas_call | solution.py:385
  23.2 3.7 %collective-permute-start.5 = (f32[520,128]{1,0:T(8,128)S(1)}, f32[520,128]{1,0:T(8,128)S(1)}, u32[]{:S(2)}, u32[]{:S(2)}) collective-permute-start(f32[520,128]{1,0:T(8,128)S(1)} %get-tuple-element.33.own), channel_id=1, source_target_pairs={{1,2},{2,1},{3,4},{4,3},{5,6},{6,5},{7,8},{8,7},{9,10},{10,9},{11,... | collective-permute-start | bytes 798728 | tf_op jit(solution)/shard_map/ppermute | solution.py:394
  26.9 22.5 %all_to_all.40.source = f32[128,4,128]{2,1,0:T(4,128)S(1)} all-to-all(f32[128,4,128]{2,1,0:T(4,128)S(1)} %get-tuple-element.32), channel_id=1, replica_groups=mesh['grp'=4,'sub'=32] {'grp','sub'}, dimensions={0} | all-to-all | bytes 524288 | tf_op jit(solution)/shard_map/all_to_all | solution.py:395
  49.4 0.0 collective-permute-done.5.beside
  49.4 1.1 collective-permute-start.6
  50.4 0.0 copy-done.1
  50.4 1.4 shard_map.126
  51.8 0.0 collective-permute-done.6.other
  51.8 13.7 %all_to_all.41.parts = f32[32,24,128]{2,1,0:T(8,128)S(1)} all-to-all(f32[32,24,128]{2,1,0:T(8,128)S(1)} %shard_map.126), channel_id=1, replica_groups=mesh['grp'=4,'sub'=32] {'sub'}, dimensions={0} | all-to-all | bytes 786432 | tf_op jit(solution)/shard_map/all_to_all | solution.py:406
  65.5 3.3 %shard_map.127 = (f32[520,128]{1,0:T(8,128)S(1)}, f32[128,4,128]{2,1,0:T(4,128)S(1)}) custom-call(f32[8,128]{1,0:T(8,128)S(1)} %get-tuple-element.30.flts, f32[32,24,128]{2,1,0:T(8,128)S(1)} %all_to_all.41.parts, f32[520,128]{1,0:T(8,128)S(1)} %get-tuple-element.33.own, f32[520,128]{1,0:T(8,128)S(1)} %collective-permute-done.5.beside, ...), custom_call_target="tpu_custom_call" | custom-call | tf_op jit(solution)/shard_map/pallas_call | solution.py:416
  68.8 1.9 %collective-permute-start.7 = (f32[520,128]{1,0:T(8,128)S(1)}, f32[520,128]{1,0:T(8,128)S(1)}, u32[]{:S(2)}, u32[]{:S(2)}) collective-permute-start(f32[520,128]{1,0:T(8,128)S(1)} %get-tuple-element.43.own), channel_id=1, source_target_pairs={{1,2},{2,1},{3,4},{4,3},{5,6},{6,5},{7,8},{8,7},{9,10},{10,9},{11,... | collective-permute-start | bytes 798728 | tf_op jit(solution)/shard_map/ppermute | solution.py:394
  70.8 16.5 %all_to_all.42.source = f32[128,4,128]{2,1,0:T(4,128)S(1)} all-to-all(f32[128,4,128]{2,1,0:T(4,128)S(1)} %get-tuple-element.42), channel_id=1, replica_groups=mesh['grp'=4,'sub'=32] {'grp','sub'}, dimensions={0} | all-to-all | bytes 524288 | tf_op jit(solution)/shard_map/all_to_all | solution.py:395
  87.3 0.0 collective-permute-done.7.beside
  87.3 1.1 collective-permute-start.8
  88.4 1.4 shard_map.128
  89.8 0.0 collective-permute-done.8.other
  89.8 13.7 %all_to_all.43.parts = f32[32,24,128]{2,1,0:T(8,128)S(1)} all-to-all(f32[32,24,128]{2,1,0:T(8,128)S(1)} %shard_map.128), channel_id=1, replica_groups=mesh['grp'=4,'sub'=32] {'sub'}, dimensions={0} | all-to-all | bytes 786432 | tf_op jit(solution)/shard_map/all_to_all | solution.py:406
  103.4 3.3 %shard_map.129 = (f32[520,128]{1,0:T(8,128)S(1)}, f32[128,4,128]{2,1,0:T(4,128)S(1)}) custom-call(f32[8,128]{1,0:T(8,128)S(1)} %get-tuple-element.30.flts, f32[32,24,128]{2,1,0:T(8,128)S(1)} %all_to_all.43.parts, f32[520,128]{1,0:T(8,128)S(1)} %get-tuple-element.43.own, f32[520,128]{1,0:T(8,128)S(1)} %collective-permute-done.7.beside, ...), custom_call_target="tpu_custom_call" | custom-call | tf_op jit(solution)/shard_map/pallas_call | solution.py:416
  106.8 1.9 %collective-permute-start.9 = (f32[520,128]{1,0:T(8,128)S(1)}, f32[520,128]{1,0:T(8,128)S(1)}, u32[]{:S(2)}, u32[]{:S(2)}) collective-permute-start(f32[520,128]{1,0:T(8,128)S(1)} %get-tuple-element.49.own), channel_id=1, source_target_pairs={{1,2},{2,1},{3,4},{4,3},{5,6},{6,5},{7,8},{8,7},{9,10},{10,9},{11,... | collective-permute-start | bytes 798728 | tf_op jit(solution)/shard_map/ppermute | solution.py:394
  108.7 16.5 %all_to_all.44.source = f32[128,4,128]{2,1,0:T(4,128)S(1)} all-to-all(f32[128,4,128]{2,1,0:T(4,128)S(1)} %get-tuple-element.48), channel_id=1, replica_groups=mesh['grp'=4,'sub'=32] {'grp','sub'}, dimensions={0} | all-to-all | bytes 524288 | tf_op jit(solution)/shard_map/all_to_all | solution.py:395
  125.2 0.0 collective-permute-done.9.beside
  125.2 1.1 collective-permute-start.10
  126.3 1.4 shard_map.130
  127.7 0.0 collective-permute-done.10.other
  127.7 13.7 %all_to_all.45.parts = f32[32,24,128]{2,1,0:T(8,128)S(1)} all-to-all(f32[32,24,128]{2,1,0:T(8,128)S(1)} %shard_map.130), channel_id=1, replica_groups=mesh['grp'=4,'sub'=32] {'sub'}, dimensions={0} | all-to-all | bytes 786432 | tf_op jit(solution)/shard_map/all_to_all | solution.py:406
  141.3 3.3 %shard_map.131 = (f32[520,128]{1,0:T(8,128)S(1)}, f32[128,8,128]{2,1,0:T(8,128)S(1)}) custom-call(f32[8,128]{1,0:T(8,128)S(1)} %get-tuple-element.30.flts, f32[32,24,128]{2,1,0:T(8,128)S(1)} %all_to_all.45.parts, f32[520,128]{1,0:T(8,128)S(1)} %get-tuple-element.49.own, f32[520,128]{1,0:T(8,128)S(1)} %collective-permute-done.9.beside, ...), custom_call_target="tpu_custom_call" | custom-call | tf_op jit(solution)/shard_map/pallas_call | solution.py:416
  144.7 16.9 %all_to_all.46.source = f32[128,8,128]{2,1,0:T(8,128)S(1)} all-to-all(f32[128,8,128]{2,1,0:T(8,128)S(1)} %get-tuple-element.54), channel_id=1, replica_groups=mesh['grp'=4,'sub'=32] {'grp','sub'}, dimensions={0} | all-to-all | bytes 1048576 | tf_op jit(solution)/shard_map/all_to_all | solution.py:395
  161.5 2.0 %shard_map.132 = f32[32,8,128]{2,1,0:T(8,128)S(1)} custom-call(s32[8,128]{1,0:T(8,128)S(1)} %get-tuple-element.31.ints, f32[128,8,128]{2,1,0:T(8,128)S(1)} %all_to_all.46.source, s32[24,128]{1,0:T(8,128)S(1)} %get-tuple-element.35.place, s32[24,128]{1,0:T(8,128)S(1)} %bitcast.9, f32[24,128,128]{2,1,0:T(8,128)S(1)} %get-tuple-element.36.maps), custom_call_target="tpu_custom_call" | custom-call | tf_op jit(solution)/shard_map/pallas_call | solution.py:399
  163.5 12.1 %all_to_all.47.parts = f32[32,8,128]{2,1,0:T(8,128)S(1)} all-to-all(f32[32,8,128]{2,1,0:T(8,128)S(1)} %shard_map.132), channel_id=1, replica_groups=mesh['grp'=4,'sub'=32] {'sub'}, dimensions={0} | all-to-all | bytes 262144 | tf_op jit(solution)/shard_map/all_to_all | solution.py:406
  175.6 1.0 shard_map.133
  (1 shorter events, 0.0 us)
Async XLA Ops:
  0.6 17.8 %copy-start = (f32[1,24,128,128]{3,2,1,0:T(8,128)S(1)}, f32[1,24,128,128]{3,2,1,0:T(8,128)}, u32[]{:S(2)}) copy-start(f32[1,24,128,128]{3,2,1,0:T(8,128)} %param.21) | copy-start | bytes 4718596
  0.6 17.8 %copy-start.2 = (s32[1,24,128]{2,1,0:T(8,128)S(1)}, s32[1,24,128]{2,1,0:T(8,128)}, u32[]{:S(2)}) copy-start(s32[1,24,128]{2,1,0:T(8,128)} %param.19) | copy-start | bytes 36868
  2.1 0.7 copy-start.3
  2.8 15.7 %copy-start.4 = (s32[4]{0:T(128)S(1)}, s32[4]{0:T(128)}, u32[]{:S(2)}) copy-start(s32[4]{0:T(128)} %kinds.1) | copy-start | bytes 52
  2.8 15.7 %copy-start.5 = (s32[4]{0:T(128)S(1)}, s32[4]{0:T(128)}, u32[]{:S(2)}) copy-start(s32[4]{0:T(128)} %partners.1) | copy-start | bytes 52
  2.8 15.7 %copy-start.6 = (s32[1,32]{1,0:T(1,128)S(1)}, s32[1,32]{1,0:T(1,128)}, u32[]{:S(2)}) copy-start(s32[1,32]{1,0:T(1,128)} %counts.1) | copy-start | bytes 388
  2.9 5.0 %collective-permute-start = (f32[1032,128]{1,0:T(8,128)S(1)}, f32[1032,128]{1,0:T(8,128)S(1)}, u32[]{:S(2)}, u32[]{:S(2)}) collective-permute-start(f32[1032,128]{1,0:T(8,128)S(1)} %shard_map.123.own), channel_id=1, source_target_pairs={{0,1},{1,0},{2,3},{3,2},{4,5},{5,4},{6,7},{7,6},{8,9},{9,8},{10,11... | collective-permute-start | bytes 1585160 | tf_op jit(solution)/shard_map/ppermute | solution.py:363
  4.4 10.5 %collective-permute-start.1 = (f32[1032,128]{1,0:T(8,128)S(1)}, f32[1032,128]{1,0:T(8,128)S(1)}, u32[]{:S(2)}, u32[]{:S(2)}) collective-permute-start(f32[1032,128]{1,0:T(8,128)S(1)} %shard_map.123.own), channel_id=1, source_target_pairs={{1,2},{2,1},{3,4},{4,3},{5,6},{6,5},{7,8},{8,7},{9,10},{10,9},{11,... | collective-permute-start | bytes 1585160 | tf_op jit(solution)/shard_map/ppermute | solution.py:362
  8.0 10.5 %collective-permute-start.3 = (f32[648,128]{1,0:T(8,128)S(1)}, f32[648,128]{1,0:T(8,128)S(1)}, u32[]{:S(2)}, u32[]{:S(2)}) collective-permute-start(f32[648,128]{1,0:T(8,128)S(1)} %shard_map.124), channel_id=1, source_target_pairs={{1,2},{2,1},{3,4},{4,3},{5,6},{6,5},{7,8},{8,7},{9,10},{10,9},{11,... | collective-permute-start | bytes 995336 | tf_op jit(solution)/shard_map/ppermute | solution.py:365
  14.9 4.7 %collective-permute-start.2 = (f32[1032,128]{1,0:T(8,128)S(1)}, f32[1032,128]{1,0:T(8,128)S(1)}, u32[]{:S(2)}, u32[]{:S(2)}) collective-permute-start(f32[1032,128]{1,0:T(8,128)S(1)} %collective-permute-done.1.near), channel_id=1, source_target_pairs={{0,1},{1,0},{2,3},{3,2},{4,5},{5,4},{6,7},{7,6},{8,9},{9,8},{10,11... | collective-permute-start | bytes 1585160 | tf_op jit(solution)/shard_map/ppermute | solution.py:377
  18.5 1.6 collective-permute-start.4
  20.1 30.4 %copy-start.1 = (s32[1,24,128]{2,1,0:T(8,128)S(1)}, s32[1,24,128]{2,1,0:T(8,128)}, u32[]{:S(2)}) copy-start(s32[1,24,128]{2,1,0:T(8,128)} %param.20) | copy-start | bytes 36868
  23.2 26.2 %collective-permute-start.5 = (f32[520,128]{1,0:T(8,128)S(1)}, f32[520,128]{1,0:T(8,128)S(1)}, u32[]{:S(2)}, u32[]{:S(2)}) collective-permute-start(f32[520,128]{1,0:T(8,128)S(1)} %get-tuple-element.33.own), channel_id=1, source_target_pairs={{1,2},{2,1},{3,4},{4,3},{5,6},{6,5},{7,8},{8,7},{9,10},{10,9},{11,... | collective-permute-start | bytes 798728 | tf_op jit(solution)/shard_map/ppermute | solution.py:394
  49.4 2.5 %collective-permute-start.6 = (f32[520,128]{1,0:T(8,128)S(1)}, f32[520,128]{1,0:T(8,128)S(1)}, u32[]{:S(2)}, u32[]{:S(2)}) collective-permute-start(f32[520,128]{1,0:T(8,128)S(1)} %collective-permute-done.5.beside), channel_id=1, source_target_pairs={{0,1},{1,0},{2,3},{3,2},{4,5},{5,4},{6,7},{7,6},{8,9},{9,8},{10,11... | collective-permute-start | bytes 798728 | tf_op jit(solution)/shard_map/ppermute | solution.py:398
  68.8 18.5 %collective-permute-start.7 = (f32[520,128]{1,0:T(8,128)S(1)}, f32[520,128]{1,0:T(8,128)S(1)}, u32[]{:S(2)}, u32[]{:S(2)}) collective-permute-start(f32[520,128]{1,0:T(8,128)S(1)} %get-tuple-element.43.own), channel_id=1, source_target_pairs={{1,2},{2,1},{3,4},{4,3},{5,6},{6,5},{7,8},{8,7},{9,10},{10,9},{11,... | collective-permute-start | bytes 798728 | tf_op jit(solution)/shard_map/ppermute | solution.py:394
  87.3 2.5 %collective-permute-start.8 = (f32[520,128]{1,0:T(8,128)S(1)}, f32[520,128]{1,0:T(8,128)S(1)}, u32[]{:S(2)}, u32[]{:S(2)}) collective-permute-start(f32[520,128]{1,0:T(8,128)S(1)} %collective-permute-done.7.beside), channel_id=1, source_target_pairs={{0,1},{1,0},{2,3},{3,2},{4,5},{5,4},{6,7},{7,6},{8,9},{9,8},{10,11... | collective-permute-start | bytes 798728 | tf_op jit(solution)/shard_map/ppermute | solution.py:398
  106.8 18.5 %collective-permute-start.9 = (f32[520,128]{1,0:T(8,128)S(1)}, f32[520,128]{1,0:T(8,128)S(1)}, u32[]{:S(2)}, u32[]{:S(2)}) collective-permute-start(f32[520,128]{1,0:T(8,128)S(1)} %get-tuple-element.49.own), channel_id=1, source_target_pairs={{1,2},{2,1},{3,4},{4,3},{5,6},{6,5},{7,8},{8,7},{9,10},{10,9},{11,... | collective-permute-start | bytes 798728 | tf_op jit(solution)/shard_map/ppermute | solution.py:394
  125.2 2.5 %collective-permute-start.10 = (f32[520,128]{1,0:T(8,128)S(1)}, f32[520,128]{1,0:T(8,128)S(1)}, u32[]{:S(2)}, u32[]{:S(2)}) collective-permute-start(f32[520,128]{1,0:T(8,128)S(1)} %collective-permute-done.9.beside), channel_id=1, source_target_pairs={{0,1},{1,0},{2,3},{3,2},{4,5},{5,4},{6,7},{7,6},{8,9},{9,8},{10,11... | collective-permute-start | bytes 798728 | tf_op jit(solution)/shard_map/ppermute | solution.py:398
